TPU v7x, 32 devices: a whole 2x2x4 slice. The times are simulated.
32 devices in a mesh: dp: 2 (over x), tp: 4 (over z), sp: 4 (over y, core).
Axes of the slice: x: 2, y: 2, z: 4, core: 2. Of those that a mesh axis runs over, the one named last changes fastest.
Arguments:
- tokens: bfloat16 [32768, 1024], P(('dp', 'sp')), parts along dimension 0
- glob_pos: int32 [2048], P('dp'), parts along dimension 0
- w_query: bfloat16 [1024, 16, 64], P(None, 'tp')
- w_key: bfloat16 [1024, 16, 64], P(None, 'tp')
- w_value: bfloat16 [1024, 16, 64], P(None, 'tp')
- w_out: bfloat16 [16, 64, 1024], P('tp')
- w_up: bfloat16 [1024, 2624], P(None, 'tp')
- w_down: bfloat16 [2624, 1024], P('tp')
Outputs:
- output: bfloat16 [32768, 1024], P(('dp', 'sp')), parts along dimension 0
There are 2 independent parts. A program takes and returns all parts, laid end to end along the dimension named above; an argument that names none is the same for every part.
All inputs are finite; a program needn't handle non-finite values.
Results may differ from a plain program's by a relative error of at most 0.00794781.
Values are sent between devices in bfloat16 or wider.
A program may use at most 1 GiB of HBM per device.

v0:
```python
import jax
import jax.numpy as jnp
from jax import lax
from jax.sharding import PartitionSpec as P
import math

WIN = 256


def local_window(q_rows, k_ext, v_ext, k_glob, v_glob, glob_pos, first_row, seq_len):
    n_rows, n_heads, head_dim = q_rows.shape
    scale = 1.0 / math.sqrt(head_dim)
    q_block = 128
    key_span = q_block + 2 * WIN

    def one_block(blk_index):
        start = blk_index * q_block
        q_blk = lax.dynamic_slice_in_dim(q_rows, start, q_block)
        k_blk = lax.dynamic_slice_in_dim(k_ext, start, key_span)
        v_blk = lax.dynamic_slice_in_dim(v_ext, start, key_span)
        q_pos = first_row + start + jnp.arange(q_block)
        k_pos = first_row + start - WIN + jnp.arange(key_span)
        k_is_glob = jnp.any(k_pos[:, None] == glob_pos[None, :], axis=1)
        k_ok = (k_pos >= 0) & (k_pos < seq_len) & jnp.logical_not(k_is_glob)
        allowed = (jnp.abs(q_pos[:, None] - k_pos[None, :]) <= WIN) & k_ok[None, :]
        s_win = jnp.einsum('qhe,khe->hqk', q_blk, k_blk, preferred_element_type=jnp.float32) * scale
        s_win = jnp.where(allowed[None], s_win, -jnp.inf)
        s_glob = jnp.einsum('qhe,ghe->hqg', q_blk, k_glob, preferred_element_type=jnp.float32) * scale
        row_max = jnp.maximum(jnp.max(s_win, axis=2, keepdims=True), jnp.max(s_glob, axis=2, keepdims=True))
        e_win = jnp.exp(s_win - row_max)
        e_glob = jnp.exp(s_glob - row_max)
        total = jnp.sum(e_win, axis=2, keepdims=True) + jnp.sum(e_glob, axis=2, keepdims=True)
        p_win = (e_win / total).astype(jnp.bfloat16)
        p_glob = (e_glob / total).astype(jnp.bfloat16)
        blk_out = jnp.einsum('hqk,khe->qhe', p_win, v_blk, preferred_element_type=jnp.float32)
        blk_out = blk_out + jnp.einsum('hqg,ghe->qhe', p_glob, v_glob, preferred_element_type=jnp.float32)
        return blk_out.astype(jnp.bfloat16)

    blocks = lax.map(one_block, jnp.arange(n_rows // q_block))
    return blocks.reshape(n_rows, n_heads, head_dim)


def pick_rows(row_array, safe_idx, owned):
    picked = jnp.take(row_array, safe_idx, axis=0)
    return jnp.where(owned[:, None, None], picked, 0)


def global_queries(q_glob, k_rows, v_rows):
    scale = 1.0 / math.sqrt(q_glob.shape[2])
    scores = jnp.einsum('ghe,rhe->hgr', q_glob, k_rows, preferred_element_type=jnp.float32) * scale
    glob_max = lax.pmax(jnp.max(scores, axis=2, keepdims=True), 'sp')
    exp_scores = jnp.exp(scores - glob_max)
    glob_sum = lax.psum(jnp.sum(exp_scores, axis=2, keepdims=True), 'sp')
    prob_rows = (exp_scores / glob_sum).astype(jnp.bfloat16)
    part_out = jnp.einsum('hgr,rhe->ghe', prob_rows, v_rows, preferred_element_type=jnp.float32)
    return lax.psum(part_out, 'sp').astype(jnp.bfloat16)


def solution(mesh):
    n_seq = mesh.shape['sp']
    to_right = [(i, i + 1) for i in range(n_seq - 1)]
    to_left = [(i + 1, i) for i in range(n_seq - 1)]

    def device_layer(tokens, glob_pos, w_query, w_key, w_value, w_out, w_up, w_down):
        n_rows = tokens.shape[0]
        first_row = lax.axis_index('sp') * n_rows
        q_rows = jnp.einsum('rd,dhe->rhe', tokens, w_query, preferred_element_type=jnp.float32).astype(jnp.bfloat16)
        k_rows = jnp.einsum('rd,dhe->rhe', tokens, w_key, preferred_element_type=jnp.float32).astype(jnp.bfloat16)
        v_rows = jnp.einsum('rd,dhe->rhe', tokens, w_value, preferred_element_type=jnp.float32).astype(jnp.bfloat16)
        left_k, left_v = lax.ppermute((k_rows[n_rows - WIN:], v_rows[n_rows - WIN:]), 'sp', to_right)
        right_k, right_v = lax.ppermute((k_rows[:WIN], v_rows[:WIN]), 'sp', to_left)
        k_ext = jnp.concatenate([left_k, k_rows, right_k], axis=0)
        v_ext = jnp.concatenate([left_v, v_rows, right_v], axis=0)
        local_idx = glob_pos - first_row
        owned = (local_idx >= 0) & (local_idx < n_rows)
        safe_idx = jnp.clip(local_idx, 0, n_rows - 1)
        picked = (pick_rows(q_rows, safe_idx, owned), pick_rows(k_rows, safe_idx, owned), pick_rows(v_rows, safe_idx, owned))
        q_glob, k_glob, v_glob = lax.psum(picked, 'sp')
        attn_rows = local_window(q_rows, k_ext, v_ext, k_glob, v_glob, glob_pos, first_row, n_rows * n_seq)
        glob_out = global_queries(q_glob, k_rows, v_rows)
        attn_rows = attn_rows.at[jnp.where(owned, local_idx, n_rows)].set(glob_out, mode='drop')
        mixed = lax.psum(jnp.einsum('rhe,hed->rd', attn_rows, w_out, preferred_element_type=jnp.float32), 'tp')
        hidden = (tokens.astype(jnp.float32) + mixed).astype(jnp.bfloat16)
        gelu_rows = jax.nn.gelu(jnp.dot(hidden, w_up, preferred_element_type=jnp.float32), approximate=True).astype(jnp.bfloat16)
        down_sum = lax.psum(jnp.dot(gelu_rows, w_down, preferred_element_type=jnp.float32), 'tp')
        return (hidden.astype(jnp.float32) + down_sum).astype(jnp.bfloat16)

    row_spec = P(('dp', 'sp'), None)
    head_spec = P(None, 'tp', None)
    in_specs = (row_spec, P('dp'), head_spec, head_spec, head_spec, P('tp', None, None), P(None, 'tp'), P('tp', None))
    return jax.shard_map(device_layer, mesh=mesh, in_specs=in_specs, out_specs=row_spec, check_vma=False)
```

profile of v0, /device:TPU:0, one launch (start us, length us, event | category | flops | bytes accessed | tf_op | source)
XLA Modules:
  0.0 1820.1 jit_solution(4913214338254444654)
XLA Ops:
  6.5 5.9 fusion.46
  13.5 3.1 collective-permute-start
  17.9 2.4 bitcast_convert_fusion
  22.3 5.2 collective-permute-start.2
  28.8 4.7 copy.21
  33.5 6.9 copy.19
  41.0 9.7 gather_fusion.1
  50.7 2.3 copy.22
  53.0 9.7 gather_fusion
  62.7 2.3 copy.20
  65.0 5.8 fusion.47
  72.5 6.9 copy.24
  79.4 9.7 gather_fusion.2
  89.1 2.3 copy.25
  91.3 2.6 select_select_fusion
  94.2 2.7 pad_maximum_fusion
  96.9 2.6 pad_maximum_fusion.1
  99.5 40.6 %all-reduce.10.cloned.1.call-done = (bf16[1024,4,64]{0,2,1:T(8,128)(2,1)}, bf16[1024,4,64]{0,2,1:T(8,128)(2,1)}, bf16[1024,4,64]{0,2,1:T(8,128)(2,1)}) async-done(((bf16[1024,4,64]{0,2,1:T(8,128)(2,1)}, bf16[1024,4,64]{0,2,1:T(8,128)(2,1)}, bf16[1024,4,64]{0,2,1:T(8,128)(2,1)}), (bf16[1024,4,64]{0,2,1:T(8,128)(2,1)}, bf16[1024,4,64]{0,2,1:T(8,128)(2,1)}, ...) | async-done | bytes 1572880 | tf_op jit(solution)/shard_map/psum | solution.py:78
  140.1 25.7 %multiply_reduce_fusion.1 = (f32[4,1024]{1,0:T(4,128)S(1)}, f32[4,1024,4096]{2,1,0:T(8,128)}) fusion(bf16[1024,4,64]{0,2,1:T(8,128)(2,1)} %get-tuple-element.154, bf16[4096,4,64]{0,2,1:T(8,128)(2,1)} %copy-done.1), kind=kOutput, calls=%fused_computation.37 | convolution fusion | flops 2181033984 | bytes 69746688 | tf_op jit(solution)/shard_map/ghe,rhe->hgr/dot_general | solution.py:50
  165.8 10.1 pmax.7
  175.9 21.2 %fusion.18 = f32[4,1024]{1,0:T(4,128)S(1)} fusion(f32[4,1024,4096]{2,1,0:T(8,128)} %get-tuple-element.171, f32[4,1024]{1,0:T(4,128)S(1)} %pmax.7), kind=kLoop, calls=%fused_computation.38 | loop fusion | flops 50327552 | bytes 67141632 | tf_op jit(solution)/shard_map/reduce_sum | solution.py:53
  197.1 10.1 psum.52
  207.2 24.8 %fusion.35 = f32[1024,4,64]{0,2,1:T(8,128)} fusion(bf16[4096,4,64]{0,2,1:T(8,128)(2,1)S(1)} %convert_element_type.53, f32[4,1024,4096]{2,1,0:T(8,128)} %get-tuple-element.171, f32[4,1024]{1,0:T(4,128)S(1)} %psum.52, f32[4,1024]{1,0:T(4,128)S(1)} %pmax.7), kind=kOutput, calls=%fused_computation.60 | convolution fusion | flops 2214592512 | bytes 70287360 | tf_op jit(solution)/shard_map/hgr,rhe->ghe/dot_general | solution.py:55
  232.0 26.5 %all-reduce.11 = bf16[1024,4,64]{0,2,1:T(8,128)(2,1)S(1)} all-reduce(f32[1024,4,64]{0,2,1:T(8,128)} %fusion.35), channel_id=1, replica_groups=mesh['dp'=2,'tp'=4,'sp'=4] {'sp'}, use_global_device_ids=true, to_apply=%region_14.16 | all-reduce | flops 262144 | bytes 1572864 | tf_op jit(solution)/shard_map/psum | solution.py:56
  259.2 284.5 %while.12 = (s32[]{:T(128)}, bf16[32,128,4,64]{1,3,2,0:T(8,128)(2,1)}, s32[32]{0:T(128)S(1)}, bf16[4608,4,64]{0,2,1:T(8,128)(2,1)}, s32[]{:T(128)}, /*index=5*/s...) while((s32[]{:T(128)}, ...), condition=%wide.region_8.10_spmd, body=%wide.region_2.9_spmd.sunk | while | flops 227150720 | bytes 14696248 | solution.py:39
  275.0 2.1 fusion.82
  292.7 2.1 fusion.82
  328.3 2.1 fusion.82
  355.0 2.1 fusion.82
  363.9 2.1 fusion.82
  372.7 2.1 fusion.82
  381.6 2.1 fusion.82
  390.5 2.1 fusion.82
  408.3 2.1 fusion.82
  417.2 2.1 fusion.82
  435.0 2.1 fusion.82
  461.6 2.1 fusion.82
  470.5 2.1 fusion.82
  497.2 2.1 fusion.82
  523.9 2.1 fusion.82
  541.7 2.1 fusion.82
  543.8 7.0 copy.23
  550.7 94.2 %scatter_fusion = bf16[4096,4,64]{2,1,0:T(4,128)(2,1)} fusion(bf16[4096,4,64]{2,1,0:T(4,128)(2,1)} %bitcast.59, s32[1024]{0:T(1024)S(1)} %copy-done.5, bf16[1024,4,64]{2,1,0:T(4,128)(2,1)S(1)} %copy.26), kind=kCustom, calls=%fused_computation.3 | custom fusion | bytes 1576960 | tf_op jit(solution)/shard_map/scatter | solution.py:81
  645.0 10.3 convolution_bitcast_fusion.2
  655.6 560.6 %all-reduce.6.cloned.1.call-done = f32[4096,1024]{1,0:T(8,128)} async-done(((f32[4096,1024]{1,0:T(8,128)}), f32[4096,1024]{1,0:T(8,128)}) %all-reduce.6.cloned.1.call-update) | async-done | bytes 16777232 | tf_op jit(solution)/shard_map/psum | solution.py:82
  1216.2 20.6 %fusion.28 = f32[4096,1024]{1,0:T(8,128)} fusion(bf16[656,1024]{1,0:T(8,128)(2,1)S(1)} %copy-done, bf16[1024,656]{0,1:T(8,128)(2,1)S(1)} %copy-done.6, f32[4096,1024]{1,0:T(8,128)} %all-reduce.6.cloned.1.call-done, bf16[4096,1024]{1,0:T(8,128)(2,1)} %param.12), kind=kOutput, calls=%fused_computation.52 | convolution fusion | flops 11042619392 | bytes 44630016 | tf_op jit(solution)/shard_map/dot_general | solution.py:85
  1236.8 558.6 %all-reduce.8.cloned.1.call-done = f32[4096,1024]{1,0:T(8,128)} async-done(((f32[4096,1024]{1,0:T(8,128)}), f32[4096,1024]{1,0:T(8,128)}) %all-reduce.8.cloned.1.call-update) | async-done | bytes 16777232 | tf_op jit(solution)/shard_map/psum | solution.py:85
  1795.5 18.1 add_convert_fusion
  (535 shorter events, 235.6 us)
Async XLA Ops:
  6.5 1209.6 %copy-start = (bf16[656,1024]{1,0:T(8,128)(2,1)S(1)}, bf16[656,1024]{1,0:T(8,128)(2,1)}, u32[]{:S(2)}) copy-start(bf16[656,1024]{1,0:T(8,128)(2,1)} %param.19) | copy-start | bytes 4030468
  6.5 133.6 %all-reduce.10.cloned.1.call-start = ((), (), s32[]{:S(2)}) async-start(), calls=%async_computation.2 | async-start | bytes 3145728 | tf_op jit(solution)/shard_map/psum | solution.py:78
  6.5 11.3 copy-start.3
  12.5 5.4 copy-start.7
  13.5 80.7 %collective-permute-start = (bf16[256,4,64]{0,2,1:T(8,128)(2,1)}, bf16[256,4,64]{0,2,1:T(8,128)(2,1)}, u32[]{:S(2)}, u32[]{:S(2)}) collective-permute-start(bf16[256,4,64]{0,2,1:T(8,128)(2,1)} %get-tuple-element.161), channel_id=1, source_target_pairs={{0,1},{1,2},{2,3},{4,5},{5,6},{6,7},{8,9},{9,10},{10,11},{12,13},{... | collective-permute-start | bytes 393224 | tf_op jit(solution)/shard_map/ppermute | solution.py:70
  16.6 77.6 %collective-permute-start.1 = (bf16[256,4,64]{0,2,1:T(8,128)(2,1)}, bf16[256,4,64]{0,2,1:T(8,128)(2,1)}, u32[]{:S(2)}, u32[]{:S(2)}) collective-permute-start(bf16[256,4,64]{0,2,1:T(8,128)(2,1)} %get-tuple-element.162), channel_id=1, source_target_pairs={{1,0},{2,1},{3,2},{5,4},{6,5},{7,6},{9,8},{10,9},{11,10},{13,12},{... | collective-permute-start | bytes 393224 | tf_op jit(solution)/shard_map/ppermute | solution.py:71
  20.3 1.3 copy-start.1
  22.3 74.6 %collective-permute-start.2 = (bf16[256,4,64]{0,2,1:T(8,128)(2,1)}, bf16[256,4,64]{0,2,1:T(8,128)(2,1)}, u32[]{:S(2)}, u32[]{:S(2)}) collective-permute-start(bf16[256,4,64]{0,2,1:T(8,128)(2,1)} %get-tuple-element.159), channel_id=1, source_target_pairs={{0,1},{1,2},{2,3},{4,5},{5,6},{6,7},{8,9},{9,10},{10,11},{12,13},{... | collective-permute-start | bytes 393224 | tf_op jit(solution)/shard_map/ppermute | solution.py:70
  27.5 69.4 %collective-permute-start.3 = (bf16[256,4,64]{0,2,1:T(8,128)(2,1)}, bf16[256,4,64]{0,2,1:T(8,128)(2,1)}, u32[]{:S(2)}, u32[]{:S(2)}) collective-permute-start(bf16[256,4,64]{0,2,1:T(8,128)(2,1)} %get-tuple-element.160), channel_id=1, source_target_pairs={{1,0},{2,1},{3,2},{5,4},{6,5},{7,6},{9,8},{10,9},{11,10},{13,12},{... | collective-permute-start | bytes 393224 | tf_op jit(solution)/shard_map/ppermute | solution.py:71
  33.5 7.0 copy-start.4
  93.9 1122.2 %all-reduce.6.cloned.1.call-start = ((), (), s32[]{:S(2)}) async-start(), calls=%async_computation | async-start | bytes 33554432 | tf_op jit(solution)/shard_map/psum | solution.py:82
  94.2 2.7 copy-start.2
  259.3 6.1 copy-start.9
  268.2 6.1 copy-start.9
  277.1 6.1 copy-start.9
  285.9 6.1 copy-start.9
  294.8 6.1 copy-start.9
  303.7 6.1 copy-start.9
  312.6 6.1 copy-start.9
  321.5 6.1 copy-start.9
  330.4 6.1 copy-start.9
  339.3 6.1 copy-start.9
  348.2 6.1 copy-start.9
  357.1 6.1 copy-start.9
  366.0 6.1 copy-start.9
  374.8 6.1 copy-start.9
  383.7 6.1 copy-start.9
  392.6 6.1 copy-start.9
  401.5 6.1 copy-start.9
  410.4 6.1 copy-start.9
  419.3 6.1 copy-start.9
  428.2 6.1 copy-start.9
  437.1 6.1 copy-start.9
  446.0 6.1 copy-start.9
  454.8 6.1 copy-start.9
  463.7 6.1 copy-start.9
  472.6 6.1 copy-start.9
  481.5 6.1 copy-start.9
  490.4 6.1 copy-start.9
  499.3 6.1 copy-start.9
  508.2 6.1 copy-start.9
  517.1 6.1 copy-start.9
  526.0 6.1 copy-start.9
  534.9 6.1 copy-start.9
  543.8 7.0 copy-start.5
  543.8 101.2 %copy-start.8 = (bf16[4,64,1024]{2,1,0:T(8,128)(2,1)S(1)}, bf16[4,64,1024]{2,1,0:T(8,128)(2,1)}, u32[]{:S(2)}) copy-start(bf16[4,64,1024]{2,1,0:T(8,128)(2,1)} %param.17) | copy-start | bytes 1572868
  655.3 560.9 %copy-start.6 = (bf16[1024,656]{0,1:T(8,128)(2,1)S(1)}, bf16[1024,656]{0,1:T(8,128)(2,1)}, u32[]{:S(2)}) copy-start(bf16[1024,656]{0,1:T(8,128)(2,1)} %param.18) | copy-start | bytes 4030468
  655.3 1140.2 %all-reduce.8.cloned.1.call-start = ((), (), s32[]{:S(2)}) async-start(), calls=%async_computation.1 | async-start | bytes 33554432 | tf_op jit(solution)/shard_map/psum | solution.py:85
Sparse Core Ops, SparseCore 0:
  94.1 45.9 all-reduce.9
  655.4 560.7 all-reduce.5
  1237.0 558.4 all-reduce.7
where the time goes:
time: 1830 us; the launch traced here: 1820 us
  waiting for transfers between devices  1160 us (63%)
  matrix products  285 us (16%)
  local copies, waits for them, and re-layouts  180 us (10%)
  other arithmetic  98.8 us (5%)
  blocking collectives  46.7 us (3%)
  loops' own time  24.8 us (1%)
    psum x1, waiting for transfers between devices, device_layer(): lax.psum(jnp.einsum('rhe,hed->rd', attn_rows, w_out, preferred_element_ty...  561 us
    psum x1, waiting for transfers between devices, device_layer(): lax.psum(jnp.dot(gelu_rows, w_down, preferred_element_type=jnp.float32),...  559 us
    scatter x1, local copies, waits for them, and re-layouts, device_layer(): attn_rows.at[jnp.where(owned, local_idx, n_rows)].set(glob_out, mode='drop')  94.2 us
    dot_general x32, matrix products, one_block(): jnp.einsum('hqk,khe->qhe', p_win, v_blk, preferred_element_type=jnp.float32)  66.7 us
    dot_general x32, matrix products, one_block(): jnp.einsum('qhe,ghe->hqg', q_blk, k_glob, preferred_element_type=jnp.floa...  52.7 us
    dot_general x32, matrix products, one_block(): jnp.einsum('qhe,khe->hqk', q_blk, k_blk, preferred_element_type=jnp.float32)  48.2 us
    psum x1, waiting for transfers between devices, device_layer(): q_glob, k_glob, v_glob = lax.psum(picked, 'sp')  40.6 us
  transfers between devices with their start and end apart: 7, of which 3 were waited for; matrix products, arithmetic and copies ran while one was open for 4% of the time, Pallas kernels for 0%

commit v1 on v0

v1 whole, which is shorter than its diff:
```python
import functools
import math

import jax
import jax.numpy as jnp
from jax import lax
from jax.experimental import pallas as pl
from jax.experimental.pallas import tpu as pltpu
from jax.sharding import PartitionSpec as P

WIN = 256
QB = 256
FLOOR = -3.0e38
F32 = jnp.float32
BF16 = jnp.bfloat16
NT = (((1,), (1,)), ((), ()))


def dot_nt(a, b):
    return lax.dot_general(a, b, NT, preferred_element_type=F32)


def dot_nn(a, b):
    return jnp.dot(a, b, preferred_element_type=F32)


def params(n_axes, vmem_mib=48):
    return pltpu.CompilerParams(
        dimension_semantics=("arbitrary",) * n_axes, vmem_limit_bytes=vmem_mib << 20)


def cost(flops, bytes_accessed, exps=0):
    return pl.CostEstimate(flops=int(flops), bytes_accessed=int(bytes_accessed), transcendentals=int(exps))


def stack_pair(q_pair):
    low = lax.broadcasted_iota(jnp.int32, q_pair.shape, 1) < 64
    zero = jnp.zeros_like(q_pair)
    return jnp.concatenate([jnp.where(low, q_pair, zero), jnp.where(low, zero, q_pair)], axis=0)


def merge_pair(rows):
    half = rows.shape[0] // 2
    low = lax.broadcasted_iota(jnp.int32, (half, 128), 1) < 64
    return jnp.where(low, jnp.broadcast_to(rows[:half], (half, 128)), jnp.broadcast_to(rows[half:], (half, 128)))


def pick_kernel(pos_ref, idx_ref, qkv_ref, out_ref, acc_ref):
    n_rows = qkv_ref.shape[0]
    n_pick = out_ref.shape[0]
    g0 = pl.program_id(0) * n_pick
    first, last = pos_ref[g0], pos_ref[g0 + n_pick - 1]
    acc_ref[...] = jnp.zeros_like(acc_ref)
    idx = idx_ref[...]

    @pl.loop(0, n_rows // QB)
    def _(r):
        lo = r * QB

        @pl.when((first < lo + QB) & (last >= lo))
        def _():
            hit = idx == lo + lax.broadcasted_iota(jnp.int32, (n_pick, QB), 1)
            acc_ref[...] += dot_nn(hit.astype(F32).astype(BF16), qkv_ref[pl.ds(pl.multiple_of(lo, QB), QB), :])

    out_ref[...] = acc_ref[...].astype(out_ref.dtype)


def pick_rows(qkv, local_idx):
    n_glob = local_idx.shape[0]
    n_rows, width = qkv.shape
    block = 128
    return pl.pallas_call(
        pick_kernel,
        grid_spec=pltpu.PrefetchScalarGridSpec(
            num_scalar_prefetch=1, grid=(n_glob // block,),
            in_specs=[pl.BlockSpec((block, 1), lambda i, p: (i, 0)),
                      pl.BlockSpec((n_rows, width), lambda i, p: (0, 0))],
            out_specs=pl.BlockSpec((block, width), lambda i, p: (i, 0)),
            scratch_shapes=[pltpu.VMEM((block, width), F32)]),
        out_shape=jax.ShapeDtypeStruct((n_glob, width), BF16),
        compiler_params=params(1), cost_estimate=cost(2e9, 8e6), name="pick",
    )(local_idx, local_idx[:, None], qkv)


def window_kernel(q_ref, kl_ref, kc_ref, kr_ref, vl_ref, vc_ref, vr_ref, hl_ref, hr_ref,
                  bl_ref, bc_ref, br_ref, acc_ref, m_ref, l_ref, tri_ref):
    i = pl.program_id(0)

    @pl.when(i == 0)
    def _():
        r_i = lax.broadcasted_iota(jnp.int32, (QB, QB), 0)
        c_i = lax.broadcasted_iota(jnp.int32, (QB, QB), 1)
        for half in range(2):
            tri_ref[0, half * QB:(half + 1) * QB] = jnp.where(c_i >= r_i, 0.0, -jnp.inf)
            tri_ref[1, half * QB:(half + 1) * QB] = jnp.where(c_i <= r_i, 0.0, -jnp.inf)

    is_first = i == 0
    is_last = i == pl.num_programs(0) - 1
    for pr in range(2):
        cols = slice(pr * 128, pr * 128 + 128)
        vcols = slice(256 + pr * 128, 256 + pr * 128 + 128)
        q2 = stack_pair(q_ref[:, cols])
        kl = jnp.where(is_first, hl_ref[:, cols], kl_ref[:, cols])
        kr = jnp.where(is_last, hr_ref[:, cols], kr_ref[:, cols])
        vl = jnp.where(is_first, hl_ref[:, vcols], vl_ref[:, cols])
        vr = jnp.where(is_last, hr_ref[:, vcols], vr_ref[:, cols])
        s_l = dot_nt(q2, kl) + (tri_ref[0] + bl_ref[...])
        s_c = dot_nt(q2, kc_ref[:, cols]) + bc_ref[...]
        s_r = dot_nt(q2, kr) + (tri_ref[1] + br_ref[...])
        top = jnp.max(jnp.maximum(jnp.maximum(s_l, s_c), s_r), axis=1, keepdims=True)
        top = jnp.maximum(top, FLOOR)
        e_l, e_c, e_r = jnp.exp(s_l - top), jnp.exp(s_c - top), jnp.exp(s_r - top)
        total = jnp.sum(e_l + e_c + e_r, axis=1, keepdims=True)
        acc = dot_nn(e_l.astype(BF16), vl) + dot_nn(e_c.astype(BF16), vc_ref[:, cols]) + dot_nn(e_r.astype(BF16), vr)
        acc_ref[:, cols] = merge_pair(acc)
        m_ref[:, cols] = merge_pair(top)
        l_ref[:, cols] = merge_pair(total)


def window_part(qkv, halo_l, halo_r, bias):
    n_rows = qkv.shape[0]
    n_blk = n_rows // QB
    left = lambda c: pl.BlockSpec((QB, 256), lambda i: (jnp.maximum(i - 1, 0), c))
    mid = lambda c: pl.BlockSpec((QB, 256), lambda i: (i, c))
    right = lambda c: pl.BlockSpec((QB, 256), lambda i: (jnp.minimum(i + 1, n_blk - 1), c))
    whole = lambda a: pl.BlockSpec(a.shape, lambda i: (0,) * a.ndim)
    out = jax.ShapeDtypeStruct((n_rows, 256), F32)
    return pl.pallas_call(
        window_kernel, grid=(n_blk,),
        in_specs=[mid(0), left(1), mid(1), right(1), left(2), mid(2), right(2), whole(halo_l), whole(halo_r),
                  pl.BlockSpec((1, QB), lambda i: (0, i)), pl.BlockSpec((1, QB), lambda i: (0, i + 1)),
                  pl.BlockSpec((1, QB), lambda i: (0, i + 2))],
        out_specs=[pl.BlockSpec((QB, 256), lambda i: (i, 0))] * 3,
        out_shape=[out, out, out], scratch_shapes=[pltpu.VMEM((2, 2 * QB, QB), F32)],
        compiler_params=params(1), cost_estimate=cost(30e9, 30e6, 12e6), name="window_part",
    )(qkv, qkv, qkv, qkv, qkv, qkv, qkv, halo_l, halo_r, bias, bias, bias)


def global_keys_kernel(q_ref, kg_ref, vg_ref, acc_ref, m_ref, l_ref, out_ref):
    for pr in range(2):
        cols = slice(pr * 128, pr * 128 + 128)
        q2 = stack_pair(q_ref[:, cols])
        s = dot_nt(q2, kg_ref[:, cols])
        top = merge_pair(jnp.max(s, axis=1, keepdims=True))
        m_win = m_ref[:, cols]
        m_all = jnp.maximum(top, m_win)
        alpha = jnp.exp(m_win - m_all)
        m_rows = jnp.concatenate([m_all[:, :1], m_all[:, 64:65]], axis=0)
        e = jnp.exp(s - m_rows)
        total = merge_pair(jnp.sum(e, axis=1, keepdims=True)) + alpha * l_ref[:, cols]
        acc = merge_pair(dot_nn(e.astype(BF16), vg_ref[:, cols])) + alpha * acc_ref[:, cols]
        out_ref[:, cols] = (acc / total).astype(out_ref.dtype)


def global_keys_part(qkv, qkv_g, acc, m, l, chunk, n_chunks):
    n_rows = qkv.shape[0] // n_chunks
    n_glob = qkv_g.shape[0]
    n_blk = n_rows // QB
    row = pl.BlockSpec((QB, 256), lambda i: (chunk * n_blk + i, 0))
    return pl.pallas_call(
        global_keys_kernel, grid=(n_blk,),
        in_specs=[row, pl.BlockSpec((n_glob, 256), lambda i: (0, 1)), pl.BlockSpec((n_glob, 256), lambda i: (0, 2)),
                  row, row, row],
        out_specs=pl.BlockSpec((QB, 256), lambda i: (i, 0)),
        out_shape=jax.ShapeDtypeStruct((n_rows, 256), BF16),
        compiler_params=params(1), cost_estimate=cost(40e9 / n_chunks, 20e6 / n_chunks, 16e6 / n_chunks),
        name="global_keys",
    )(qkv, qkv_g, qkv_g, acc, m, l)


def global_queries_kernel(q_ref, k_ref, v_ref, out_ref, acc_ref, m_ref, l_ref):
    j = pl.program_id(1)

    @pl.when(j == 0)
    def _():
        acc_ref[...] = jnp.zeros_like(acc_ref)
        l_ref[...] = jnp.zeros_like(l_ref)
        m_ref[...] = jnp.full_like(m_ref, FLOOR)

    for pr in range(2):
        cols = slice(pr * 128, pr * 128 + 128)
        q2 = stack_pair(q_ref[:, cols])
        s = dot_nt(q2, k_ref[:, cols])
        m_old = m_ref[pr]
        m_new = jnp.maximum(m_old, jnp.max(s, axis=1, keepdims=True))
        alpha = jnp.exp(m_old - m_new)
        e = jnp.exp(s - m_new[:, :1])
        part = e[:, :128]
        for c in range(1, e.shape[1] // 128):
            part = part + e[:, c * 128:(c + 1) * 128]
        l_ref[pr] = alpha * l_ref[pr] + part
        acc_ref[pr] = alpha * acc_ref[pr] + dot_nn(e.astype(BF16), v_ref[:, cols])
        m_ref[pr] = m_new

    @pl.when(j == pl.num_programs(1) - 1)
    def _():
        for pr in range(2):
            out_ref[:, pr * 128:pr * 128 + 128] = merge_pair(acc_ref[pr])
            out_ref[:, 256 + pr * 128:256 + pr * 128 + 128] = merge_pair(m_ref[pr])
            out_ref[:, 512 + pr * 128:512 + pr * 128 + 128] = merge_pair(jnp.sum(l_ref[pr], axis=1, keepdims=True))


def global_queries_part(qkv_g, qkv):
    n_glob = qkv_g.shape[0]
    n_rows = qkv.shape[0]
    kb = 1024
    return pl.pallas_call(
        global_queries_kernel, grid=(n_glob // QB, n_rows // kb),
        in_specs=[pl.BlockSpec((QB, 256), lambda i, j: (i, 0)), pl.BlockSpec((kb, 256), lambda i, j: (j, 1)),
                  pl.BlockSpec((kb, 256), lambda i, j: (j, 2))],
        out_specs=pl.BlockSpec((QB, 768), lambda i, j: (i, 0)),
        out_shape=jax.ShapeDtypeStruct((n_glob, 768), F32),
        scratch_shapes=[pltpu.VMEM((2, 2 * QB, 128), F32)] * 3,
        compiler_params=params(2), cost_estimate=cost(34e9, 20e6, 16e6), name="global_queries",
    )(qkv_g, qkv, qkv)


def place_kernel(pos_ref, idx_ref, glob_ref, o_ref, out_ref, acc_ref, hit_ref, *, chunk_row):
    lo = chunk_row + pl.program_id(0) * QB
    acc_ref[...] = jnp.zeros_like(acc_ref)
    hit_ref[...] = jnp.zeros_like(hit_ref)

    @pl.loop(0, glob_ref.shape[0] // 128)
    def _(b):
        g0 = b * 128

        @pl.when((pos_ref[g0] < lo + QB) & (pos_ref[g0 + 127] >= lo))
        def _():
            g = pl.multiple_of(g0, 128)
            hit = idx_ref[:, pl.ds(g, 128)] == lo + lax.broadcasted_iota(jnp.int32, (QB, 128), 0)
            hit = hit.astype(F32)
            acc_ref[...] += dot_nn(hit.astype(BF16), glob_ref[pl.ds(g, 128), :])
            hit_ref[...] += hit

    mine = jnp.sum(hit_ref[...], axis=1, keepdims=True) > 0.5
    out_ref[...] = jnp.where(mine, acc_ref[...], o_ref[...].astype(F32)).astype(out_ref.dtype)


def place_rows(o, glob_out, local_idx, chunk_row):
    n_rows, width = o.shape
    n_glob = local_idx.shape[0]
    return pl.pallas_call(
        functools.partial(place_kernel, chunk_row=chunk_row),
        grid_spec=pltpu.PrefetchScalarGridSpec(
            num_scalar_prefetch=1, grid=(n_rows // QB,),
            in_specs=[pl.BlockSpec((1, n_glob), lambda i, p: (0, 0)), pl.BlockSpec((n_glob, width), lambda i, p: (0, 0)),
                      pl.BlockSpec((QB, width), lambda i, p: (i, 0))],
            out_specs=pl.BlockSpec((QB, width), lambda i, p: (i, 0)),
            scratch_shapes=[pltpu.VMEM((QB, width), F32), pltpu.VMEM((QB, 128), F32)]),
        out_shape=jax.ShapeDtypeStruct((n_rows, width), BF16),
        compiler_params=params(1), cost_estimate=cost(1e9, 2e6), name="place",
    )(local_idx, local_idx[None, :], glob_out, o)


def mlp_kernel(x_ref, o_ref, w_ref, *refs, n_tp, n_rep, d_o, d_f):
    y_ref, wo_ref, w2_ref, w1_ref, sem = refs[-5:]

    @pl.when(pl.program_id(0) == 0)
    def _():
        copies = []
        piece = wo_ref.shape[1] // n_rep
        for j in range(n_rep):
            for t in range(n_tp):
                lanes = pl.ds(j * piece, piece)
                copies.append(pltpu.make_async_copy(
                    w_ref.at[j, t, pl.ds(0, d_o)], wo_ref.at[pl.ds(t * d_o, d_o), lanes], sem))
                copies.append(pltpu.make_async_copy(
                    w_ref.at[j, t, pl.ds(d_o, d_f)], w2_ref.at[pl.ds(t * d_f, d_f), lanes], sem))
                copies.append(pltpu.make_async_copy(
                    w_ref.at[j, t, pl.ds(d_o + d_f, d_f)], w1_ref.at[pl.ds(t * d_f, d_f), lanes], sem))
        for c in copies:
            c.start()
        for c in copies:
            c.wait()

    mixed = dot_nn(o_ref[0], wo_ref[:d_o, :])
    for t in range(1, n_tp):
        mixed += dot_nn(o_ref[t], wo_ref[t * d_o:(t + 1) * d_o, :])
    h = (x_ref[...].astype(F32) + mixed).astype(BF16)
    width = n_tp * d_f
    acc = h.astype(F32)
    for f0 in range(0, width, 512):
        f1 = min(f0 + 512, width)
        z = dot_nt(h, w1_ref[f0:f1, :])
        u = 0.5 * z * (1.0 + jnp.tanh(math.sqrt(2.0 / math.pi) * (z + 0.044715 * (z * z * z))))
        acc += dot_nn(u.astype(BF16), w2_ref[f0:f1, :])
    y_ref[...] = acc.astype(y_ref.dtype)


def mlp_rows(tokens, o_all, w_all, y, chunk, d_o, d_f):
    n_tp, n_rows, _ = o_all.shape
    n_rep = w_all.shape[0]
    dim = tokens.shape[1]
    rb = min(512, n_rows)
    n_blk = n_rows // rb
    earlier = () if y is None else (y,)
    return pl.pallas_call(
        functools.partial(mlp_kernel, n_tp=n_tp, n_rep=n_rep, d_o=d_o, d_f=d_f), grid=(n_blk,),
        in_specs=[pl.BlockSpec((rb, dim), lambda i: (chunk * n_blk + i, 0)),
                  pl.BlockSpec((n_tp, rb, d_o), lambda i: (0, i, 0)),
                  pl.BlockSpec(memory_space=pl.ANY)] + [pl.BlockSpec(memory_space=pl.ANY)] * len(earlier),
        out_specs=pl.BlockSpec((rb, dim), lambda i: (chunk * n_blk + i, 0)),
        out_shape=jax.ShapeDtypeStruct(tokens.shape, BF16),
        input_output_aliases={3: 0} if earlier else {},
        scratch_shapes=[pltpu.VMEM((n_tp * d_o, dim), BF16), pltpu.VMEM((n_tp * d_f, dim), BF16),
                        pltpu.VMEM((n_tp * d_f, dim), BF16), pltpu.SemaphoreType.DMA],
        compiler_params=params(1, 56), cost_estimate=cost(2 * n_rows * dim * (dim + 2 * n_tp * d_f), 20e6), name="mlp",
    )(tokens, o_all, w_all, *earlier)


def combine(a, b):
    acc_a, m_a, l_a = a[:, :256], a[:, 256:512], a[:, 512:]
    acc_b, m_b, l_b = b[:, :256], b[:, 256:512], b[:, 512:]
    m = jnp.maximum(m_a, m_b)
    e_a, e_b = jnp.exp(m_a - m), jnp.exp(m_b - m)
    return acc_a * e_a + acc_b * e_b, m, l_a * e_a + l_b * e_b


def solution(mesh):
    n_seq = mesh.shape['sp']
    to_right = [(i, i + 1) for i in range(n_seq - 1)]
    to_left = [(i + 1, i) for i in range(n_seq - 1)]
    core_swap = [(i, i ^ 1) for i in range(n_seq)]
    chip_swap = [(i, i ^ 2) for i in range(n_seq)]

    def device_layer(tokens, glob_pos, w_query, w_key, w_value, w_out, w_up, w_down):
        n_rows, dim = tokens.shape
        n_glob = glob_pos.shape[0]
        sp = lax.axis_index('sp')
        core, chip = sp % 2, sp // 2
        first_row = sp * n_rows
        seq_len = n_rows * n_seq
        local_idx = glob_pos - first_row

        d_o, d_f = w_out.shape[0] * w_out.shape[1], w_down.shape[0]
        shard = jnp.concatenate([w_out.reshape(d_o, dim), w_down, w_up.T], axis=0)
        rep = lax.axis_index('dp') * n_seq + sp
        n_tp, n_rep = mesh.shape['tp'], mesh.shape['dp'] * n_seq
        piece = dim // n_rep
        w_slice = lax.dynamic_slice_in_dim(shard, rep * piece, piece, axis=1)
        w_all = lax.all_gather(w_slice, ('dp', 'sp', 'tp'))
        w_all = w_all.reshape(n_rep, n_tp, d_o + 2 * d_f, piece)

        w_cat = jnp.concatenate([w_query.reshape(dim, -1) * jnp.asarray(0.125, BF16),
                                 w_key.reshape(dim, -1), w_value.reshape(dim, -1)], axis=1)
        qkv = jnp.dot(tokens, w_cat, preferred_element_type=F32).astype(BF16)
        halo_l = lax.ppermute(qkv[n_rows - WIN:, 256:], 'sp', to_right)
        halo_r = lax.ppermute(qkv[:WIN, 256:], 'sp', to_left)

        k_pos = first_row - WIN + jnp.arange(n_rows + 2 * WIN)
        k_off = jnp.any(glob_pos[:, None] == k_pos[None, :], axis=0) | (k_pos < 0) | (k_pos >= seq_len)
        bias = jnp.where(k_off, -jnp.inf, 0.0).astype(F32)[None, :]

        picked = pick_rows(qkv, local_idx)
        half = n_glob // 2
        mine = lax.dynamic_slice_in_dim(picked, core * half, half)
        other = lax.ppermute(lax.dynamic_slice_in_dim(picked, (1 - core) * half, half), 'sp', core_swap)
        mine = mine + other
        got = lax.ppermute(mine, 'sp', chip_swap)
        acc, m, l = window_part(qkv, halo_l, halo_r, bias)
        got, acc = lax.optimization_barrier((got, acc))
        mine = mine + got
        other = lax.ppermute(mine, 'sp', core_swap)
        qkv_g = jnp.concatenate([jnp.where(core == 0, mine, other), jnp.where(core == 0, other, mine)], axis=0)

        part = global_queries_part(qkv_g, qkv)

        quarter = n_glob // 4
        got = lax.ppermute(lax.dynamic_slice_in_dim(part, (1 - core) * half, half), 'sp', core_swap)
        joined = jnp.concatenate(combine(lax.dynamic_slice_in_dim(part, core * half, half), got), axis=1)
        got = lax.ppermute(lax.dynamic_slice_in_dim(joined, (1 - chip) * quarter, quarter), 'sp', chip_swap)
        n_chunks = 4
        o_first = global_keys_part(qkv, qkv_g, acc, m, l, 0, n_chunks)
        got, o_first = lax.optimization_barrier((got, o_first))
        g_acc, _, g_l = combine(lax.dynamic_slice_in_dim(joined, chip * quarter, quarter), got)
        mine = (g_acc / g_l).astype(BF16)
        other = lax.ppermute(mine, 'sp', chip_swap)
        mine = jnp.concatenate([jnp.where(chip == 0, mine, other), jnp.where(chip == 0, other, mine)], axis=0)
        other = lax.ppermute(mine, 'sp', core_swap)
        glob_out = jnp.concatenate([jnp.where(core == 0, mine, other), jnp.where(core == 0, other, mine)], axis=0)

        glob_out, w_all = lax.optimization_barrier((glob_out, w_all))
        y = None
        for c in range(n_chunks):
            o = o_first if c == 0 else global_keys_part(qkv, qkv_g, acc, m, l, c, n_chunks)
            o = place_rows(o, glob_out, local_idx, c * (n_rows // n_chunks))
            o_all = lax.all_gather(o, 'tp')
            y = mlp_rows(tokens, o_all, w_all, y, c, d_o, d_f)
        return y

    row_spec = P(('dp', 'sp'), None)
    head_spec = P(None, 'tp', None)
    in_specs = (row_spec, P('dp'), head_spec, head_spec, head_spec, P('tp', None, None), P(None, 'tp'), P('tp', None))
    return jax.shard_map(device_layer, mesh=mesh, in_specs=in_specs, out_specs=row_spec, check_vma=False)
```

time: 1830 us -> 377 us (0.21)
  waiting for transfers between devices: 1160 us -> 91.3 us
  matrix products: 285 us -> 11.7 us
  Pallas kernels: 0 us -> 229 us
  local copies, waits for them, and re-layouts: 180 us -> 5.89 us
  other arithmetic: 98.8 us -> 9.64 us
  blocking collectives: 46.7 us -> 0 us
  loops' own time: 24.8 us -> 0 us
    psum x3 -> x0, waiting for transfers between devices: 1160 us -> none  [the longest x1 561 us: device_layer(): lax.psum(jnp.einsum('rhe,hed->rd', attn_rows, w_out, preferred_element_ty...]
    dot_general x132 -> x1, matrix products: 271 us -> 11.7 us  [device_layer(): qkv = jnp.dot(tokens, w_cat, preferred_element_type=F32).astype(BF16)]
    pallas_call x0 -> x15, Pallas kernels: none -> 229 us  [the longest x4 93.6 us: mlp_rows(): pl.pallas_call(functools.partial(mlp_kernel, n_tp=n_tp, n_rep=n_rep, d_o=...]
    scatter x1 -> x0, local copies, waits for them, and re-layouts: 94.2 us -> none  [device_layer(): attn_rows.at[jnp.where(owned, local_idx, n_rows)].set(glob_out, mode='drop')]
    all_gather x0 -> x5, waiting for transfers between devices: none -> 73.4 us  [the longest x4 73.3 us: device_layer(): o_all = lax.all_gather(o, 'tp')]
    reduce_sum x65 -> x0, other arithmetic: 49.8 us -> none  [the longest x1 21.2 us: global_queries(): glob_sum = lax.psum(jnp.sum(exp_scores, axis=2, keepdims=True), 'sp')]
    psum x2 -> x0, blocking collectives: 36.6 us -> none  [the longest x1 26.5 us: global_queries(): return lax.psum(part_out, 'sp').astype(jnp.bfloat16)]
    gather x6 -> x0, local copies, waits for them, and re-layouts: 35.9 us -> none  [pick_rows(): picked = jnp.take(row_array, safe_idx, axis=0)]
  transfers between devices with their start and end apart: 7 -> 14, of which waited for: 3 -> 9; matrix products, arithmetic and copies ran while one was open for 4% -> 6% of each run, Pallas kernels for 0% -> 54%
where the time goes in v1:
time: 377 us; the launch traced here: 373 us
  Pallas kernels  229 us (61%)
  waiting for transfers between devices  91.3 us (24%)
  between operations  14 us (4%)
  starting transfers between devices  11.7 us (3%)
  matrix products  11.7 us (3%)
  other arithmetic  9.64 us (3%)
  local copies, waits for them, and re-layouts  5.89 us (2%)
    pallas_call x4, Pallas kernels, mlp_rows(): pl.pallas_call(functools.partial(mlp_kernel, n_tp=n_tp, n_rep=n_rep, d_o=...  93.6 us
    all_gather x4, waiting for transfers between devices, device_layer(): o_all = lax.all_gather(o, 'tp')  73.3 us
    pallas_call x1, Pallas kernels, global_queries_part(): pl.pallas_call(global_queries_kernel, grid=(n_glob // QB, n_rows // kb),...  42 us
    pallas_call x4, Pallas kernels, global_keys_part(): pl.pallas_call(global_keys_kernel, grid=(n_blk,), in_specs=[row, pl.Block...  40.8 us
    pallas_call x1, Pallas kernels, window_part(): pl.pallas_call(window_kernel, grid=(n_blk,), in_specs=[mid(0), left(1), m...  30.4 us
    pallas_call x4, Pallas kernels, place_rows(): pl.pallas_call(functools.partial(place_kernel, chunk_row=chunk_row), grid...  12.9 us
    dot_general x1, matrix products, device_layer(): qkv = jnp.dot(tokens, w_cat, preferred_element_type=F32).astype(BF16)  11.7 us
    pallas_call x1, Pallas kernels, pick_rows(): pl.pallas_call(pick_kernel, grid_spec=pltpu.PrefetchScalarGridSpec(num_sc...  9.54 us
  transfers between devices with their start and end apart: 14, of which 9 were waited for; matrix products, arithmetic and copies ran while one was open for 6% of the time, Pallas kernels for 54%

profile of v1, /device:TPU:0, one launch (start us, length us, event | category | flops | bytes accessed | tf_op | source)
XLA Modules:
  0.0 373.5 jit_solution(10271887206212845646)
XLA Ops:
  6.5 1.9 fusion.9
  8.6 11.7 %fusion.qkv_ref.q_ref.kl_ref.kc_ref.kr_ref.vl_ref.vc_ref.vr_ref.k_ref.v_ref = bf16[4096,768]{1,0:T(8,128)(2,1)S(1)} fusion(bf16[4096,1024]{1,0:T(8,128)(2,1)} %x_ref.7, bf16[1024,256]{0,1:T(8,128)(2,1)S(1)} %bitcast.31, bf16[1024,256]{0,1:T(8,128)(2,1)S(1)} %bitcast.32, bf16[1024,256]{0,1:T(8,128)(2,1)S(1)} %bitcast.21), kind=kOutput, calls=%fused_computation.2 | convolution fusion | flops 6450315264 | bytes 16252928 | tf_op jit(solution)/shard_map/dot_general | solution.py:346
  20.4 1.3 collective-permute-start.3
  21.7 1.3 copy-done.3
  23.0 3.0 collective-permute-start.2
  26.0 0.2 copy.16.idx_ref
  26.2 9.5 %pick.1 = bf16[1024,768]{1,0:T(8,128)(2,1)S(1)} custom-call(s32[1024]{0:T(1024)S(1)} %broadcast_subtract_fusion.pos_ref, s32[1024,1]{1,0:T(8,128)S(1)} %copy.16.idx_ref, bf16[4096,768]{1,0:T(8,128)(2,1)} %copy-done.3), custom_call_target="tpu_custom_call" | custom-call | flops 2000000000 | bytes 8000000 | tf_op jit(solution)/shard_map/pick/pallas_call | solution.py:72
  35.8 0.9 constant_dynamic-slice_fusion.2
  36.7 2.8 collective-permute-start
  39.6 2.5 compare_reduce_fusion
  42.2 1.3 dynamic-slice_add_fusion
  43.6 30.4 %window_part.1 = (f32[4096,256]{1,0:T(8,128)S(1)}, f32[4096,256]{1,0:T(8,128)}, f32[4096,256]{1,0:T(8,128)}) custom-call(bf16[4096,768]{1,0:T(8,128)(2,1)} %copy-done.3, bf16[4096,768]{1,0:T(8,128)(2,1)} %copy-done.3, bf16[4096,768]{1,0:T(8,128)(2,1)} %copy-done.3, bf16[4096,768]{1,0:T(8,128)(2,1)} %copy-done.3, bf16[4096,768]{1,0:T(8,128)(2,1)} %copy-done.3, ...), custom_call_target="tpu_custom_call" | custom-call | flops 30000001024 | bytes 30000000 | tf_op jit(solution)/shard_map/window_part/pallas_call | solution.py:128
  73.9 2.0 copy-done.2
  76.0 0.2 add.72
  76.2 2.3 collective-permute-done.4
  78.5 0.1 broadcast_select_fusion.1
  78.6 0.1 pad_maximum_fusion.q_ref.kg_ref.vg_ref
  78.7 42.0 %global_queries.1 = f32[1024,768]{1,0:T(8,128)S(1)} custom-call(bf16[1024,768]{1,0:T(8,128)(2,1)S(1)} %pad_maximum_fusion.q_ref.kg_ref.vg_ref, bf16[4096,768]{1,0:T(8,128)(2,1)} %copy-done.3, bf16[4096,768]{1,0:T(8,128)(2,1)} %copy-done.3), custom_call_target="tpu_custom_call" | custom-call | flops 33999998976 | bytes 20000000 | tf_op jit(solution)/shard_map/global_queries/pallas_call | solution.py:207
  120.7 1.2 constant_dynamic-slice_fusion.1
  122.0 0.2 collective-permute-start.5
  122.2 3.2 collective-permute-done.5
  125.3 1.5 fusion.7
  126.8 1.5 fusion.6
  128.3 0.1 pad_maximum_fusion.1
  128.4 2.0 collective-permute-start.6
  130.5 10.2 %global_keys.4.o_ref = bf16[1024,256]{1,0:T(8,128)(2,1)S(1)} custom-call(bf16[4096,768]{1,0:T(8,128)(2,1)} %copy-done.3, bf16[1024,768]{1,0:T(8,128)(2,1)S(1)} %copy-done.1, bf16[1024,768]{1,0:T(8,128)(2,1)S(1)} %copy-done.1, f32[4096,256]{1,0:T(8,128)} %copy-done.2, f32[4096,256]{1,0:T(8,128)} %get-tuple-element.17.m_ref, f32[4096,256]{1,0:T(8,128)} %get-tuple-element.18.l_ref), custom_call_target="tpu_custom_call" | custom-call | flops 10000000000 | bytes 5000000 | tf_op jit(solution)/shard_map/global_keys/pallas_call | solution.py:160
  140.7 7.7 %collective-permute-done.6 = f32[256,768]{1,0:T(8,128)S(1)} collective-permute-done((f32[256,768]{1,0:T(8,128)S(1)}, f32[256,768]{1,0:T(8,128)S(1)}, u32[]{:S(2)}, u32[]{:S(2)}) %collective-permute-start.6) | collective-permute-done | bytes 786464 | tf_op jit(solution)/shard_map/ppermute | solution.py:371
  148.4 0.2 fusion.15
  148.5 1.8 collective-permute-start.7
  150.3 3.2 collective-permute-done.7
  153.7 1.5 collective-permute-done.8
  155.2 0.1 broadcast_select_fusion.3
  155.4 3.2 place.7
  158.6 0.2 all-gather.17.cloned.1.call-start
  158.9 10.2 %global_keys.7.o_ref = bf16[1024,256]{1,0:T(8,128)(2,1)S(1)} custom-call(bf16[4096,768]{1,0:T(8,128)(2,1)} %copy-done.3, bf16[1024,768]{1,0:T(8,128)(2,1)S(1)} %copy-done.1, bf16[1024,768]{1,0:T(8,128)(2,1)S(1)} %copy-done.1, f32[4096,256]{1,0:T(8,128)} %copy-done.2, f32[4096,256]{1,0:T(8,128)} %get-tuple-element.17.m_ref, f32[4096,256]{1,0:T(8,128)} %get-tuple-element.18.l_ref), custom_call_target="tpu_custom_call" | custom-call | flops 10000000000 | bytes 5000000 | tf_op jit(solution)/shard_map/global_keys/pallas_call | solution.py:160
  169.1 3.2 place.6
  172.3 10.2 %global_keys.6.o_ref = bf16[1024,256]{1,0:T(8,128)(2,1)S(1)} custom-call(bf16[4096,768]{1,0:T(8,128)(2,1)} %copy-done.3, bf16[1024,768]{1,0:T(8,128)(2,1)S(1)} %copy-done.1, bf16[1024,768]{1,0:T(8,128)(2,1)S(1)} %copy-done.1, f32[4096,256]{1,0:T(8,128)} %copy-done.2, f32[4096,256]{1,0:T(8,128)} %get-tuple-element.17.m_ref, f32[4096,256]{1,0:T(8,128)} %get-tuple-element.18.l_ref), custom_call_target="tpu_custom_call" | custom-call | flops 10000000000 | bytes 5000000 | tf_op jit(solution)/shard_map/global_keys/pallas_call | solution.py:160
  182.6 3.3 place.5
  186.0 10.2 %global_keys.5.o_ref = bf16[1024,256]{1,0:T(8,128)(2,1)S(1)} custom-call(bf16[4096,768]{1,0:T(8,128)(2,1)} %copy-done.3, bf16[1024,768]{1,0:T(8,128)(2,1)S(1)} %copy-done.1, bf16[1024,768]{1,0:T(8,128)(2,1)S(1)} %copy-done.1, f32[4096,256]{1,0:T(8,128)} %copy-done.2, f32[4096,256]{1,0:T(8,128)} %get-tuple-element.17.m_ref, f32[4096,256]{1,0:T(8,128)} %get-tuple-element.18.l_ref), custom_call_target="tpu_custom_call" | custom-call | flops 10000000000 | bytes 5000000 | tf_op jit(solution)/shard_map/global_keys/pallas_call | solution.py:160
  196.2 3.2 place.4
  199.4 6.1 %all-gather.19.cloned.1.call-done = bf16[4096,256]{1,0:T(8,128)(2,1)} async-done(((bf16[1024,256]{1,0:T(8,128)(2,1)}), bf16[4096,256]{1,0:T(8,128)(2,1)}) %all-gather.19.cloned.1.call-update) | async-done | bytes 2097168 | tf_op jit(solution)/shard_map/all_gather | solution.py:387
  205.5 23.2 %mlp.4.refs_0_ = bf16[4096,1024]{1,0:T(8,128)(2,1)} custom-call(bf16[4096,1024]{1,0:T(8,128)(2,1)} %x_ref.7, bf16[4,1024,256]{2,1,0:T(8,128)(2,1)} %bitcast.27, bf16[8,4,1568,128]{3,2,1,0:T(8,128)(2,1)} %bitcast.23), custom_call_target="tpu_custom_call" | custom-call | flops 13153337344 | bytes 20000000 | tf_op jit(solution)/shard_map/mlp/pallas_call | solution.py:297
  228.7 22.7 %all-gather.17.cloned.1.call-done = bf16[4096,256]{1,0:T(8,128)(2,1)} async-done(((bf16[1024,256]{1,0:T(8,128)(2,1)}), bf16[4096,256]{1,0:T(8,128)(2,1)}) %all-gather.17.cloned.1.call-update) | async-done | bytes 2097168 | tf_op jit(solution)/shard_map/all_gather | solution.py:387
  251.4 23.4 %mlp.5.refs_0_ = bf16[4096,1024]{1,0:T(8,128)(2,1)} custom-call(bf16[4096,1024]{1,0:T(8,128)(2,1)} %x_ref.7, bf16[4,1024,256]{2,1,0:T(8,128)(2,1)} %bitcast.28, bf16[8,4,1568,128]{3,2,1,0:T(8,128)(2,1)} %bitcast.24, bf16[4096,1024]{1,0:T(8,128)(2,1)} %mlp.4.refs_0_), custom_call_target="tpu_custom_call", output_to_operand_aliasing={{}: (3, {})} | custom-call | flops 13153337344 | bytes 20000000 | tf_op jit(solution)/shard_map/mlp/pallas_call | solution.py:297
  274.8 22.3 %all-gather.15.cloned.1.call-done = bf16[4096,256]{1,0:T(8,128)(2,1)} async-done(((bf16[1024,256]{1,0:T(8,128)(2,1)}), bf16[4096,256]{1,0:T(8,128)(2,1)}) %all-gather.15.cloned.1.call-update) | async-done | bytes 2097168 | tf_op jit(solution)/shard_map/all_gather | solution.py:387
  297.2 23.5 %mlp.6.refs_0_ = bf16[4096,1024]{1,0:T(8,128)(2,1)} custom-call(bf16[4096,1024]{1,0:T(8,128)(2,1)} %x_ref.7, bf16[4,1024,256]{2,1,0:T(8,128)(2,1)} %bitcast.29, bf16[8,4,1568,128]{3,2,1,0:T(8,128)(2,1)} %bitcast.25, bf16[4096,1024]{1,0:T(8,128)(2,1)} %mlp.5.refs_0_), custom_call_target="tpu_custom_call", output_to_operand_aliasing={{}: (3, {})} | custom-call | flops 13153337344 | bytes 20000000 | tf_op jit(solution)/shard_map/mlp/pallas_call | solution.py:297
  320.6 22.3 %all-gather.13.cloned.1.call-done = bf16[4096,256]{1,0:T(8,128)(2,1)} async-done(((bf16[1024,256]{1,0:T(8,128)(2,1)}), bf16[4096,256]{1,0:T(8,128)(2,1)}) %all-gather.13.cloned.1.call-update) | async-done | bytes 2097168 | tf_op jit(solution)/shard_map/all_gather | solution.py:387
  342.9 23.5 %mlp.7 = bf16[4096,1024]{1,0:T(8,128)(2,1)} custom-call(bf16[4096,1024]{1,0:T(8,128)(2,1)} %x_ref.7, bf16[4,1024,256]{2,1,0:T(8,128)(2,1)} %bitcast.30, bf16[8,4,1568,128]{3,2,1,0:T(8,128)(2,1)} %bitcast.26, bf16[4096,1024]{1,0:T(8,128)(2,1)} %mlp.6.refs_0_), custom_call_target="tpu_custom_call", output_to_operand_aliasing={{}: (3, {})} | custom-call | flops 13153337344 | bytes 20000000 | tf_op jit(solution)/shard_map/mlp/pallas_call | solution.py:297
  (40 shorter events, 0.8 us)
Async XLA Ops:
  6.5 2.0 copy-start.4
  6.5 148.9 %all-gather.11.cloned.1.call-start = ((), (), s32[]{:S(2)}) async-start(), calls=%async_computation | async-start | bytes 13246464 | tf_op jit(solution)/shard_map/all_gather | solution.py:341
  6.5 2.1 copy-start.6
  6.5 2.1 copy-start.7
  8.5 197.0 %all-gather.19.cloned.1.call-start = ((), (), s32[]{:S(2)}) async-start(), calls=%async_computation.4 | async-start | bytes 2621440 | tf_op jit(solution)/shard_map/all_gather | solution.py:387
  8.6 17.4 %copy-start.5 = (s32[1024]{0:T(1024)S(1)}, s32[1024]{0:T(1024)}, u32[]{:S(2)}) copy-start(s32[1024]{0:T(1024)} %param.9) | copy-start | bytes 12292
  20.3 2.7 copy-start.3
  20.4 23.2 %collective-permute-start.3 = (bf16[256,512]{1,0:T(8,128)(2,1)S(1)}, bf16[256,512]{1,0:T(8,128)(2,1)S(1)}, u32[]{:S(2)}, u32[]{:S(2)}) collective-permute-start(bf16[256,512]{1,0:T(8,128)(2,1)S(1)} %get-tuple-element.25), channel_id=1, source_target_pairs={{1,0},{2,1},{3,2},{5,4},{6,5},{7,6},{9,8},{10,9},{11,10},{13,12},{... | collective-permute-start | bytes 786440 | tf_op jit(solution)/shard_map/ppermute | solution.py:348
  23.0 20.6 %collective-permute-start.2 = (bf16[256,512]{1,0:T(8,128)(2,1)S(1)}, bf16[256,512]{1,0:T(8,128)(2,1)S(1)}, u32[]{:S(2)}, u32[]{:S(2)}) collective-permute-start(bf16[256,512]{1,0:T(8,128)(2,1)S(1)} %get-tuple-element.26), channel_id=1, source_target_pairs={{0,1},{1,2},{2,3},{4,5},{5,6},{6,7},{8,9},{9,10},{10,11},{12,13},{... | collective-permute-start | bytes 786440 | tf_op jit(solution)/shard_map/ppermute | solution.py:347
  36.7 5.4 %collective-permute-start = (bf16[512,768]{1,0:T(8,128)(2,1)}, bf16[512,768]{1,0:T(8,128)(2,1)}, u32[]{:S(2)}, u32[]{:S(2)}) collective-permute-start(bf16[512,768]{1,0:T(8,128)(2,1)} %constant_dynamic-slice_fusion.2), channel_id=1, source_target_pairs={{0,1},{1,0},{2,3},{3,2},{4,5},{5,4},{6,7},{7,6},{8,9},{9,8},{10,11... | collective-permute-start | bytes 2359304 | tf_op jit(solution)/shard_map/ppermute | solution.py:357
  43.5 32.5 %collective-permute-start.1 = (bf16[512,768]{1,0:T(8,128)(2,1)S(1)}, bf16[512,768]{1,0:T(8,128)(2,1)S(1)}, u32[]{:S(2)}, u32[]{:S(2)}) collective-permute-start(bf16[512,768]{1,0:T(8,128)(2,1)S(1)} %dynamic-slice_add_fusion), channel_id=1, source_target_pairs={{0,2},{1,3},{2,0},{3,1},{4,6},{5,7},{6,4},{7,5},{8,10},{9,11},{10,... | collective-permute-start | bytes 2359304 | tf_op jit(solution)/shard_map/ppermute | solution.py:359
  73.9 2.0 copy-start.2
  76.2 2.4 collective-permute-start.4
  78.7 42.0 %copy-start = (bf16[1024,768]{1,0:T(8,128)(2,1)}, bf16[1024,768]{1,0:T(8,128)(2,1)S(1)}, u32[]{:S(2)}) copy-start(bf16[1024,768]{1,0:T(8,128)(2,1)S(1)} %pad_maximum_fusion.q_ref.kg_ref.vg_ref) | copy-start | bytes 4718596
  122.0 3.4 collective-permute-start.5
  128.2 2.2 copy-start.1
  128.4 19.9 %collective-permute-start.6 = (f32[256,768]{1,0:T(8,128)S(1)}, f32[256,768]{1,0:T(8,128)S(1)}, u32[]{:S(2)}, u32[]{:S(2)}) collective-permute-start(f32[256,768]{1,0:T(8,128)S(1)} %constant_dynamic-slice_fusion), channel_id=1, source_target_pairs={{0,2},{1,3},{2,0},{3,1},{4,6},{5,7},{6,4},{7,5},{8,10},{9,11},{10,... | collective-permute-start | bytes 2359304 | tf_op jit(solution)/shard_map/ppermute | solution.py:371
  148.5 5.0 %collective-permute-start.7 = (bf16[256,256]{1,0:T(8,128)(2,1)S(1)}, bf16[256,256]{1,0:T(8,128)(2,1)S(1)}, u32[]{:S(2)}, u32[]{:S(2)}) collective-permute-start(bf16[256,256]{1,0:T(8,128)(2,1)S(1)} %fusion.15), channel_id=1, source_target_pairs={{0,2},{1,3},{2,0},{3,1},{4,6},{5,7},{6,4},{7,5},{8,10},{9,11},{10,... | collective-permute-start | bytes 393224 | tf_op jit(solution)/shard_map/ppermute | solution.py:377
  153.6 1.6 collective-permute-start.8
  158.6 92.8 %all-gather.17.cloned.1.call-start = ((), (), s32[]{:S(2)}) async-start(), calls=%async_computation.3 | async-start | bytes 2621440 | tf_op jit(solution)/shard_map/all_gather | solution.py:387
  172.3 124.9 %all-gather.15.cloned.1.call-start = ((), (), s32[]{:S(2)}) async-start(), calls=%async_computation.2 | async-start | bytes 2621440 | tf_op jit(solution)/shard_map/all_gather | solution.py:387
  185.9 157.0 %all-gather.13.cloned.1.call-start = ((), (), s32[]{:S(2)}) async-start(), calls=%async_computation.1 | async-start | bytes 2621440 | tf_op jit(solution)/shard_map/all_gather | solution.py:387
Sparse Core Ops, SparseCore 0:
  10.2 99.3 all-gather.10
  158.8 46.7 all-gather.18
  207.1 44.2 all-gather.16
  252.8 44.2 all-gather.14
  298.6 44.2 all-gather.12

commit v2 on v0

v2 whole, which is shorter than its diff:
```python
import functools
import math

import jax
import jax.numpy as jnp
from jax import lax
from jax.experimental import pallas as pl
from jax.experimental.pallas import tpu as pltpu
from jax.sharding import PartitionSpec as P

WIN = 256
QB = 256
CHUNKS = (4, 4, 4, 4)
FLOOR = -3.0e38
F32 = jnp.float32
BF16 = jnp.bfloat16
NT = (((1,), (1,)), ((), ()))


def dot_nt(a, b):
    return lax.dot_general(a, b, NT, preferred_element_type=F32)


def dot_nn(a, b):
    return jnp.dot(a, b, preferred_element_type=F32)


def params(n_axes, vmem_mib=48):
    return pltpu.CompilerParams(
        dimension_semantics=("arbitrary",) * n_axes, vmem_limit_bytes=vmem_mib << 20)


def cost(flops, bytes_accessed, exps=0):
    return pl.CostEstimate(flops=int(flops), bytes_accessed=int(bytes_accessed), transcendentals=int(exps))


def head_sums(rows):
    n = rows.shape[1]
    r = lax.broadcasted_iota(jnp.int32, (n, n), 0) // 64
    c = lax.broadcasted_iota(jnp.int32, (n, n), 1) // 64
    pick = jnp.where(r == (c + 1 - 2 * (c % 2)), 1.0, 0.0).astype(BF16)
    wide = rows.astype(F32)
    return dot_nn((wide * wide).astype(BF16), pick)


def qkv_kernel(pos_ref, idx_ref, x_ref, w_ref, qkv_ref, pick_ref, kmax_ref, acc_ref):
    step = pl.program_id(0)
    n_blk = x_ref.shape[0]
    lo = step * n_blk
    gb = 128

    @pl.when(step == 0)
    def _():
        acc_ref[...] = jnp.zeros_like(acc_ref)
        kmax_ref[...] = jnp.zeros_like(kmax_ref)

    rows = dot_nn(x_ref[...], w_ref[...]).astype(BF16)
    qkv_ref[...] = rows
    kmax_ref[...] = jnp.maximum(kmax_ref[...], jnp.max(head_sums(rows[:, 256:512]), axis=0, keepdims=True))

    @pl.loop(0, idx_ref.shape[0] // gb)
    def _(b):
        g0 = pl.multiple_of(b * gb, gb)

        @pl.when((pos_ref[g0] < lo + n_blk) & (pos_ref[g0 + gb - 1] >= lo))
        def _():
            hit = idx_ref[pl.ds(g0, gb), :] == lo + lax.broadcasted_iota(jnp.int32, (gb, n_blk), 1)
            acc_ref[pl.ds(g0, gb), :] += dot_nn(hit.astype(F32).astype(BF16), qkv_ref[...])

    @pl.when(step == pl.num_programs(0) - 1)
    def _():
        pick_ref[...] = acc_ref[...].astype(pick_ref.dtype)


def qkv_part(tokens, w_cat, local_idx):
    n_rows, dim = tokens.shape
    n_glob = local_idx.shape[0]
    width = w_cat.shape[1]
    rb = 512
    return pl.pallas_call(
        qkv_kernel,
        grid_spec=pltpu.PrefetchScalarGridSpec(
            num_scalar_prefetch=1, grid=(n_rows // rb,),
            in_specs=[pl.BlockSpec((n_glob, 1), lambda i, p: (0, 0)), pl.BlockSpec((rb, dim), lambda i, p: (i, 0)),
                      pl.BlockSpec((dim, width), lambda i, p: (0, 0))],
            out_specs=[pl.BlockSpec((rb, width), lambda i, p: (i, 0)), pl.BlockSpec((n_glob, width), lambda i, p: (0, 0)),
                       pl.BlockSpec((1, 256), lambda i, p: (0, 0))],
            scratch_shapes=[pltpu.VMEM((n_glob, width), F32)]),
        out_shape=[jax.ShapeDtypeStruct((n_rows, width), BF16), jax.ShapeDtypeStruct((n_glob, width), BF16),
                   jax.ShapeDtypeStruct((1, 256), F32)],
        compiler_params=params(1), cost_estimate=cost(8e9, 24e6), name="qkv",
    )(local_idx, local_idx[:, None], tokens, w_cat)


def low_lanes(n):
    return lax.broadcasted_iota(jnp.int32, (n, 128), 1) < 64


def shifts(q, kmax):
    return (-1.02 * jnp.sqrt(head_sums(q) * kmax)).astype(BF16)


def own_half(pair, other, half):
    low = low_lanes(pair.shape[0])
    return jnp.where(low, pair, other) if half == 0 else jnp.where(low, other, pair)


def query_rows(q, neg, half):
    lane = lax.broadcasted_iota(jnp.int32, q.shape, 1) % 64
    return own_half(q, jnp.where(lane == 0, neg, jnp.ones_like(neg)), half)


def key_extra(n):
    return jnp.where(lax.broadcasted_iota(jnp.int32, (n, 128), 1) % 64 == 0, 1.0, 0.0).astype(BF16)


def stream(q_rows, tiles):
    acc = total = None
    for keys, values in tiles:
        e = jnp.exp(dot_nt(q_rows, keys))
        part = e[:, :128] + e[:, 128:]
        out = dot_nn(e.astype(BF16), values)
        acc = out if acc is None else acc + out
        total = part if total is None else total + part
    return acc, total


def row_sum(lanes):
    return jnp.sum(lanes, axis=1, keepdims=True)


def out_of_range(*totals):
    good = [jnp.logical_and(jnp.min(t) > 1e-25, jnp.max(t) < 1e30) for t in totals]
    return jnp.logical_not(functools.reduce(jnp.logical_and, good))


def exact_head(q, half, n_keys, key_rows, acc_ref, m_ref, l_ref):
    low = low_lanes(q.shape[0])
    q1 = jnp.where(low if half == 0 else jnp.logical_not(low), q, jnp.zeros_like(q))
    acc_ref[half] = jnp.zeros(q.shape, F32)
    l_ref[half] = jnp.zeros(q.shape, F32)
    m_ref[half] = jnp.full(q.shape, FLOOR, F32)

    @pl.loop(0, n_keys // 256)
    def _(c):
        keys, values, bias = key_rows(c)
        s = dot_nt(q1, keys)
        if bias is not None:
            s = s + bias
        m_old = m_ref[half]
        m_new = jnp.maximum(m_old, jnp.max(s, axis=1, keepdims=True))
        alpha = jnp.exp(m_old - m_new)
        e = jnp.exp(s - m_new[:, :1])
        l_ref[half] = alpha * l_ref[half] + row_sum(e)
        acc_ref[half] = alpha * acc_ref[half] + dot_nn(e.astype(BF16), values)
        m_ref[half] = m_new


def window_kernel(q_ref, kl_ref, kc_ref, kr_ref, vl_ref, vc_ref, vr_ref, hkl_ref, hkr_ref, hvl_ref, hvr_ref,
                  extra_ref, bias_ref, kmax_ref, acc_ref, m_ref, l_ref, tri_ref, key_ref, val_ref, ea_ref, em_ref, el_ref):
    i = pl.program_id(1)
    n = q_ref.shape[0]
    is_first = i == 0
    is_last = i == pl.num_programs(1) - 1

    @pl.when(i == 0)
    def _():
        r_i = lax.broadcasted_iota(jnp.int32, (QB, QB), 0)
        c_i = lax.broadcasted_iota(jnp.int32, (QB, QB), 1)
        tri_ref[:QB] = jnp.where(c_i <= r_i, 0.0, -jnp.inf)
        tri_ref[QB:2 * QB] = jnp.zeros((QB, QB), F32)
        tri_ref[2 * QB:] = jnp.where(c_i >= r_i, 0.0, -jnp.inf)

    key_ref[:QB] = jnp.where(is_first, hkl_ref[...], kl_ref[...])
    key_ref[QB:QB + n] = kc_ref[...]
    key_ref[QB + n:] = jnp.where(is_last, hkr_ref[...], kr_ref[...])
    val_ref[:QB] = jnp.where(is_first, hvl_ref[...], vl_ref[...])
    val_ref[QB:QB + n] = vc_ref[...]
    val_ref[QB + n:] = jnp.where(is_last, hvr_ref[...], vr_ref[...])

    q = q_ref[...]
    neg = shifts(q, kmax_ref[...])
    accs, sums = [], []
    for half in range(2):
        qx = query_rows(q, neg, half)
        acc, total = [None] * (n // QB), [None] * (n // QB)
        for t in range(n // QB + 2):
            b0, b1 = max(t - 2, 0), min(t + 1, n // QB)
            extra = extra_ref[pl.ds(pl.multiple_of(i * n + t * QB, QB), QB), :]
            s = dot_nt(qx[b0 * QB:b1 * QB], own_half(key_ref[t * QB:(t + 1) * QB], extra, half))
            e = jnp.exp(s + window_mask(tri_ref, t, b0, b1))
            part = e[:, :128] + e[:, 128:]
            out = dot_nn(e.astype(BF16), val_ref[t * QB:(t + 1) * QB])
            for b in range(b0, b1):
                r = slice((b - b0) * QB, (b - b0 + 1) * QB)
                acc[b] = out[r] if acc[b] is None else acc[b] + out[r]
                total[b] = part[r] if total[b] is None else total[b] + part[r]
        accs.append(jnp.concatenate(acc, axis=0))
        sums.append(row_sum(jnp.concatenate(total, axis=0)))
    low = low_lanes(n)
    acc_ref[...] = jnp.where(low, accs[0], accs[1])
    l_ref[...] = jnp.where(low, sums[0], sums[1])
    m_ref[...] = -pltpu.roll(neg.astype(F32), 64, 1)

    @pl.when(out_of_range(*sums))
    def _():
        @pl.loop(0, n // QB)
        def _(b):
            rows = pl.ds(pl.multiple_of(b * QB, QB), QB)

            def key_rows(c):
                at = pl.ds(pl.multiple_of((b + c) * QB, QB), QB)
                bias = bias_ref[:, pl.ds(pl.multiple_of(i * n + (b + c) * QB, QB), QB)]
                return key_ref[at], val_ref[at], bias + tri_ref[pl.ds(pl.multiple_of((2 - c) * QB, QB), QB)]

            for half in range(2):
                exact_head(q_ref[rows], half, 3 * QB, key_rows, ea_ref, em_ref, el_ref)
            low = low_lanes(QB)
            for out, src in ((acc_ref, ea_ref), (m_ref, em_ref), (l_ref, el_ref)):
                out[rows] = jnp.where(low, src[0], src[1])


def window_mask(tri_ref, t, b0, b1):
    return tri_ref[(b0 - t + 2) * QB:(b1 - t + 2) * QB]


def window_part(qkv, halo_l, halo_r, extra, bias, kmax):
    n_rows = qkv.shape[0]
    rb = min(1024, n_rows)
    per = rb // QB
    n_blk, n_small = n_rows // rb, n_rows // QB
    mid = lambda c: pl.BlockSpec((rb, 128), lambda p, i: (i, 2 * c + p))
    left = lambda c: pl.BlockSpec((QB, 128), lambda p, i: (jnp.maximum(i * per - 1, 0), 2 * c + p))
    right = lambda c: pl.BlockSpec((QB, 128), lambda p, i: (jnp.minimum(i * per + per, n_small - 1), 2 * c + p))
    halo = lambda c: pl.BlockSpec((QB, 128), lambda p, i: (0, 2 * c + p))
    whole = lambda a: pl.BlockSpec(a.shape, lambda p, i: (0,) * a.ndim)
    out = jax.ShapeDtypeStruct((n_rows, 256), F32)
    pair = pltpu.VMEM((2, QB, 128), F32)
    return pl.pallas_call(
        window_kernel, grid=(2, n_blk),
        in_specs=[mid(0), left(1), mid(1), right(1), left(2), mid(2), right(2), halo(0), halo(0), halo(1), halo(1),
                  whole(extra), whole(bias), pl.BlockSpec((1, 128), lambda p, i: (0, p))],
        out_specs=[pl.BlockSpec((rb, 128), lambda p, i: (i, p))] * 3,
        out_shape=[out, out, out],
        scratch_shapes=[pltpu.VMEM((3 * QB, QB), F32), pltpu.VMEM((rb + 2 * QB, 128), BF16),
                        pltpu.VMEM((rb + 2 * QB, 128), BF16), pair, pair, pair],
        compiler_params=params(2), cost_estimate=cost(30e9, 30e6, 12e6), name="window_part",
    )(qkv, qkv, qkv, qkv, qkv, qkv, qkv, halo_l, halo_r, halo_l, halo_r, extra, bias, kmax)


def global_keys_kernel(q_ref, kg_ref, vg_ref, kmax_ref, acc_ref, m_ref, l_ref, idx_ref, glob_ref, out_ref,
                       k_ref, o_ref, ea_ref, em_ref, el_ref, *, first):
    n = q_ref.shape[0]
    i = pl.program_id(1)

    @pl.when(i == 0)
    def _():
        extra = key_extra(kg_ref.shape[0])
        for half in range(2):
            k_ref[half] = own_half(kg_ref[...], extra, half)

    def finish(acc, m, total):
        m_all = jnp.maximum(m, m_ref[...])
        a, b = jnp.exp(m - m_all), jnp.exp(m_ref[...] - m_all)
        o_ref[...] = (acc * a + acc_ref[...] * b) / (total * a + l_ref[...] * b)

    q = q_ref[...]
    neg = shifts(q, kmax_ref[...])
    low = low_lanes(n)
    res = [stream(query_rows(q, neg, half), [(k_ref[half, t:t + 256], vg_ref[t:t + 256]) for t in range(0, vg_ref.shape[0], 256)])
           for half in range(2)]
    sums = [row_sum(r[1]) for r in res]
    finish(jnp.where(low, res[0][0], res[1][0]), -pltpu.roll(neg.astype(F32), 64, 1), jnp.where(low, sums[0], sums[1]))

    @pl.when(out_of_range(*sums))
    def _():
        def key_rows(c):
            at = pl.ds(pl.multiple_of(c * 256, 256), 256)
            return kg_ref[at], vg_ref[at], None

        for half in range(2):
            exact_head(q_ref[...], half, vg_ref.shape[0], key_rows, ea_ref, em_ref, el_ref)
        finish(*(jnp.where(low, r[0], r[1]) for r in (ea_ref, em_ref, el_ref)))

    row = first * QB + i * n + lax.broadcasted_iota(jnp.int32, (n, 1), 0)
    hit = jnp.where(idx_ref[...] == row, 1.0, 0.0)
    placed = dot_nn(hit.astype(BF16), glob_ref[...])
    mine = row_sum(hit) > 0.5
    out_ref[...] = jnp.where(mine, placed, o_ref[...]).astype(out_ref.dtype)


def global_keys_part(qkv, qkv_g, kmax, win, local_idx, glob_out, first, n_blk):
    n_glob = qkv_g.shape[0]
    rb = min(512, n_blk * QB)
    base = first * QB // rb
    n_rows = n_blk * QB
    row = pl.BlockSpec((rb, 128), lambda p, i: (base + i, p))
    whole = lambda a: pl.BlockSpec(a.shape, lambda p, i: (0,) * a.ndim)
    idx = local_idx[None, :]
    pair = pltpu.VMEM((2, rb, 128), F32)
    return pl.pallas_call(
        functools.partial(global_keys_kernel, first=first), grid=(2, n_rows // rb),
        in_specs=[row, pl.BlockSpec((n_glob, 128), lambda p, i: (0, 2 + p)), pl.BlockSpec((n_glob, 128), lambda p, i: (0, 4 + p)),
                  pl.BlockSpec((1, 128), lambda p, i: (0, p)), row, row, row, whole(idx),
                  pl.BlockSpec((n_glob, 128), lambda p, i: (0, p))],
        out_specs=pl.BlockSpec((rb, 128), lambda p, i: (i, p)),
        out_shape=jax.ShapeDtypeStruct((n_rows, 256), BF16),
        scratch_shapes=[pltpu.VMEM((2, n_glob, 128), BF16), pltpu.VMEM((rb, 128), F32), pair, pair, pair],
        compiler_params=params(2), cost_estimate=cost(2.5e9 * n_blk, 2e6 * n_blk, 1e6 * n_blk),
        name="global_keys",
    )(qkv, qkv_g, qkv_g, kmax, *win, idx, glob_out)


def global_queries_kernel(q_ref, k_ref, v_ref, kmax_ref, out_ref, acc_ref, m_ref, l_ref, *, kb):
    j = pl.program_id(2)
    n = q_ref.shape[0]
    low = low_lanes(n)

    @pl.when(j == 0)
    def _():
        acc_ref[...] = jnp.zeros_like(acc_ref)
        l_ref[...] = jnp.zeros_like(l_ref)

    extra = key_extra(256)
    q = q_ref[...]
    neg = shifts(q, kmax_ref[...])
    for half in range(2):
        rows = [pl.ds(pl.multiple_of(j * kb, kb) + t, 256) for t in range(0, kb, 256)]
        acc, total = stream(query_rows(q, neg, half), [(own_half(k_ref[r], extra, half), v_ref[r]) for r in rows])
        acc_ref[half] += acc
        l_ref[half] += total

    @pl.when(j == pl.num_programs(2) - 1)
    def _():
        sums = [row_sum(l_ref[half]) for half in range(2)]
        out_ref[0] = jnp.where(low, acc_ref[0], acc_ref[1])
        out_ref[1] = -pltpu.roll(neg.astype(F32), 64, 1)
        out_ref[2] = jnp.where(low, sums[0], sums[1])

        @pl.when(out_of_range(*sums))
        def _():
            def key_rows(c):
                at = pl.ds(pl.multiple_of(c * 256, 256), 256)
                return k_ref[at], v_ref[at], None

            for half in range(2):
                exact_head(q_ref[...], half, v_ref.shape[0], key_rows, acc_ref, m_ref, l_ref)
            for k, r in enumerate((acc_ref, m_ref, l_ref)):
                out_ref[k] = jnp.where(low, r[0], r[1])


def global_queries_part(qkv_g, qkv, kmax):
    n_glob = qkv_g.shape[0]
    n_rows = qkv.shape[0]
    rb = 512
    kb = min(1024, n_rows)
    return pl.pallas_call(
        functools.partial(global_queries_kernel, kb=kb), grid=(2, n_glob // rb, n_rows // kb),
        in_specs=[pl.BlockSpec((rb, 128), lambda p, i, j: (i, p)), pl.BlockSpec((n_rows, 128), lambda p, i, j: (0, 2 + p)),
                  pl.BlockSpec((n_rows, 128), lambda p, i, j: (0, 4 + p)), pl.BlockSpec((1, 128), lambda p, i, j: (0, p))],
        out_specs=pl.BlockSpec((3, rb, 128), lambda p, i, j: (0, i, p)),
        out_shape=jax.ShapeDtypeStruct((3, n_glob, 256), F32),
        scratch_shapes=[pltpu.VMEM((2, rb, 128), F32)] * 3,
        compiler_params=params(3), cost_estimate=cost(34e9, 20e6, 16e6), name="global_queries",
    )(qkv_g, qkv, qkv, kmax)


def mlp_kernel(x_ref, o_ref, w_ref, *refs, n_tp, n_rep, d_o, d_f):
    y_ref, wo_ref, w2_ref, w1_ref, sem = refs[-5:]

    @pl.when(pl.program_id(0) == 0)
    def _():
        copies = []
        piece = wo_ref.shape[1] // n_rep
        for j in range(n_rep):
            for t in range(n_tp):
                lanes = pl.ds(j * piece, piece)
                copies.append(pltpu.make_async_copy(
                    w_ref.at[j, t, pl.ds(0, d_o)], wo_ref.at[pl.ds(t * d_o, d_o), lanes], sem))
                copies.append(pltpu.make_async_copy(
                    w_ref.at[j, t, pl.ds(d_o, d_f)], w2_ref.at[pl.ds(t * d_f, d_f), lanes], sem))
                copies.append(pltpu.make_async_copy(
                    w_ref.at[j, t, pl.ds(d_o + d_f, d_f)], w1_ref.at[pl.ds(t * d_f, d_f), lanes], sem))
        for c in copies:
            c.start()
        for c in copies:
            c.wait()

    mixed = dot_nn(o_ref[0], wo_ref[:d_o, :])
    for t in range(1, n_tp):
        mixed += dot_nn(o_ref[t], wo_ref[t * d_o:(t + 1) * d_o, :])
    h = (x_ref[...].astype(F32) + mixed).astype(BF16)
    width = n_tp * d_f
    acc = h.astype(F32)
    for f0 in range(0, width, 512):
        f1 = min(f0 + 512, width)
        z = dot_nt(h, w1_ref[f0:f1, :])
        u = 0.5 * z * (1.0 + jnp.tanh(math.sqrt(2.0 / math.pi) * (z + 0.044715 * (z * z * z))))
        acc += dot_nn(u.astype(BF16), w2_ref[f0:f1, :])
    y_ref[...] = acc.astype(y_ref.dtype)


def mlp_rows(tokens, o_all, w_all, y, first, d_o, d_f):
    n_tp, n_rows, _ = o_all.shape
    n_rep = w_all.shape[0]
    dim = tokens.shape[1]
    rb = min(512, n_rows)
    n_blk = n_rows // rb
    base = first * QB // rb
    earlier = () if y is None else (y,)
    return pl.pallas_call(
        functools.partial(mlp_kernel, n_tp=n_tp, n_rep=n_rep, d_o=d_o, d_f=d_f), grid=(n_blk,),
        in_specs=[pl.BlockSpec((rb, dim), lambda i: (base + i, 0)),
                  pl.BlockSpec((n_tp, rb, d_o), lambda i: (0, i, 0)),
                  pl.BlockSpec(memory_space=pl.ANY)] + [pl.BlockSpec(memory_space=pl.ANY)] * len(earlier),
        out_specs=pl.BlockSpec((rb, dim), lambda i: (base + i, 0)),
        out_shape=jax.ShapeDtypeStruct(tokens.shape, BF16),
        input_output_aliases={3: 0} if earlier else {},
        scratch_shapes=[pltpu.VMEM((n_tp * d_o, dim), BF16), pltpu.VMEM((n_tp * d_f, dim), BF16),
                        pltpu.VMEM((n_tp * d_f, dim), BF16), pltpu.SemaphoreType.DMA],
        compiler_params=params(1, 56), cost_estimate=cost(2 * n_rows * dim * (dim + 2 * n_tp * d_f), 20e6), name="mlp",
    )(tokens, o_all, w_all, *earlier)


def combine(a, b):
    m = jnp.maximum(a[1], b[1])
    e_a, e_b = jnp.exp(a[1] - m), jnp.exp(b[1] - m)
    return a[0] * e_a + b[0] * e_b, m, a[2] * e_a + b[2] * e_b


def solution(mesh):
    n_seq = mesh.shape['sp']
    to_right = [(i, i + 1) for i in range(n_seq - 1)]
    to_left = [(i + 1, i) for i in range(n_seq - 1)]
    core_swap = [(i, i ^ 1) for i in range(n_seq)]
    chip_swap = [(i, i ^ 2) for i in range(n_seq)]

    def device_layer(tokens, glob_pos, w_query, w_key, w_value, w_out, w_up, w_down):
        n_rows, dim = tokens.shape
        n_glob = glob_pos.shape[0]
        sp = lax.axis_index('sp')
        core, chip = sp % 2, sp // 2
        first_row = sp * n_rows
        seq_len = n_rows * n_seq
        local_idx = glob_pos - first_row

        d_o, d_f = w_out.shape[0] * w_out.shape[1], w_down.shape[0]
        shard = jnp.concatenate([w_out.reshape(d_o, dim), w_down, w_up.T], axis=0)
        rep = lax.axis_index('dp') * n_seq + sp
        n_tp, n_rep = mesh.shape['tp'], mesh.shape['dp'] * n_seq
        piece = dim // n_rep
        w_slice = lax.dynamic_slice_in_dim(shard, rep * piece, piece, axis=1)
        w_all = lax.all_gather(w_slice, ('dp', 'sp', 'tp'))
        w_all = w_all.reshape(n_rep, n_tp, d_o + 2 * d_f, piece)

        w_cat = jnp.concatenate([w_query.reshape(dim, -1) * jnp.asarray(0.125, BF16),
                                 w_key.reshape(dim, -1), w_value.reshape(dim, -1)], axis=1)
        qkv, picked, kmax = qkv_part(tokens, w_cat, local_idx)
        halo_l = lax.ppermute(qkv[n_rows - WIN:, 256:], 'sp', to_right)
        halo_r = lax.ppermute(qkv[:WIN, 256:], 'sp', to_left)

        k_pos = first_row - WIN + jnp.arange(n_rows + 2 * WIN)
        k_off = jnp.any(glob_pos[:, None] == k_pos[None, :], axis=0) | (k_pos < 0) | (k_pos >= seq_len)
        bias = jnp.where(k_off, -jnp.inf, 0.0).astype(F32)[None, :]
        lane = jnp.arange(128) % 64
        extra = jnp.where(lane == 0, 1.0, jnp.where((lane == 1) & k_off[:, None], FLOOR, 0.0)).astype(BF16)

        half = n_glob // 2
        mine = lax.dynamic_slice_in_dim(picked, core * half, half)
        other = lax.ppermute(lax.dynamic_slice_in_dim(picked, (1 - core) * half, half), 'sp', core_swap)
        mine = mine + other
        got = lax.ppermute(mine, 'sp', chip_swap)
        win = window_part(qkv, halo_l, halo_r, extra, bias, kmax)
        got, win = lax.optimization_barrier((got, win))
        mine = mine + got
        other = lax.ppermute(mine, 'sp', core_swap)
        qkv_g = jnp.concatenate([jnp.where(core == 0, mine, other), jnp.where(core == 0, other, mine)], axis=0)

        part = global_queries_part(qkv_g, qkv, kmax)

        quarter = n_glob // 4
        got = lax.ppermute(lax.dynamic_slice_in_dim(part, (1 - core) * half, half, axis=1), 'sp', core_swap)
        joined = jnp.stack(combine(lax.dynamic_slice_in_dim(part, core * half, half, axis=1), got))
        got = lax.ppermute(lax.dynamic_slice_in_dim(joined, (1 - chip) * quarter, quarter, axis=1), 'sp', chip_swap)
        g_acc, _, g_l = combine(lax.dynamic_slice_in_dim(joined, chip * quarter, quarter, axis=1), got)
        mine = (g_acc / g_l).astype(BF16)
        other = lax.ppermute(mine, 'sp', chip_swap)
        mine = jnp.concatenate([jnp.where(chip == 0, mine, other), jnp.where(chip == 0, other, mine)], axis=0)
        other = lax.ppermute(mine, 'sp', core_swap)
        glob_out = jnp.concatenate([jnp.where(core == 0, mine, other), jnp.where(core == 0, other, mine)], axis=0)

        glob_out, w_all = lax.optimization_barrier((glob_out, w_all))
        y, first = None, 0
        for n_blk in CHUNKS if n_rows == 16 * QB else (n_rows // QB // 2,) * 2:
            o = global_keys_part(qkv, qkv_g, kmax, win, local_idx, glob_out, first, n_blk)
            o_all = lax.all_gather(o, 'tp')
            y = mlp_rows(tokens, o_all, w_all, y, first, d_o, d_f)
            first += n_blk
        return y

    row_spec = P(('dp', 'sp'), None)
    head_spec = P(None, 'tp', None)
    in_specs = (row_spec, P('dp'), head_spec, head_spec, head_spec, P('tp', None, None), P(None, 'tp'), P('tp', None))
    return jax.shard_map(device_layer, mesh=mesh, in_specs=in_specs, out_specs=row_spec, check_vma=False)
```

time: 1830 us -> 613 us (0.33)
  waiting for transfers between devices: 1160 us -> 29 us
  Pallas kernels: 0 us -> 532 us
  matrix products: 285 us -> 0 us
  local copies, waits for them, and re-layouts: 180 us -> 8.3 us
  other arithmetic: 98.8 us -> 13.3 us
  blocking collectives: 46.7 us -> 0 us
  loops' own time: 24.8 us -> 0 us
    psum x3 -> x0, waiting for transfers between devices: 1160 us -> none  [the longest x1 561 us: device_layer(): lax.psum(jnp.einsum('rhe,hed->rd', attn_rows, w_out, preferred_element_ty...]
    pallas_call x0 -> x11, Pallas kernels: none -> 532 us  [the longest x4 151 us: global_keys_part(): pl.pallas_call(functools.partial(global_keys_kernel, first=first), grid=(...]
    dot_general x132 -> x0, matrix products: 271 us -> none  [the longest x32 66.7 us: one_block(): jnp.einsum('hqk,khe->qhe', p_win, v_blk, preferred_element_type=jnp.float32)]
    scatter x1 -> x0, local copies, waits for them, and re-layouts: 94.2 us -> none  [device_layer(): attn_rows.at[jnp.where(owned, local_idx, n_rows)].set(glob_out, mode='drop')]
    reduce_sum x65 -> x0, other arithmetic: 49.8 us -> none  [the longest x1 21.2 us: global_queries(): glob_sum = lax.psum(jnp.sum(exp_scores, axis=2, keepdims=True), 'sp')]
    psum x2 -> x0, blocking collectives: 36.6 us -> none  [the longest x1 26.5 us: global_queries(): return lax.psum(part_out, 'sp').astype(jnp.bfloat16)]
    gather x6 -> x0, local copies, waits for them, and re-layouts: 35.9 us -> none  [pick_rows(): picked = jnp.take(row_array, safe_idx, axis=0)]
    ppermute x4 -> x9, waiting for transfers between devices: 0.01 us -> 28.1 us  [the longest x1 18 us: device_layer(): lax.ppermute(lax.dynamic_slice_in_dim(joined, (1 - chip) * quarter, quart...]
  transfers between devices with their start and end apart: 7 -> 14, of which waited for: 3 -> 6; matrix products, arithmetic and copies ran while one was open for 4% -> 3% of each run, Pallas kernels for 0% -> 77%
where the time goes in v2:
time: 613 us; the launch traced here: 608 us
  Pallas kernels  532 us (87%)
  waiting for transfers between devices  29 us (5%)
  between operations  14 us (2%)
  other arithmetic  13.3 us (2%)
  starting transfers between devices  11.8 us (2%)
  local copies, waits for them, and re-layouts  8.3 us (1%)
    pallas_call x4, Pallas kernels, global_keys_part(): pl.pallas_call(functools.partial(global_keys_kernel, first=first), grid=(...  151 us
    pallas_call x1, Pallas kernels, global_queries_part(): pl.pallas_call(functools.partial(global_queries_kernel, kb=kb), grid=(2,...  137 us
    pallas_call x1, Pallas kernels, window_part(): pl.pallas_call(window_kernel, grid=(2, n_blk), in_specs=[mid(0), left(1),...  135 us
    pallas_call x4, Pallas kernels, mlp_rows(): pl.pallas_call(functools.partial(mlp_kernel, n_tp=n_tp, n_rep=n_rep, d_o=...  93.7 us
    ppermute x1, waiting for transfers between devices, device_layer(): lax.ppermute(lax.dynamic_slice_in_dim(joined, (1 - chip) * quarter, quart...  18 us
    pallas_call x1, Pallas kernels, qkv_part(): pl.pallas_call(qkv_kernel, grid_spec=pltpu.PrefetchScalarGridSpec(num_sca...  15.5 us
  transfers between devices with their start and end apart: 14, of which 6 were waited for; matrix products, arithmetic and copies ran while one was open for 3% of the time, Pallas kernels for 77%

profile of v2, /device:TPU:0, one launch (start us, length us, event | category | flops | bytes accessed | tf_op | source)
XLA Modules:
  0.0 608.3 jit_solution(17278210523913216304)
XLA Ops:
  6.5 1.9 fusion.3
  8.5 0.2 copy.22.idx_ref
  8.8 0.2 copy.19
  9.0 0.4 copy-done.4
  9.4 0.2 copy.20
  9.7 0.2 copy.21
  9.9 0.1 pad_maximum_fusion.w_ref
  10.0 15.5 %qkv.1 = (bf16[4096,768]{1,0:T(8,128)(2,1)}, bf16[1024,768]{1,0:T(8,128)(2,1)S(1)}, f32[1,256]{1,0:T(1,128)S(1)}) custom-call(s32[1024]{0:T(1024)S(1)} %broadcast_subtract_fusion.pos_ref, s32[1024,1]{1,0:T(8,128)S(1)} %copy.22.idx_ref, bf16[4096,1024]{1,0:T(8,128)(2,1)} %x_ref.9, bf16[1024,768]{1,0:T(8,128)(2,1)S(1)} %pad_maximum_fusion.w_ref), custom_call_target="tpu_custom_call" | custom-call | flops 8000000000 | bytes 24000000 | tf_op jit(solution)/shard_map/qkv/pallas_call | solution.py:80
  25.5 1.9 fusion.14
  27.4 1.3 collective-permute-start.3
  28.7 3.4 collective-permute-start.2
  32.1 0.9 constant_dynamic-slice_fusion.2
  33.0 2.6 collective-permute-start
  35.6 2.5 compare_reduce_fusion
  38.2 2.6 select_convert_fusion.extra_ref
  40.9 1.3 dynamic-slice_add_fusion
  42.2 0.5 collective-permute-start.1
  42.7 135.3 %window_part.1 = (f32[4096,256]{1,0:T(8,128)S(1)}, f32[4096,256]{1,0:T(8,128)}, f32[4096,256]{1,0:T(8,128)}) custom-call(bf16[4096,768]{1,0:T(8,128)(2,1)} %get-tuple-element.17.q_ref.kl_ref.kc_ref.kr_ref.vl_ref.vc_ref.vr_ref.k_ref.v_ref, bf16[4096,768]{1,0:T(8,128)(2,1)} %get-tuple-element.17.q_ref.kl_ref.kc_ref.kr_ref.vl_ref.vc_ref.vr_ref.k_ref.v_ref, ...), custom_call_target="tpu_custom_call" | custom-call | flops 30000001024 | bytes 30000000 | tf_op jit(solution)/shard_map/window_part/pallas_call | solution.py:239
  178.0 2.0 copy-done.2
  180.0 0.2 add.91
  180.2 0.3 collective-permute-start.4
  180.5 2.1 collective-permute-done.4
  182.6 0.1 broadcast_select_fusion.1
  182.7 0.1 pad_maximum_fusion.1.q_ref.kg_ref.vg_ref
  182.8 136.6 %global_queries.1 = f32[3,1024,256]{2,1,0:T(8,128)S(1)} custom-call(bf16[1024,768]{1,0:T(8,128)(2,1)S(1)} %pad_maximum_fusion.1.q_ref.kg_ref.vg_ref, bf16[4096,768]{1,0:T(8,128)(2,1)} %get-tuple-element.17.q_ref.kl_ref.kc_ref.kr_ref.vl_ref.vc_ref.vr_ref.k_ref.v_ref, ...), custom_call_target="tpu_custom_call" | custom-call | flops 33999998976 | bytes 20000000 | tf_op jit(solution)/shard_map/global_queries/pallas_call | solution.py:357
  319.4 1.2 constant_dynamic-slice_fusion.1
  320.7 0.2 collective-permute-start.5
  320.9 3.1 collective-permute-done.5
  324.0 1.4 fusion.1
  325.4 1.4 fusion
  326.8 0.1 pad_maximum_fusion.2
  326.9 0.9 constant_dynamic-slice_fusion
  327.9 1.6 collective-permute-start.6
  329.5 18.0 %collective-permute-done.6 = f32[3,256,256]{2,1,0:T(8,128)} collective-permute-done((f32[3,256,256]{2,1,0:T(8,128)}, f32[3,256,256]{2,1,0:T(8,128)}, u32[]{:S(2)}, u32[]{:S(2)}) %collective-permute-start.6) | collective-permute-done | bytes 786464 | tf_op jit(solution)/shard_map/ppermute | solution.py:484
  347.5 1.2 fusion.13
  348.8 1.7 collective-permute-start.7
  350.4 3.4 collective-permute-done.7
  354.0 1.5 collective-permute-done.8
  355.5 0.1 broadcast_select_fusion.3
  355.7 38.0 %global_keys.7 = bf16[1024,256]{1,0:T(8,128)(2,1)} custom-call(bf16[4096,768]{1,0:T(8,128)(2,1)} %get-tuple-element.17.q_ref.kl_ref.kc_ref.kr_ref.vl_ref.vc_ref.vr_ref.k_ref.v_ref, bf16[1024,768]{1,0:T(8,128)(2,1)S(1)} %copy-done.1, bf16[1024,768]{1,0:T(8,128)(2,1)S(1)} %copy-done.1, f32[1,256]{1,0:T(1,128)S(1)} %get-tuple-element.19.kmax_ref, ...), custom_call_target="tpu_custom_call" | custom-call | flops 10000000000 | bytes 8000000 | tf_op jit(solution)/shard_map/global_keys/pallas_call | solution.py:301
  393.7 37.6 %global_keys.6 = bf16[1024,256]{1,0:T(8,128)(2,1)} custom-call(bf16[4096,768]{1,0:T(8,128)(2,1)} %get-tuple-element.17.q_ref.kl_ref.kc_ref.kr_ref.vl_ref.vc_ref.vr_ref.k_ref.v_ref, bf16[1024,768]{1,0:T(8,128)(2,1)S(1)} %copy-done.1, bf16[1024,768]{1,0:T(8,128)(2,1)S(1)} %copy-done.1, f32[1,256]{1,0:T(1,128)S(1)} %get-tuple-element.19.kmax_ref, ...), custom_call_target="tpu_custom_call" | custom-call | flops 10000000000 | bytes 8000000 | tf_op jit(solution)/shard_map/global_keys/pallas_call | solution.py:301
  431.3 37.6 %global_keys.5 = bf16[1024,256]{1,0:T(8,128)(2,1)} custom-call(bf16[4096,768]{1,0:T(8,128)(2,1)} %get-tuple-element.17.q_ref.kl_ref.kc_ref.kr_ref.vl_ref.vc_ref.vr_ref.k_ref.v_ref, bf16[1024,768]{1,0:T(8,128)(2,1)S(1)} %copy-done.1, bf16[1024,768]{1,0:T(8,128)(2,1)S(1)} %copy-done.1, f32[1,256]{1,0:T(1,128)S(1)} %get-tuple-element.19.kmax_ref, ...), custom_call_target="tpu_custom_call" | custom-call | flops 10000000000 | bytes 8000000 | tf_op jit(solution)/shard_map/global_keys/pallas_call | solution.py:301
  469.0 37.8 %global_keys.4 = bf16[1024,256]{1,0:T(8,128)(2,1)} custom-call(bf16[4096,768]{1,0:T(8,128)(2,1)} %get-tuple-element.17.q_ref.kl_ref.kc_ref.kr_ref.vl_ref.vc_ref.vr_ref.k_ref.v_ref, bf16[1024,768]{1,0:T(8,128)(2,1)S(1)} %copy-done.1, bf16[1024,768]{1,0:T(8,128)(2,1)S(1)} %copy-done.1, f32[1,256]{1,0:T(1,128)S(1)} %get-tuple-element.19.kmax_ref, ...), custom_call_target="tpu_custom_call" | custom-call | flops 10000000000 | bytes 8000000 | tf_op jit(solution)/shard_map/global_keys/pallas_call | solution.py:301
  506.8 23.2 %mlp.4.refs_0_ = bf16[4096,1024]{1,0:T(8,128)(2,1)} custom-call(bf16[4096,1024]{1,0:T(8,128)(2,1)} %x_ref.9, bf16[4,1024,256]{2,1,0:T(8,128)(2,1)} %bitcast.74, bf16[8,4,1568,128]{3,2,1,0:T(8,128)(2,1)} %bitcast.70), custom_call_target="tpu_custom_call" | custom-call | flops 13153337344 | bytes 20000000 | tf_op jit(solution)/shard_map/mlp/pallas_call | solution.py:411
  530.1 23.5 %mlp.5.refs_0_ = bf16[4096,1024]{1,0:T(8,128)(2,1)} custom-call(bf16[4096,1024]{1,0:T(8,128)(2,1)} %x_ref.9, bf16[4,1024,256]{2,1,0:T(8,128)(2,1)} %bitcast.75, bf16[8,4,1568,128]{3,2,1,0:T(8,128)(2,1)} %bitcast.71, bf16[4096,1024]{1,0:T(8,128)(2,1)} %mlp.4.refs_0_), custom_call_target="tpu_custom_call", output_to_operand_aliasing={{}: (3, {})} | custom-call | flops 13153337344 | bytes 20000000 | tf_op jit(solution)/shard_map/mlp/pallas_call | solution.py:411
  553.6 23.5 %mlp.6.refs_0_ = bf16[4096,1024]{1,0:T(8,128)(2,1)} custom-call(bf16[4096,1024]{1,0:T(8,128)(2,1)} %x_ref.9, bf16[4,1024,256]{2,1,0:T(8,128)(2,1)} %bitcast.76, bf16[8,4,1568,128]{3,2,1,0:T(8,128)(2,1)} %bitcast.72, bf16[4096,1024]{1,0:T(8,128)(2,1)} %mlp.5.refs_0_), custom_call_target="tpu_custom_call", output_to_operand_aliasing={{}: (3, {})} | custom-call | flops 13153337344 | bytes 20000000 | tf_op jit(solution)/shard_map/mlp/pallas_call | solution.py:411
  577.1 0.7 all-gather.13.cloned.1.call-done
  577.8 23.5 %mlp.7 = bf16[4096,1024]{1,0:T(8,128)(2,1)} custom-call(bf16[4096,1024]{1,0:T(8,128)(2,1)} %x_ref.9, bf16[4,1024,256]{2,1,0:T(8,128)(2,1)} %bitcast.77, bf16[8,4,1568,128]{3,2,1,0:T(8,128)(2,1)} %bitcast.73, bf16[4096,1024]{1,0:T(8,128)(2,1)} %mlp.6.refs_0_), custom_call_target="tpu_custom_call", output_to_operand_aliasing={{}: (3, {})} | custom-call | flops 13153337344 | bytes 20000000 | tf_op jit(solution)/shard_map/mlp/pallas_call | solution.py:411
  (40 shorter events, 0.7 us)
Async XLA Ops:
  6.5 1.9 copy-start.6
  6.5 349.1 %all-gather.11.cloned.1.call-start = ((), (), s32[]{:S(2)}) async-start(), calls=%async_computation | async-start | bytes 13246464 | tf_op jit(solution)/shard_map/all_gather | solution.py:453
  6.5 2.2 copy-start.3
  8.4 1.0 copy-start.4
  8.4 1.2 copy-start.5
  8.4 498.4 %all-gather.19.cloned.1.call-start = ((), (), s32[]{:S(2)}) async-start(), calls=%async_computation.4 | async-start | bytes 2621440 | tf_op jit(solution)/shard_map/all_gather | solution.py:496
  27.4 15.3 %collective-permute-start.3 = (bf16[256,512]{1,0:T(8,128)(2,1)}, bf16[256,512]{1,0:T(8,128)(2,1)S(1)}, u32[]{:S(2)}, u32[]{:S(2)}) collective-permute-start(bf16[256,512]{1,0:T(8,128)(2,1)} %get-tuple-element.31), channel_id=1, source_target_pairs={{1,0},{2,1},{3,2},{5,4},{6,5},{7,6},{9,8},{10,9},{11,10},{13,12},{... | collective-permute-start | bytes 786440 | tf_op jit(solution)/shard_map/ppermute | solution.py:460
  28.7 14.0 %collective-permute-start.2 = (bf16[256,512]{1,0:T(8,128)(2,1)}, bf16[256,512]{1,0:T(8,128)(2,1)S(1)}, u32[]{:S(2)}, u32[]{:S(2)}) collective-permute-start(bf16[256,512]{1,0:T(8,128)(2,1)} %get-tuple-element.32), channel_id=1, source_target_pairs={{0,1},{1,2},{2,3},{4,5},{5,6},{6,7},{8,9},{9,10},{10,11},{12,13},{... | collective-permute-start | bytes 786440 | tf_op jit(solution)/shard_map/ppermute | solution.py:459
  33.0 7.8 %collective-permute-start = (bf16[512,768]{1,0:T(8,128)(2,1)}, bf16[512,768]{1,0:T(8,128)(2,1)}, u32[]{:S(2)}, u32[]{:S(2)}) collective-permute-start(bf16[512,768]{1,0:T(8,128)(2,1)} %constant_dynamic-slice_fusion.2), channel_id=1, source_target_pairs={{0,1},{1,0},{2,3},{3,2},{4,5},{5,4},{6,7},{7,6},{8,9},{9,8},{10,11... | collective-permute-start | bytes 2359304 | tf_op jit(solution)/shard_map/ppermute | solution.py:470
  42.2 137.8 %collective-permute-start.1 = (bf16[512,768]{1,0:T(8,128)(2,1)S(1)}, bf16[512,768]{1,0:T(8,128)(2,1)S(1)}, u32[]{:S(2)}, u32[]{:S(2)}) collective-permute-start(bf16[512,768]{1,0:T(8,128)(2,1)S(1)} %dynamic-slice_add_fusion), channel_id=1, source_target_pairs={{0,2},{1,3},{2,0},{3,1},{4,6},{5,7},{6,4},{7,5},{8,10},{9,11},{10,... | collective-permute-start | bytes 2359304 | tf_op jit(solution)/shard_map/ppermute | solution.py:472
  178.0 2.0 copy-start.2
  180.2 2.4 collective-permute-start.4
  182.8 136.6 %copy-start = (bf16[1024,768]{1,0:T(8,128)(2,1)}, bf16[1024,768]{1,0:T(8,128)(2,1)S(1)}, u32[]{:S(2)}) copy-start(bf16[1024,768]{1,0:T(8,128)(2,1)S(1)} %pad_maximum_fusion.1.q_ref.kg_ref.vg_ref) | copy-start | bytes 4718596
  320.7 3.4 collective-permute-start.5
  327.9 19.7 %collective-permute-start.6 = (f32[3,256,256]{2,1,0:T(8,128)}, f32[3,256,256]{2,1,0:T(8,128)}, u32[]{:S(2)}, u32[]{:S(2)}) collective-permute-start(f32[3,256,256]{2,1,0:T(8,128)} %constant_dynamic-slice_fusion), channel_id=1, source_target_pairs={{0,2},{1,3},{2,0},{3,1},{4,6},{5,7},{6,4},{7,5},{8,10},{9,11},{10,... | collective-permute-start | bytes 2359304 | tf_op jit(solution)/shard_map/ppermute | solution.py:484
  329.5 26.2 %copy-start.1 = (bf16[1024,768]{1,0:T(8,128)(2,1)S(1)}, bf16[1024,768]{1,0:T(8,128)(2,1)}, u32[]{:S(2)}) copy-start(bf16[1024,768]{1,0:T(8,128)(2,1)} %copy-done) | copy-start | bytes 4718596
  348.8 5.0 collective-permute-start.7
  353.9 1.6 collective-permute-start.8
  393.6 136.4 %all-gather.17.cloned.1.call-start = ((), (), s32[]{:S(2)}) async-start(), calls=%async_computation.3 | async-start | bytes 2621440 | tf_op jit(solution)/shard_map/all_gather | solution.py:496
  431.3 122.3 %all-gather.15.cloned.1.call-start = ((), (), s32[]{:S(2)}) async-start(), calls=%async_computation.2 | async-start | bytes 2621440 | tf_op jit(solution)/shard_map/all_gather | solution.py:496
  469.0 108.8 %all-gather.13.cloned.1.call-start = ((), (), s32[]{:S(2)}) async-start(), calls=%async_computation.1 | async-start | bytes 2621440 | tf_op jit(solution)/shard_map/all_gather | solution.py:496
Sparse Core Ops, SparseCore 0:
  10.2 99.7 all-gather.10
  393.8 46.6 all-gather.18
  442.0 44.2 all-gather.16
  487.7 44.2 all-gather.14
  533.4 44.3 all-gather.12

commit v3 on v2

--- a/solution.py
+++ b/solution.py
@@ -10,7 +10,6 @@
 
 WIN = 256
 QB = 256
-CHUNKS = (4, 4, 4, 4)
 FLOOR = -3.0e38
 F32 = jnp.float32
 BF16 = jnp.bfloat16
@@ -248,8 +247,8 @@
     )(qkv, qkv, qkv, qkv, qkv, qkv, qkv, halo_l, halo_r, halo_l, halo_r, extra, bias, kmax)
 
 
-def global_keys_kernel(q_ref, kg_ref, vg_ref, kmax_ref, acc_ref, m_ref, l_ref, idx_ref, glob_ref, out_ref,
-                       k_ref, o_ref, ea_ref, em_ref, el_ref, *, first):
+def global_keys_kernel(q_ref, kg_ref, vg_ref, kmax_ref, acc_ref, m_ref, l_ref, out_ref,
+                       k_ref, ea_ref, em_ref, el_ref):
     n = q_ref.shape[0]
     i = pl.program_id(1)
 
@@ -262,7 +261,7 @@
     def finish(acc, m, total):
         m_all = jnp.maximum(m, m_ref[...])
         a, b = jnp.exp(m - m_all), jnp.exp(m_ref[...] - m_all)
-        o_ref[...] = (acc * a + acc_ref[...] * b) / (total * a + l_ref[...] * b)
+        out_ref[...] = ((acc * a + acc_ref[...] * b) / (total * a + l_ref[...] * b)).astype(out_ref.dtype)
 
     q = q_ref[...]
     neg = shifts(q, kmax_ref[...])
@@ -282,33 +281,42 @@
             exact_head(q_ref[...], half, vg_ref.shape[0], key_rows, ea_ref, em_ref, el_ref)
         finish(*(jnp.where(low, r[0], r[1]) for r in (ea_ref, em_ref, el_ref)))
 
-    row = first * QB + i * n + lax.broadcasted_iota(jnp.int32, (n, 1), 0)
+
+def global_keys_part(qkv, qkv_g, kmax, win):
+    n_rows, n_glob = qkv.shape[0], qkv_g.shape[0]
+    rb = 512
+    row = pl.BlockSpec((rb, 128), lambda p, i: (i, p))
+    pair = pltpu.VMEM((2, rb, 128), F32)
+    return pl.pallas_call(
+        global_keys_kernel, grid=(2, n_rows // rb),
+        in_specs=[row, pl.BlockSpec((n_glob, 128), lambda p, i: (0, 2 + p)), pl.BlockSpec((n_glob, 128), lambda p, i: (0, 4 + p)),
+                  pl.BlockSpec((1, 128), lambda p, i: (0, p)), row, row, row],
+        out_specs=row, out_shape=jax.ShapeDtypeStruct((n_rows, 256), BF16),
+        scratch_shapes=[pltpu.VMEM((2, n_glob, 128), BF16), pair, pair, pair],
+        compiler_params=params(2), cost_estimate=cost(40e9, 32e6, 16e6), name="global_keys",
+    )(qkv, qkv_g, qkv_g, kmax, *win)
+
+
+def place_kernel(idx_ref, glob_ref, o_ref, out_ref):
+    n = o_ref.shape[0]
+    row = pl.program_id(0) * n + lax.broadcasted_iota(jnp.int32, (n, 1), 0)
     hit = jnp.where(idx_ref[...] == row, 1.0, 0.0)
     placed = dot_nn(hit.astype(BF16), glob_ref[...])
-    mine = row_sum(hit) > 0.5
-    out_ref[...] = jnp.where(mine, placed, o_ref[...]).astype(out_ref.dtype)
-
-
-def global_keys_part(qkv, qkv_g, kmax, win, local_idx, glob_out, first, n_blk):
-    n_glob = qkv_g.shape[0]
-    rb = min(512, n_blk * QB)
-    base = first * QB // rb
-    n_rows = n_blk * QB
-    row = pl.BlockSpec((rb, 128), lambda p, i: (base + i, p))
-    whole = lambda a: pl.BlockSpec(a.shape, lambda p, i: (0,) * a.ndim)
-    idx = local_idx[None, :]
-    pair = pltpu.VMEM((2, rb, 128), F32)
+    out_ref[...] = jnp.where(row_sum(hit) > 0.5, placed, o_ref[...].astype(F32)).astype(out_ref.dtype)
+
+
+def place_rows(o, glob_out, local_idx):
+    n_rows, width = o.shape
+    n_glob = local_idx.shape[0]
+    rb = 512
     return pl.pallas_call(
-        functools.partial(global_keys_kernel, first=first), grid=(2, n_rows // rb),
-        in_specs=[row, pl.BlockSpec((n_glob, 128), lambda p, i: (0, 2 + p)), pl.BlockSpec((n_glob, 128), lambda p, i: (0, 4 + p)),
-                  pl.BlockSpec((1, 128), lambda p, i: (0, p)), row, row, row, whole(idx),
-                  pl.BlockSpec((n_glob, 128), lambda p, i: (0, p))],
-        out_specs=pl.BlockSpec((rb, 128), lambda p, i: (i, p)),
-        out_shape=jax.ShapeDtypeStruct((n_rows, 256), BF16),
-        scratch_shapes=[pltpu.VMEM((2, n_glob, 128), BF16), pltpu.VMEM((rb, 128), F32), pair, pair, pair],
-        compiler_params=params(2), cost_estimate=cost(2.5e9 * n_blk, 2e6 * n_blk, 1e6 * n_blk),
-        name="global_keys",
-    )(qkv, qkv_g, qkv_g, kmax, *win, idx, glob_out)
+        place_kernel, grid=(n_rows // rb,),
+        in_specs=[pl.BlockSpec((1, n_glob), lambda i: (0, 0)), pl.BlockSpec((n_glob, width), lambda i: (0, 0)),
+                  pl.BlockSpec((rb, width), lambda i: (i, 0))],
+        out_specs=pl.BlockSpec((rb, width), lambda i: (i, 0)),
+        out_shape=jax.ShapeDtypeStruct((n_rows, width), BF16),
+        compiler_params=params(1), cost_estimate=cost(2e9, 5e6), name="place",
+    )(local_idx[None, :], glob_out, o)
 
 
 def global_queries_kernel(q_ref, k_ref, v_ref, kmax_ref, out_ref, acc_ref, m_ref, l_ref, *, kb):
@@ -365,61 +373,162 @@
     )(qkv_g, qkv, qkv, kmax)
 
 
-def mlp_kernel(x_ref, o_ref, w_ref, *refs, n_tp, n_rep, d_o, d_f):
-    y_ref, wo_ref, w2_ref, w1_ref, sem = refs[-5:]
-
-    @pl.when(pl.program_id(0) == 0)
-    def _():
-        copies = []
-        piece = wo_ref.shape[1] // n_rep
-        for j in range(n_rep):
-            for t in range(n_tp):
-                lanes = pl.ds(j * piece, piece)
-                copies.append(pltpu.make_async_copy(
-                    w_ref.at[j, t, pl.ds(0, d_o)], wo_ref.at[pl.ds(t * d_o, d_o), lanes], sem))
-                copies.append(pltpu.make_async_copy(
-                    w_ref.at[j, t, pl.ds(d_o, d_f)], w2_ref.at[pl.ds(t * d_f, d_f), lanes], sem))
-                copies.append(pltpu.make_async_copy(
-                    w_ref.at[j, t, pl.ds(d_o + d_f, d_f)], w1_ref.at[pl.ds(t * d_f, d_f), lanes], sem))
-        for c in copies:
-            c.start()
-        for c in copies:
-            c.wait()
-
-    mixed = dot_nn(o_ref[0], wo_ref[:d_o, :])
-    for t in range(1, n_tp):
-        mixed += dot_nn(o_ref[t], wo_ref[t * d_o:(t + 1) * d_o, :])
-    h = (x_ref[...].astype(F32) + mixed).astype(BF16)
+def exchange_mlp_kernel(x_hbm, o_hbm, w_hbm, y_hbm, x_ref, o_ref, wo_ref, w2_ref, w1_ref, load_sem, y_sem,
+                        up_send, up_recv, down_send, down_recv, *, n_tp, n_rep, d_o, d_f, rb):
+    me = lax.axis_index('tp')
+    n_blk = x_ref.shape[0] // rb
     width = n_tp * d_f
-    acc = h.astype(F32)
-    for f0 in range(0, width, 512):
-        f1 = min(f0 + 512, width)
-        z = dot_nt(h, w1_ref[f0:f1, :])
-        u = 0.5 * z * (1.0 + jnp.tanh(math.sqrt(2.0 / math.pi) * (z + 0.044715 * (z * z * z))))
-        acc += dot_nn(u.astype(BF16), w2_ref[f0:f1, :])
-    y_ref[...] = acc.astype(y_ref.dtype)
-
-
-def mlp_rows(tokens, o_all, w_all, y, first, d_o, d_f):
-    n_tp, n_rows, _ = o_all.shape
+
+    barrier = pltpu.get_barrier_semaphore()
+
+    @pl.when(me > 0)
+    def _():
+        pl.semaphore_signal(barrier, inc=1, device_id={'tp': me - 1}, device_id_type=pl.DeviceIdType.MESH)
+
+    @pl.when(me < n_tp - 1)
+    def _():
+        pl.semaphore_signal(barrier, inc=1, device_id={'tp': me + 1}, device_id_type=pl.DeviceIdType.MESH)
+
+    own = pltpu.make_async_copy(o_hbm, o_ref.at[me], load_sem.at[0])
+    own.start()
+    copies = [pltpu.make_async_copy(x_hbm, x_ref, load_sem.at[1])]
+    piece = wo_ref.shape[1] // n_rep
+    for j in range(n_rep):
+        for t in range(n_tp):
+            lanes = pl.ds(j * piece, piece)
+            for src, n, dst in ((0, d_o, wo_ref), (d_o, d_f, w2_ref), (d_o + d_f, d_f, w1_ref)):
+                copies.append(pltpu.make_async_copy(w_hbm.at[j, t, pl.ds(src, n)], dst.at[pl.ds(t * n, n), lanes],
+                                                    load_sem.at[2 + len(copies)]))
+    for c in copies:
+        c.start()
+
+    ends = jnp.logical_or(me == 0, me == n_tp - 1)
+
+    @pl.when(ends)
+    def _():
+        pl.semaphore_wait(barrier, 1)
+
+    @pl.when(jnp.logical_not(ends))
+    def _():
+        pl.semaphore_wait(barrier, 2)
+
+    own.wait()
+
+    def rows_of(b):
+        return pl.ds(pl.multiple_of(b * rb, rb), rb)
+
+    def up(d, b):
+        at = o_ref.at[me - d, rows_of(b)]
+        return pltpu.make_async_remote_copy(at, at, up_send.at[d, b], up_recv.at[d, b], device_id={'tp': me + 1},
+                                            device_id_type=pl.DeviceIdType.MESH)
+
+    def down(d, b):
+        at = o_ref.at[me + d, rows_of(b)]
+        return pltpu.make_async_remote_copy(at, at, down_send.at[d, b], down_recv.at[d, b], device_id={'tp': me - 1},
+                                            device_id_type=pl.DeviceIdType.MESH)
+
+    def landed(recv, d, shard, b):
+        at = o_ref.at[shard, rows_of(b)]
+        pltpu.make_async_remote_copy(at, at, up_send.at[0, b], recv.at[d - 1, b], device_id={'tp': me},
+                                     device_id_type=pl.DeviceIdType.MESH).wait_recv()
+
+    def send_own(b):
+        @pl.when(me < n_tp - 1)
+        def _():
+            up(0, b).start()
+
+        @pl.when(me > 0)
+        def _():
+            down(0, b).start()
+
+    ahead = min(2, n_blk)
+    for b in range(ahead):
+        send_own(b)
+
+    def step(s, carry):
+        @pl.when(s + ahead < n_blk)
+        def _():
+            send_own(s + ahead)
+
+        for d in range(1, n_tp):
+            b = s - (d - 1)
+
+            @pl.when((b >= 0) & (b < n_blk) & (me >= d))
+            def _():
+                landed(up_recv, d, me - d, b)
+                if d < n_tp - 1:
+                    @pl.when(me < n_tp - 1)
+                    def _():
+                        up(d, b).start()
+
+            @pl.when((b >= 0) & (b < n_blk) & (me + d <= n_tp - 1))
+            def _():
+                landed(down_recv, d, me + d, b)
+                if d < n_tp - 1:
+                    @pl.when(me > 0)
+                    def _():
+                        down(d, b).start()
+
+        @pl.when(s == n_tp - 2)
+        def _():
+            for c in copies:
+                c.wait()
+
+        @pl.when(s >= n_tp - 2)
+        def _():
+            b = s - (n_tp - 2)
+            rows = rows_of(b)
+            mixed = dot_nn(o_ref[0, rows], wo_ref[:d_o, :])
+            for t in range(1, n_tp):
+                mixed += dot_nn(o_ref[t, rows], wo_ref[t * d_o:(t + 1) * d_o, :])
+            h = (x_ref[rows].astype(F32) + mixed).astype(BF16)
+            acc = h.astype(F32)
+            for f0 in range(0, width, 512):
+                f1 = min(f0 + 512, width)
+                z = dot_nt(h, w1_ref[f0:f1, :])
+                u = 0.5 * z * (1.0 + jnp.tanh(math.sqrt(2.0 / math.pi) * (z + 0.044715 * (z * z * z))))
+                acc += dot_nn(u.astype(BF16), w2_ref[f0:f1, :])
+            x_ref[rows] = acc.astype(BF16)
+            pltpu.make_async_copy(x_ref.at[rows], y_hbm.at[rows], y_sem.at[b]).start()
+
+        return carry
+
+    lax.fori_loop(0, n_blk + n_tp - 2, step, 0)
+
+    def finish(b, carry):
+        rows = rows_of(b)
+        pltpu.make_async_copy(x_ref.at[rows], y_hbm.at[rows], y_sem.at[b]).wait()
+        for d in range(n_tp - 1):
+            @pl.when((me < n_tp - 1) & (me >= d))
+            def _():
+                up(d, b).wait_send()
+
+            @pl.when((me > 0) & (me + d <= n_tp - 1))
+            def _():
+                down(d, b).wait_send()
+
+        return carry
+
+    lax.fori_loop(0, n_blk, finish, 0)
+
+
+def exchange_mlp(tokens, o, w_all, n_tp, d_o, d_f):
+    n_rows, dim = tokens.shape
     n_rep = w_all.shape[0]
-    dim = tokens.shape[1]
-    rb = min(512, n_rows)
+    rb = min(512, n_rows // 2)
     n_blk = n_rows // rb
-    base = first * QB // rb
-    earlier = () if y is None else (y,)
+    anywhere = pl.BlockSpec(memory_space=pl.ANY)
+    dma = pltpu.SemaphoreType.DMA
     return pl.pallas_call(
-        functools.partial(mlp_kernel, n_tp=n_tp, n_rep=n_rep, d_o=d_o, d_f=d_f), grid=(n_blk,),
-        in_specs=[pl.BlockSpec((rb, dim), lambda i: (base + i, 0)),
-                  pl.BlockSpec((n_tp, rb, d_o), lambda i: (0, i, 0)),
-                  pl.BlockSpec(memory_space=pl.ANY)] + [pl.BlockSpec(memory_space=pl.ANY)] * len(earlier),
-        out_specs=pl.BlockSpec((rb, dim), lambda i: (base + i, 0)),
-        out_shape=jax.ShapeDtypeStruct(tokens.shape, BF16),
-        input_output_aliases={3: 0} if earlier else {},
-        scratch_shapes=[pltpu.VMEM((n_tp * d_o, dim), BF16), pltpu.VMEM((n_tp * d_f, dim), BF16),
-                        pltpu.VMEM((n_tp * d_f, dim), BF16), pltpu.SemaphoreType.DMA],
-        compiler_params=params(1, 56), cost_estimate=cost(2 * n_rows * dim * (dim + 2 * n_tp * d_f), 20e6), name="mlp",
-    )(tokens, o_all, w_all, *earlier)
+        functools.partial(exchange_mlp_kernel, n_tp=n_tp, n_rep=n_rep, d_o=d_o, d_f=d_f, rb=rb),
+        in_specs=[anywhere] * 3, out_specs=anywhere, out_shape=jax.ShapeDtypeStruct(tokens.shape, BF16),
+        scratch_shapes=[pltpu.VMEM((n_rows, dim), BF16), pltpu.VMEM((n_tp, n_rows, d_o), BF16),
+                        pltpu.VMEM((n_tp * d_o, dim), BF16), pltpu.VMEM((n_tp * d_f, dim), BF16),
+                        pltpu.VMEM((n_tp * d_f, dim), BF16), dma((2 + 3 * n_rep * n_tp + 1,)), dma((n_blk,)),
+                        dma((n_tp - 1, n_blk)), dma((n_tp - 1, n_blk)), dma((n_tp - 1, n_blk)), dma((n_tp - 1, n_blk))],
+        compiler_params=pltpu.CompilerParams(collective_id=1, has_side_effects=True, vmem_limit_bytes=56 << 20),
+        cost_estimate=cost(2 * n_rows * dim * (dim + 2 * n_tp * d_f), 40e6), name="exchange_mlp",
+    )(tokens, o, w_all)
 
 
 def combine(a, b):
@@ -482,6 +591,8 @@
         got = lax.ppermute(lax.dynamic_slice_in_dim(part, (1 - core) * half, half, axis=1), 'sp', core_swap)
         joined = jnp.stack(combine(lax.dynamic_slice_in_dim(part, core * half, half, axis=1), got))
         got = lax.ppermute(lax.dynamic_slice_in_dim(joined, (1 - chip) * quarter, quarter, axis=1), 'sp', chip_swap)
+        o = global_keys_part(qkv, qkv_g, kmax, win)
+        got, o = lax.optimization_barrier((got, o))
         g_acc, _, g_l = combine(lax.dynamic_slice_in_dim(joined, chip * quarter, quarter, axis=1), got)
         mine = (g_acc / g_l).astype(BF16)
         other = lax.ppermute(mine, 'sp', chip_swap)
@@ -489,14 +600,8 @@
         other = lax.ppermute(mine, 'sp', core_swap)
         glob_out = jnp.concatenate([jnp.where(core == 0, mine, other), jnp.where(core == 0, other, mine)], axis=0)
 
-        glob_out, w_all = lax.optimization_barrier((glob_out, w_all))
-        y, first = None, 0
-        for n_blk in CHUNKS if n_rows == 16 * QB else (n_rows // QB // 2,) * 2:
-            o = global_keys_part(qkv, qkv_g, kmax, win, local_idx, glob_out, first, n_blk)
-            o_all = lax.all_gather(o, 'tp')
-            y = mlp_rows(tokens, o_all, w_all, y, first, d_o, d_f)
-            first += n_blk
-        return y
+        o = place_rows(o, glob_out, local_idx)
+        return exchange_mlp(tokens, o, w_all, n_tp, d_o, d_f)
 
     row_spec = P(('dp', 'sp'), None)
     head_spec = P(None, 'tp', None)

time: 613 us -> 646 us (1.054)
  Pallas kernels: 532 us -> 580 us
  waiting for transfers between devices: 29 us -> 11.8 us
  local copies, waits for them, and re-layouts: 8.3 us -> 17.6 us
    pallas_call x8 -> x3, Pallas kernels: 245 us -> 292 us  [the longest x1 153 us: exchange_mlp(): pl.pallas_call(functools.partial(exchange_mlp_kernel, n_tp=n_tp, n_rep=n_...]
    ppermute x1, waiting for transfers between devices: 18 us -> 0.01 us  [device_layer(): lax.ppermute(lax.dynamic_slice_in_dim(joined, (1 - chip) * quarter, quart...]
    unnamed x14 -> x17, local copies, waits for them, and re-layouts: 2.48 us -> 12.7 us
  transfers between devices with their start and end apart: 14 -> 10, of which waited for: 6 -> 4; matrix products, arithmetic and copies ran while one was open for 3% -> 2% of each run, Pallas kernels for 77% -> 66%
where the time goes in v3:
time: 646 us
  Pallas kernels  580 us (90%)
  local copies, waits for them, and re-layouts  17.6 us (3%)
  between operations  13.7 us (2%)
  other arithmetic  12 us (2%)
  waiting for transfers between devices  11.8 us (2%)
  starting transfers between devices  10.5 us (2%)
    pallas_call x1, Pallas kernels, exchange_mlp(): pl.pallas_call(functools.partial(exchange_mlp_kernel, n_tp=n_tp, n_rep=n_...  153 us
    pallas_call x1, Pallas kernels, global_queries_part(): pl.pallas_call(functools.partial(global_queries_kernel, kb=kb), grid=(2,...  137 us
    pallas_call x1, Pallas kernels, global_keys_part(): pl.pallas_call(global_keys_kernel, grid=(2, n_rows // rb), in_specs=[row,...  136 us
    pallas_call x1, Pallas kernels, window_part(): pl.pallas_call(window_kernel, grid=(2, n_blk), in_specs=[mid(0), left(1),...  135 us
    pallas_call x1, Pallas kernels, qkv_part(): pl.pallas_call(qkv_kernel, grid_spec=pltpu.PrefetchScalarGridSpec(num_sca...  15.5 us
  transfers between devices with their start and end apart: 10, of which 4 were waited for; matrix products, arithmetic and copies ran while one was open for 2% of the time, Pallas kernels for 66%

profile of v3, /device:TPU:0, one launch (start us, length us, event | category | flops | bytes accessed | tf_op | source)
XLA Modules:
  0.0 645.5 jit_solution(10203862061816436199)
XLA Ops:
  6.5 1.8 fusion.3
  8.4 0.0 all-gather.3.cloned.1.call-update
  8.4 0.2 copy.19.idx_ref
  8.7 0.2 copy.16
  9.0 0.5 copy-done.5
  9.4 0.2 copy.17
  9.6 0.2 copy.18
  9.9 0.1 pad_maximum_fusion.w_ref
  10.0 15.5 %qkv.1 = (bf16[4096,768]{1,0:T(8,128)(2,1)}, bf16[1024,768]{1,0:T(8,128)(2,1)S(1)}, f32[1,256]{1,0:T(1,128)S(1)}) custom-call(s32[1024]{0:T(1024)S(1)} %broadcast_subtract_fusion.pos_ref, s32[1024,1]{1,0:T(8,128)S(1)} %copy.19.idx_ref, bf16[4096,1024]{1,0:T(8,128)(2,1)} %x_hbm.1, bf16[1024,768]{1,0:T(8,128)(2,1)S(1)} %pad_maximum_fusion.w_ref), custom_call_target="tpu_custom_call" | custom-call | flops 8000000000 | bytes 24000000 | tf_op jit(solution)/shard_map/qkv/pallas_call | solution.py:79
  25.5 1.0 constant_dynamic-slice_fusion.2
  26.5 1.1 collective-permute-start
  27.6 1.8 fusion.12
  29.4 1.9 collective-permute-start.2
  31.3 1.5 collective-permute-start.3
  32.8 2.5 compare_reduce_fusion
  35.3 2.4 select_convert_fusion.extra_ref
  37.7 0.1 or_select_fusion.bias_ref
  37.8 1.4 dynamic-slice_add_fusion
  39.2 4.6 collective-permute-start.1
  43.8 135.5 %window_part.1 = (f32[4096,256]{1,0:T(8,128)S(1)}, f32[4096,256]{1,0:T(8,128)}, f32[4096,256]{1,0:T(8,128)}) custom-call(bf16[4096,768]{1,0:T(8,128)(2,1)} %get-tuple-element.18.q_ref.kl_ref.kc_ref.kr_ref.vl_ref.vc_ref.vr_ref.k_ref.v_ref, bf16[4096,768]{1,0:T(8,128)(2,1)} %get-tuple-element.18.q_ref.kl_ref.kc_ref.kr_ref.vl_ref.vc_ref.vr_ref.k_ref.v_ref, ...), custom_call_target="tpu_custom_call" | custom-call | flops 30000001024 | bytes 30000000 | tf_op jit(solution)/shard_map/window_part/pallas_call | solution.py:238
  179.3 2.0 copy-done.3
  181.3 0.2 add.91
  181.5 0.1 collective-permute-start.4
  181.6 2.3 collective-permute-done.4
  183.9 0.1 broadcast_select_fusion.1
  184.0 0.1 pad_maximum_fusion.1.q_ref.kg_ref.vg_ref
  184.1 136.6 %global_queries.1 = f32[3,1024,256]{2,1,0:T(8,128)S(1)} custom-call(bf16[1024,768]{1,0:T(8,128)(2,1)S(1)} %pad_maximum_fusion.1.q_ref.kg_ref.vg_ref, bf16[4096,768]{1,0:T(8,128)(2,1)} %get-tuple-element.18.q_ref.kl_ref.kc_ref.kr_ref.vl_ref.vc_ref.vr_ref.k_ref.v_ref, ...), custom_call_target="tpu_custom_call" | custom-call | flops 33999998976 | bytes 20000000 | tf_op jit(solution)/shard_map/global_queries/pallas_call | solution.py:365
  320.7 1.3 constant_dynamic-slice_fusion.1
  322.0 0.1 collective-permute-start.5
  322.1 3.2 collective-permute-done.5
  325.3 1.4 fusion.1
  326.8 1.4 fusion
  328.2 0.1 pad_maximum_fusion.2
  328.3 0.1 constant_dynamic-slice_fusion
  328.4 0.1 collective-permute-start.6
  328.5 1.1 copy-done.1
  329.6 135.5 %global_keys.1.o_ref = bf16[4096,256]{1,0:T(8,128)(2,1)S(1)} custom-call(bf16[4096,768]{1,0:T(8,128)(2,1)} %get-tuple-element.18.q_ref.kl_ref.kc_ref.kr_ref.vl_ref.vc_ref.vr_ref.k_ref.v_ref, bf16[1024,768]{1,0:T(8,128)(2,1)S(1)} %copy-done.1, bf16[1024,768]{1,0:T(8,128)(2,1)S(1)} %copy-done.1, f32[1,256]{1,0:T(1,128)S(1)} %get-tuple-element.19.kmax_ref, ...), custom_call_target="tpu_custom_call" | custom-call | flops 40000000000 | bytes 32000000 | tf_op jit(solution)/shard_map/global_keys/pallas_call | solution.py:290
  465.1 0.2 fusion.11
  465.3 0.9 collective-permute-start.7
  466.2 4.7 collective-permute-done.7
  471.0 0.1 collective-permute-start.8
  471.0 1.5 collective-permute-done.8
  472.6 0.1 broadcast_select_fusion.3
  472.7 4.0 place.1.o_hbm
  476.7 0.0 copy-start.2
  476.7 1.3 copy-done.2
  478.0 152.9 %exchange_mlp.1 = bf16[4096,1024]{1,0:T(8,128)(2,1)} custom-call(bf16[4096,1024]{1,0:T(8,128)(2,1)} %x_hbm.1, bf16[4096,256]{1,0:T(8,128)(2,1)} %copy-done.2, bf16[8,4,1568,128]{3,2,1,0:T(8,128)(2,1)} %bitcast.57), custom_call_target="tpu_custom_call" | custom-call | flops 52613349376 | bytes 40000000 | tf_op jit(solution)/shard_map/exchange_mlp/pallas_call | solution.py:522
  630.9 7.8 %copy.21 = bf16[4096,1024]{1,0:T(8,128)(2,1)} copy(bf16[4096,1024]{1,0:T(8,128)(2,1)} %exchange_mlp.1) | data formatting | bytes 16777216
  (26 shorter events, 0.2 us)
Async XLA Ops:
  6.5 1.9 copy-start.7
  6.5 471.5 %all-gather.3.cloned.1.call-start = ((), (), s32[]{:S(2)}) async-start(), calls=%async_computation | async-start | bytes 13246464 | tf_op jit(solution)/shard_map/all_gather | solution.py:562
  6.5 2.1 copy-start.4
  8.4 1.0 copy-start.5
  8.4 1.2 copy-start.6
  26.5 11.3 %collective-permute-start = (bf16[512,768]{1,0:T(8,128)(2,1)}, bf16[512,768]{1,0:T(8,128)(2,1)}, u32[]{:S(2)}, u32[]{:S(2)}) collective-permute-start(bf16[512,768]{1,0:T(8,128)(2,1)} %constant_dynamic-slice_fusion.2), channel_id=1, source_target_pairs={{0,1},{1,0},{2,3},{3,2},{4,5},{5,4},{6,7},{7,6},{8,9},{9,8},{10,11... | collective-permute-start | bytes 2359304 | tf_op jit(solution)/shard_map/ppermute | solution.py:579
  29.4 14.4 %collective-permute-start.2 = (bf16[256,512]{1,0:T(8,128)(2,1)}, bf16[256,512]{1,0:T(8,128)(2,1)S(1)}, u32[]{:S(2)}, u32[]{:S(2)}) collective-permute-start(bf16[256,512]{1,0:T(8,128)(2,1)} %get-tuple-element.32), channel_id=1, source_target_pairs={{0,1},{1,2},{2,3},{4,5},{5,6},{6,7},{8,9},{9,10},{10,11},{12,13},{... | collective-permute-start | bytes 786440 | tf_op jit(solution)/shard_map/ppermute | solution.py:568
  31.3 12.5 %collective-permute-start.3 = (bf16[256,512]{1,0:T(8,128)(2,1)S(1)}, bf16[256,512]{1,0:T(8,128)(2,1)S(1)}, u32[]{:S(2)}, u32[]{:S(2)}) collective-permute-start(bf16[256,512]{1,0:T(8,128)(2,1)S(1)} %get-tuple-element.31), channel_id=1, source_target_pairs={{1,0},{2,1},{3,2},{5,4},{6,5},{7,6},{9,8},{10,9},{11,10},{13,12},{... | collective-permute-start | bytes 786440 | tf_op jit(solution)/shard_map/ppermute | solution.py:569
  39.2 142.1 %collective-permute-start.1 = (bf16[512,768]{1,0:T(8,128)(2,1)S(1)}, bf16[512,768]{1,0:T(8,128)(2,1)S(1)}, u32[]{:S(2)}, u32[]{:S(2)}) collective-permute-start(bf16[512,768]{1,0:T(8,128)(2,1)S(1)} %dynamic-slice_add_fusion), channel_id=1, source_target_pairs={{0,2},{1,3},{2,0},{3,1},{4,6},{5,7},{6,4},{7,5},{8,10},{9,11},{10,... | collective-permute-start | bytes 2359304 | tf_op jit(solution)/shard_map/ppermute | solution.py:581
  179.3 2.0 copy-start.3
  181.5 2.4 collective-permute-start.4
  184.1 136.6 %copy-start = (bf16[1024,768]{1,0:T(8,128)(2,1)}, bf16[1024,768]{1,0:T(8,128)(2,1)S(1)}, u32[]{:S(2)}) copy-start(bf16[1024,768]{1,0:T(8,128)(2,1)S(1)} %pad_maximum_fusion.1.q_ref.kg_ref.vg_ref) | copy-start | bytes 4718596
  322.0 3.4 collective-permute-start.5
  328.2 1.4 copy-start.1
  328.4 136.7 %collective-permute-start.6 = (f32[3,256,256]{2,1,0:T(8,128)S(1)}, f32[3,256,256]{2,1,0:T(8,128)S(1)}, u32[]{:S(2)}, u32[]{:S(2)}) collective-permute-start(f32[3,256,256]{2,1,0:T(8,128)S(1)} %constant_dynamic-slice_fusion), channel_id=1, source_target_pairs={{0,2},{1,3},{2,0},{3,1},{4,6},{5,7},{6,4},{7,5},{8,10},{9,11},{10,... | collective-permute-start | bytes 2359304 | tf_op jit(solution)/shard_map/ppermute | solution.py:593
  465.3 5.7 collective-permute-start.7
  471.0 1.6 collective-permute-start.8
  476.7 1.3 copy-start.2
Sparse Core Ops, SparseCore 0:
  10.2 99.7 all-gather.2

commit v4 on v3

--- a/solution.py
+++ b/solution.py
@@ -247,78 +247,6 @@
     )(qkv, qkv, qkv, qkv, qkv, qkv, qkv, halo_l, halo_r, halo_l, halo_r, extra, bias, kmax)
 
 
-def global_keys_kernel(q_ref, kg_ref, vg_ref, kmax_ref, acc_ref, m_ref, l_ref, out_ref,
-                       k_ref, ea_ref, em_ref, el_ref):
-    n = q_ref.shape[0]
-    i = pl.program_id(1)
-
-    @pl.when(i == 0)
-    def _():
-        extra = key_extra(kg_ref.shape[0])
-        for half in range(2):
-            k_ref[half] = own_half(kg_ref[...], extra, half)
-
-    def finish(acc, m, total):
-        m_all = jnp.maximum(m, m_ref[...])
-        a, b = jnp.exp(m - m_all), jnp.exp(m_ref[...] - m_all)
-        out_ref[...] = ((acc * a + acc_ref[...] * b) / (total * a + l_ref[...] * b)).astype(out_ref.dtype)
-
-    q = q_ref[...]
-    neg = shifts(q, kmax_ref[...])
-    low = low_lanes(n)
-    res = [stream(query_rows(q, neg, half), [(k_ref[half, t:t + 256], vg_ref[t:t + 256]) for t in range(0, vg_ref.shape[0], 256)])
-           for half in range(2)]
-    sums = [row_sum(r[1]) for r in res]
-    finish(jnp.where(low, res[0][0], res[1][0]), -pltpu.roll(neg.astype(F32), 64, 1), jnp.where(low, sums[0], sums[1]))
-
-    @pl.when(out_of_range(*sums))
-    def _():
-        def key_rows(c):
-            at = pl.ds(pl.multiple_of(c * 256, 256), 256)
-            return kg_ref[at], vg_ref[at], None
-
-        for half in range(2):
-            exact_head(q_ref[...], half, vg_ref.shape[0], key_rows, ea_ref, em_ref, el_ref)
-        finish(*(jnp.where(low, r[0], r[1]) for r in (ea_ref, em_ref, el_ref)))
-
-
-def global_keys_part(qkv, qkv_g, kmax, win):
-    n_rows, n_glob = qkv.shape[0], qkv_g.shape[0]
-    rb = 512
-    row = pl.BlockSpec((rb, 128), lambda p, i: (i, p))
-    pair = pltpu.VMEM((2, rb, 128), F32)
-    return pl.pallas_call(
-        global_keys_kernel, grid=(2, n_rows // rb),
-        in_specs=[row, pl.BlockSpec((n_glob, 128), lambda p, i: (0, 2 + p)), pl.BlockSpec((n_glob, 128), lambda p, i: (0, 4 + p)),
-                  pl.BlockSpec((1, 128), lambda p, i: (0, p)), row, row, row],
-        out_specs=row, out_shape=jax.ShapeDtypeStruct((n_rows, 256), BF16),
-        scratch_shapes=[pltpu.VMEM((2, n_glob, 128), BF16), pair, pair, pair],
-        compiler_params=params(2), cost_estimate=cost(40e9, 32e6, 16e6), name="global_keys",
-    )(qkv, qkv_g, qkv_g, kmax, *win)
-
-
-def place_kernel(idx_ref, glob_ref, o_ref, out_ref):
-    n = o_ref.shape[0]
-    row = pl.program_id(0) * n + lax.broadcasted_iota(jnp.int32, (n, 1), 0)
-    hit = jnp.where(idx_ref[...] == row, 1.0, 0.0)
-    placed = dot_nn(hit.astype(BF16), glob_ref[...])
-    out_ref[...] = jnp.where(row_sum(hit) > 0.5, placed, o_ref[...].astype(F32)).astype(out_ref.dtype)
-
-
-def place_rows(o, glob_out, local_idx):
-    n_rows, width = o.shape
-    n_glob = local_idx.shape[0]
-    rb = 512
-    return pl.pallas_call(
-        place_kernel, grid=(n_rows // rb,),
-        in_specs=[pl.BlockSpec((1, n_glob), lambda i: (0, 0)), pl.BlockSpec((n_glob, width), lambda i: (0, 0)),
-                  pl.BlockSpec((rb, width), lambda i: (i, 0))],
-        out_specs=pl.BlockSpec((rb, width), lambda i: (i, 0)),
-        out_shape=jax.ShapeDtypeStruct((n_rows, width), BF16),
-        compiler_params=params(1), cost_estimate=cost(2e9, 5e6), name="place",
-    )(local_idx[None, :], glob_out, o)
-
-
 def global_queries_kernel(q_ref, k_ref, v_ref, kmax_ref, out_ref, acc_ref, m_ref, l_ref, *, kb):
     j = pl.program_id(2)
     n = q_ref.shape[0]
@@ -373,7 +301,8 @@
     )(qkv_g, qkv, qkv, kmax)
 
 
-def exchange_mlp_kernel(x_hbm, o_hbm, w_hbm, y_hbm, x_ref, o_ref, wo_ref, w2_ref, w1_ref, load_sem, y_sem,
+def exchange_mlp_kernel(x_hbm, w_hbm, qkv_hbm, qkvg_hbm, acc_hbm, m_hbm, l_hbm, glob_hbm, idx_ref, y_hbm,
+                        x_ref, o_ref, wo_ref, w2_ref, w1_ref, q_ref, kg_ref, glob_ref, win_ref, load_sem, win_sem, y_sem,
                         up_send, up_recv, down_send, down_recv, *, n_tp, n_rep, d_o, d_f, rb):
     me = lax.axis_index('tp')
     n_blk = x_ref.shape[0] // rb
@@ -389,16 +318,27 @@
     def _():
         pl.semaphore_signal(barrier, inc=1, device_id={'tp': me + 1}, device_id_type=pl.DeviceIdType.MESH)
 
-    own = pltpu.make_async_copy(o_hbm, o_ref.at[me], load_sem.at[0])
-    own.start()
-    copies = [pltpu.make_async_copy(x_hbm, x_ref, load_sem.at[1])]
+    early = [pltpu.make_async_copy(qkv_hbm.at[:, pl.ds(0, 256)], q_ref, load_sem.at[0]),
+             pltpu.make_async_copy(qkvg_hbm.at[:, pl.ds(256, 512)], kg_ref, load_sem.at[1]),
+             pltpu.make_async_copy(glob_hbm, glob_ref, load_sem.at[2])]
+
+    def rows_of(b):
+        return pl.ds(pl.multiple_of(b * rb, rb), rb)
+
+    def fetch(b):
+        return [pltpu.make_async_copy(h.at[rows_of(b)], win_ref.at[b % 2, n], win_sem.at[b % 2, n])
+                for n, h in enumerate((acc_hbm, m_hbm, l_hbm))]
+
+    for c in early + fetch(0):
+        c.start()
+    copies = [pltpu.make_async_copy(x_hbm, x_ref, load_sem.at[3])]
     piece = wo_ref.shape[1] // n_rep
     for j in range(n_rep):
         for t in range(n_tp):
             lanes = pl.ds(j * piece, piece)
             for src, n, dst in ((0, d_o, wo_ref), (d_o, d_f, w2_ref), (d_o + d_f, d_f, w1_ref)):
                 copies.append(pltpu.make_async_copy(w_hbm.at[j, t, pl.ds(src, n)], dst.at[pl.ds(t * n, n), lanes],
-                                                    load_sem.at[2 + len(copies)]))
+                                                    load_sem.at[3 + len(copies)]))
     for c in copies:
         c.start()
 
@@ -412,10 +352,44 @@
     def _():
         pl.semaphore_wait(barrier, 2)
 
-    own.wait()
-
-    def rows_of(b):
-        return pl.ds(pl.multiple_of(b * rb, rb), rb)
+    for c in early:
+        c.wait()
+
+    def attend(b):
+        @pl.when(b + 1 < n_blk)
+        def _():
+            for c in fetch(b + 1):
+                c.start()
+
+        for c in fetch(b):
+            c.wait()
+
+        @pl.loop(0, rb // QB)
+        def _(r):
+            at = pl.ds(pl.multiple_of(r * QB, QB), QB)
+            rows = pl.ds(pl.multiple_of(b * rb + r * QB, QB), QB)
+            low = low_lanes(QB)
+            parts = []
+            for pr in range(2):
+                cols = slice(pr * 128, pr * 128 + 128)
+                q = q_ref[rows, cols]
+                zero = jnp.zeros_like(q)
+                q2 = jnp.concatenate([jnp.where(low, q, zero), jnp.where(low, zero, q)], axis=0)
+                sc = dot_nt(q2, kg_ref[:, cols])
+                top = jnp.max(sc, axis=1, keepdims=True)
+                e = jnp.exp(sc - top)
+                total = row_sum(e)
+                acc = dot_nn(e.astype(BF16), kg_ref[:, 256 + pr * 128:256 + pr * 128 + 128])
+                acc, m, total = (jnp.where(low, v[:QB], v[QB:]) for v in (acc, top, total))
+                acc_w, m_w, l_w = (win_ref[b % 2, n, at, cols] for n in range(3))
+                m_all = jnp.maximum(m, m_w)
+                f, f_w = jnp.exp(m - m_all), jnp.exp(m_w - m_all)
+                parts.append((acc * f + acc_w * f_w) / (total * f + l_w * f_w))
+            row = b * rb + r * QB + lax.broadcasted_iota(jnp.int32, (QB, 1), 0)
+            hit = jnp.where(idx_ref[...] == row, 1.0, 0.0)
+            placed = dot_nn(hit.astype(BF16), glob_ref[...])
+            mine = row_sum(hit) > 0.5
+            o_ref[me, rows] = jnp.where(mine, placed, jnp.concatenate(parts, axis=1)).astype(BF16)
 
     def up(d, b):
         at = o_ref.at[me - d, rows_of(b)]
@@ -441,14 +415,14 @@
         def _():
             down(0, b).start()
 
-    ahead = min(2, n_blk)
-    for b in range(ahead):
-        send_own(b)
+    attend(0)
+    attend(1)
+    send_own(0)
 
     def step(s, carry):
-        @pl.when(s + ahead < n_blk)
-        def _():
-            send_own(s + ahead)
+        @pl.when(s + 1 < n_blk)
+        def _():
+            send_own(s + 1)
 
         for d in range(1, n_tp):
             b = s - (d - 1)
@@ -468,6 +442,10 @@
                     @pl.when(me > 0)
                     def _():
                         down(d, b).start()
+
+        @pl.when(s + 2 < n_blk)
+        def _():
+            attend(s + 2)
 
         @pl.when(s == n_tp - 2)
         def _():
@@ -512,8 +490,9 @@
     lax.fori_loop(0, n_blk, finish, 0)
 
 
-def exchange_mlp(tokens, o, w_all, n_tp, d_o, d_f):
+def exchange_mlp(tokens, w_all, qkv, qkv_g, win, glob_out, local_idx, n_tp, d_o, d_f):
     n_rows, dim = tokens.shape
+    n_glob = local_idx.shape[0]
     n_rep = w_all.shape[0]
     rb = min(512, n_rows // 2)
     n_blk = n_rows // rb
@@ -521,14 +500,29 @@
     dma = pltpu.SemaphoreType.DMA
     return pl.pallas_call(
         functools.partial(exchange_mlp_kernel, n_tp=n_tp, n_rep=n_rep, d_o=d_o, d_f=d_f, rb=rb),
-        in_specs=[anywhere] * 3, out_specs=anywhere, out_shape=jax.ShapeDtypeStruct(tokens.shape, BF16),
+        in_specs=[anywhere] * 8 + [pl.BlockSpec(memory_space=pltpu.VMEM)], out_specs=anywhere,
+        out_shape=jax.ShapeDtypeStruct(tokens.shape, BF16),
         scratch_shapes=[pltpu.VMEM((n_rows, dim), BF16), pltpu.VMEM((n_tp, n_rows, d_o), BF16),
                         pltpu.VMEM((n_tp * d_o, dim), BF16), pltpu.VMEM((n_tp * d_f, dim), BF16),
-                        pltpu.VMEM((n_tp * d_f, dim), BF16), dma((2 + 3 * n_rep * n_tp + 1,)), dma((n_blk,)),
+                        pltpu.VMEM((n_tp * d_f, dim), BF16), pltpu.VMEM((n_rows, d_o), BF16),
+                        pltpu.VMEM((n_glob, 2 * d_o), BF16), pltpu.VMEM((n_glob, d_o), BF16),
+                        pltpu.VMEM((2, 3, rb, d_o), F32), dma((4 + 3 * n_rep * n_tp,)), dma((2, 3)), dma((n_blk,)),
                         dma((n_tp - 1, n_blk)), dma((n_tp - 1, n_blk)), dma((n_tp - 1, n_blk)), dma((n_tp - 1, n_blk))],
-        compiler_params=pltpu.CompilerParams(collective_id=1, has_side_effects=True, vmem_limit_bytes=56 << 20),
+        compiler_params=pltpu.CompilerParams(collective_id=1, has_side_effects=True, vmem_limit_bytes=60 << 20),
         cost_estimate=cost(2 * n_rows * dim * (dim + 2 * n_tp * d_f), 40e6), name="exchange_mlp",
-    )(tokens, o, w_all)
+    )(tokens, w_all, qkv, qkv_g, *win, glob_out, local_idx[None, :])
+
+
+def copy_kernel(a_ref, b_ref):
+    b_ref[...] = a_ref[...]
+
+
+def streamed(a):
+    rb = a.shape[0] // 4
+    spec = pl.BlockSpec((rb, a.shape[1]), lambda i: (i, 0))
+    return pl.pallas_call(copy_kernel, grid=(4,), in_specs=[spec], out_specs=spec,
+                          out_shape=jax.ShapeDtypeStruct(a.shape, a.dtype),
+                          compiler_params=params(1), name="result")(a)
 
 
 def combine(a, b):
@@ -579,20 +573,19 @@
         other = lax.ppermute(lax.dynamic_slice_in_dim(picked, (1 - core) * half, half), 'sp', core_swap)
         mine = mine + other
         got = lax.ppermute(mine, 'sp', chip_swap)
-        win = window_part(qkv, halo_l, halo_r, extra, bias, kmax)
-        got, win = lax.optimization_barrier((got, win))
         mine = mine + got
         other = lax.ppermute(mine, 'sp', core_swap)
         qkv_g = jnp.concatenate([jnp.where(core == 0, mine, other), jnp.where(core == 0, other, mine)], axis=0)
 
         part = global_queries_part(qkv_g, qkv, kmax)
+        part, kmax = lax.optimization_barrier((part, kmax))
 
         quarter = n_glob // 4
         got = lax.ppermute(lax.dynamic_slice_in_dim(part, (1 - core) * half, half, axis=1), 'sp', core_swap)
         joined = jnp.stack(combine(lax.dynamic_slice_in_dim(part, core * half, half, axis=1), got))
         got = lax.ppermute(lax.dynamic_slice_in_dim(joined, (1 - chip) * quarter, quarter, axis=1), 'sp', chip_swap)
-        o = global_keys_part(qkv, qkv_g, kmax, win)
-        got, o = lax.optimization_barrier((got, o))
+        win = window_part(qkv, halo_l, halo_r, extra, bias, kmax)
+        got, win = lax.optimization_barrier((got, win))
         g_acc, _, g_l = combine(lax.dynamic_slice_in_dim(joined, chip * quarter, quarter, axis=1), got)
         mine = (g_acc / g_l).astype(BF16)
         other = lax.ppermute(mine, 'sp', chip_swap)
@@ -600,8 +593,7 @@
         other = lax.ppermute(mine, 'sp', core_swap)
         glob_out = jnp.concatenate([jnp.where(core == 0, mine, other), jnp.where(core == 0, other, mine)], axis=0)
 
-        o = place_rows(o, glob_out, local_idx)
-        return exchange_mlp(tokens, o, w_all, n_tp, d_o, d_f)
+        return streamed(exchange_mlp(tokens, w_all, qkv, qkv_g, win, glob_out, local_idx, n_tp, d_o, d_f))
 
     row_spec = P(('dp', 'sp'), None)
     head_spec = P(None, 'tp', None)

time: 646 us -> 532 us (0.82)
  Pallas kernels: 580 us -> 463 us
  waiting for transfers between devices: 11.8 us -> 27.8 us
  local copies, waits for them, and re-layouts: 17.6 us -> 4.71 us
    pallas_call x2 -> x1, Pallas kernels: 139 us -> 7.12 us  [streamed(): pl.pallas_call(copy_kernel, grid=(4,), in_specs=[spec], out_specs=spec, o...]
    ppermute x1, waiting for transfers between devices: 0.01 us -> 18.2 us  [device_layer(): got = lax.ppermute(mine, 'sp', chip_swap)]
    pallas_call x1, Pallas kernels: 153 us -> 168 us  [exchange_mlp(): pl.pallas_call(functools.partial(exchange_mlp_kernel, n_tp=n_tp, n_rep=n_...]
    unnamed x17 -> x14, local copies, waits for them, and re-layouts: 12.7 us -> 2.59 us
  transfers between devices with their start and end apart: 10 -> 10, of which waited for: 4 -> 5; matrix products, arithmetic and copies ran while one was open for 2% -> 2% of each run, Pallas kernels for 66% -> 54%
where the time goes in v4:
time: 532 us; the launch traced here: 531 us
  Pallas kernels  463 us (87%)
  waiting for transfers between devices  27.8 us (5%)
  between operations  13.7 us (3%)
  starting transfers between devices  11.1 us (2%)
  other arithmetic  10.4 us (2%)
    pallas_call x1, Pallas kernels, exchange_mlp(): pl.pallas_call(functools.partial(exchange_mlp_kernel, n_tp=n_tp, n_rep=n_...  168 us
    pallas_call x1, Pallas kernels, global_queries_part(): pl.pallas_call(functools.partial(global_queries_kernel, kb=kb), grid=(2,...  137 us
    pallas_call x1, Pallas kernels, window_part(): pl.pallas_call(window_kernel, grid=(2, n_blk), in_specs=[mid(0), left(1),...  135 us
    ppermute x1, waiting for transfers between devices, device_layer(): got = lax.ppermute(mine, 'sp', chip_swap)  18.2 us
    pallas_call x1, Pallas kernels, qkv_part(): pl.pallas_call(qkv_kernel, grid_spec=pltpu.PrefetchScalarGridSpec(num_sca...  15.9 us
  transfers between devices with their start and end apart: 10, of which 5 were waited for; matrix products, arithmetic and copies ran while one was open for 2% of the time, Pallas kernels for 54%

profile of v4, /device:TPU:0, one launch (start us, length us, event | category | flops | bytes accessed | tf_op | source)
XLA Modules:
  0.0 531.1 jit_solution(11735112296026046042)
XLA Ops:
  6.5 1.9 fusion.3
  8.4 0.0 all-gather.3.cloned.1.call-update
  8.5 0.2 copy.19.idx_ref
  8.7 0.0 copy-start.5
  8.8 0.2 copy.16
  9.0 0.5 copy-done.4
  9.5 0.2 copy.17
  9.7 0.1 copy-done.5
  9.8 0.2 copy.18
  10.0 0.1 pad_maximum_fusion.w_ref
  10.1 15.9 %qkv.1 = (bf16[4096,768]{1,0:T(8,128)(2,1)}, bf16[1024,768]{1,0:T(8,128)(2,1)S(1)}, f32[1,256]{1,0:T(1,128)S(1)}) custom-call(s32[1024]{0:T(1024)S(1)} %broadcast_subtract_fusion.pos_ref, s32[1024,1]{1,0:T(8,128)S(1)} %copy.19.idx_ref, bf16[4096,1024]{1,0:T(8,128)(2,1)} %x_hbm.1, bf16[1024,768]{1,0:T(8,128)(2,1)S(1)} %pad_maximum_fusion.w_ref), custom_call_target="tpu_custom_call" | custom-call | flops 8000000000 | bytes 24000000 | tf_op jit(solution)/shard_map/qkv/pallas_call | solution.py:79
  26.0 0.1 constant_dynamic-slice_fusion.2
  26.1 0.3 collective-permute-start
  26.3 2.0 collective-permute-done
  28.4 1.3 dynamic-slice_add_fusion
  29.7 3.1 collective-permute-start.1
  32.8 1.1 fusion.12
  33.8 1.3 collective-permute-start.6
  35.1 3.0 collective-permute-start.5
  38.2 18.2 %collective-permute-done.1 = bf16[512,768]{1,0:T(8,128)(2,1)S(1)} collective-permute-done((bf16[512,768]{1,0:T(8,128)(2,1)S(1)}, bf16[512,768]{1,0:T(8,128)(2,1)S(1)}, u32[]{:S(2)}, u32[]{:S(2)}) %collective-permute-start.1) | collective-permute-done | bytes 786464 | tf_op jit(solution)/shard_map/ppermute | solution.py:575
  56.4 0.2 add.88
  56.6 0.1 collective-permute-start.2
  56.7 2.5 compare_reduce_fusion
  59.3 0.1 broadcast_select_fusion.1
  59.4 0.1 pad_maximum_fusion.1.q_ref.qkvg_hbm
  59.5 136.6 %global_queries.1 = f32[3,1024,256]{2,1,0:T(8,128)S(1)} custom-call(bf16[1024,768]{1,0:T(8,128)(2,1)S(1)} %pad_maximum_fusion.1.q_ref.qkvg_hbm, bf16[4096,768]{1,0:T(8,128)(2,1)} %get-tuple-element.17.k_ref.v_ref.q_ref.kl_ref.kc_ref.kr_ref.vl_ref.vc_ref.vr_ref.qkv_hbm, ...), custom_call_target="tpu_custom_call" | custom-call | flops 33999998976 | bytes 20000000 | tf_op jit(solution)/shard_map/global_queries/pallas_call | solution.py:293
  196.1 0.1 constant_dynamic-slice_fusion.1
  196.2 0.5 collective-permute-start.3
  196.8 0.1 or_select_fusion.bias_ref
  196.9 2.4 select_convert_fusion.extra_ref
  199.3 0.6 collective-permute-done.3
  199.8 0.2 fusion.1
  200.0 0.2 fusion
  200.2 0.1 pad_maximum_fusion.2
  200.3 0.1 constant_dynamic-slice_fusion
  200.4 2.6 collective-permute-start.4
  203.0 135.5 %window_part.1 = (f32[4096,256]{1,0:T(8,128)S(1)}, f32[4096,256]{1,0:T(8,128)}, f32[4096,256]{1,0:T(8,128)}) custom-call(bf16[4096,768]{1,0:T(8,128)(2,1)} %get-tuple-element.17.k_ref.v_ref.q_ref.kl_ref.kc_ref.kr_ref.vl_ref.vc_ref.vr_ref.qkv_hbm, bf16[4096,768]{1,0:T(8,128)(2,1)} %get-tuple-element.17.k_ref.v_ref.q_ref.kl_ref.kc_ref.kr_ref.vl_ref.vc_ref.vr_ref.qkv_hbm, ...), custom_call_target="tpu_custom_call" | custom-call | flops 30000001024 | bytes 30000000 | tf_op jit(solution)/shard_map/window_part/pallas_call | solution.py:238
  338.5 2.0 copy-done.2
  340.4 0.0 collective-permute-done.4
  340.4 0.1 fusion.11
  340.6 0.1 collective-permute-start.7
  340.7 5.4 %collective-permute-done.7 = bf16[256,256]{1,0:T(8,128)(2,1)S(1)} collective-permute-done((bf16[256,256]{1,0:T(8,128)(2,1)S(1)}, bf16[256,256]{1,0:T(8,128)(2,1)S(1)}, u32[]{:S(2)}, u32[]{:S(2)}) %collective-permute-start.7) | collective-permute-done | bytes 131104 | tf_op jit(solution)/shard_map/ppermute | solution.py:591
  346.2 0.1 collective-permute-start.8
  346.3 1.5 collective-permute-done.8
  347.8 0.1 broadcast_select_fusion.3
  347.9 0.8 pad_maximum_fusion.3.glob_hbm
  348.7 168.4 %exchange_mlp.1.a_ref = bf16[4096,1024]{1,0:T(8,128)(2,1)} custom-call(bf16[4096,1024]{1,0:T(8,128)(2,1)} %x_hbm.1, bf16[8,4,1568,128]{3,2,1,0:T(8,128)(2,1)} %bitcast.57, bf16[4096,768]{1,0:T(8,128)(2,1)} %get-tuple-element.17.k_ref.v_ref.q_ref.kl_ref.kc_ref.kr_ref.vl_ref.vc_ref.vr_ref.qkv_hbm, bf16[1024,768]{1,0:T(8,128)(2,1)} %copy-done, ...), custom_call_target="tpu_custom_call" | custom-call | flops 52613349376 | bytes 40000000 | tf_op jit(solution)/shard_map/exchange_mlp/pallas_call | solution.py:501
  517.2 7.1 %result.1 = bf16[4096,1024]{1,0:T(8,128)(2,1)} custom-call(bf16[4096,1024]{1,0:T(8,128)(2,1)} %exchange_mlp.1.a_ref), custom_call_target="tpu_custom_call" | custom-call | tf_op jit(solution)/shard_map/result/pallas_call | solution.py:523
  (22 shorter events, 0.2 us)
Async XLA Ops:
  6.5 342.2 %all-gather.3.cloned.1.call-start = ((), (), s32[]{:S(2)}) async-start(), calls=%async_computation | async-start | bytes 13246464 | tf_op jit(solution)/shard_map/all_gather | solution.py:556
  6.5 1.9 copy-start.6
  6.5 2.2 copy-start.3
  8.4 1.0 copy-start.4
  8.5 1.7 copy-start.1
  8.7 1.1 copy-start.5
  26.1 2.3 collective-permute-start
  29.7 26.7 %collective-permute-start.1 = (bf16[512,768]{1,0:T(8,128)(2,1)S(1)}, bf16[512,768]{1,0:T(8,128)(2,1)S(1)}, u32[]{:S(2)}, u32[]{:S(2)}) collective-permute-start(bf16[512,768]{1,0:T(8,128)(2,1)S(1)} %dynamic-slice_add_fusion), channel_id=1, source_target_pairs={{0,2},{1,3},{2,0},{3,1},{4,6},{5,7},{6,4},{7,5},{8,10},{9,11},{10,... | collective-permute-start | bytes 2359304 | tf_op jit(solution)/shard_map/ppermute | solution.py:575
  33.8 169.1 %collective-permute-start.6 = (bf16[256,512]{1,0:T(8,128)(2,1)S(1)}, bf16[256,512]{1,0:T(8,128)(2,1)S(1)}, u32[]{:S(2)}, u32[]{:S(2)}) collective-permute-start(bf16[256,512]{1,0:T(8,128)(2,1)S(1)} %get-tuple-element.31), channel_id=1, source_target_pairs={{1,0},{2,1},{3,2},{5,4},{6,5},{7,6},{9,8},{10,9},{11,10},{13,12},{... | collective-permute-start | bytes 786440 | tf_op jit(solution)/shard_map/ppermute | solution.py:563
  35.1 167.8 %collective-permute-start.5 = (bf16[256,512]{1,0:T(8,128)(2,1)S(1)}, bf16[256,512]{1,0:T(8,128)(2,1)S(1)}, u32[]{:S(2)}, u32[]{:S(2)}) collective-permute-start(bf16[256,512]{1,0:T(8,128)(2,1)S(1)} %get-tuple-element.32), channel_id=1, source_target_pairs={{0,1},{1,2},{2,3},{4,5},{5,6},{6,7},{8,9},{9,10},{10,11},{12,13},{... | collective-permute-start | bytes 786440 | tf_op jit(solution)/shard_map/ppermute | solution.py:562
  56.6 2.6 collective-permute-start.2
  59.5 136.6 %copy-start = (bf16[1024,768]{1,0:T(8,128)(2,1)}, bf16[1024,768]{1,0:T(8,128)(2,1)S(1)}, u32[]{:S(2)}) copy-start(bf16[1024,768]{1,0:T(8,128)(2,1)S(1)} %pad_maximum_fusion.1.q_ref.qkvg_hbm) | copy-start | bytes 4718596
  196.2 3.6 collective-permute-start.3
  200.4 140.1 %collective-permute-start.4 = (f32[3,256,256]{2,1,0:T(8,128)S(1)}, f32[3,256,256]{2,1,0:T(8,128)S(1)}, u32[]{:S(2)}, u32[]{:S(2)}) collective-permute-start(f32[3,256,256]{2,1,0:T(8,128)S(1)} %constant_dynamic-slice_fusion), channel_id=1, source_target_pairs={{0,2},{1,3},{2,0},{3,1},{4,6},{5,7},{6,4},{7,5},{8,10},{9,11},{10,... | collective-permute-start | bytes 2359304 | tf_op jit(solution)/shard_map/ppermute | solution.py:586
  338.5 2.0 copy-start.2
  340.6 5.6 %collective-permute-start.7 = (bf16[256,256]{1,0:T(8,128)(2,1)S(1)}, bf16[256,256]{1,0:T(8,128)(2,1)S(1)}, u32[]{:S(2)}, u32[]{:S(2)}) collective-permute-start(bf16[256,256]{1,0:T(8,128)(2,1)S(1)} %fusion.11), channel_id=1, source_target_pairs={{0,2},{1,3},{2,0},{3,1},{4,6},{5,7},{6,4},{7,5},{8,10},{9,11},{10,... | collective-permute-start | bytes 393224 | tf_op jit(solution)/shard_map/ppermute | solution.py:591
  346.2 1.6 collective-permute-start.8
Sparse Core Ops, SparseCore 0:
  10.2 101.3 all-gather.2

commit v5 on v4

--- a/solution.py
+++ b/solution.py
@@ -13,6 +13,8 @@
 FLOOR = -3.0e38
 F32 = jnp.float32
 BF16 = jnp.bfloat16
+LANES = 128
+HEAD = 64
 NT = (((1,), (1,)), ((), ()))
 
 
@@ -24,7 +26,7 @@
     return jnp.dot(a, b, preferred_element_type=F32)
 
 
-def params(n_axes, vmem_mib=48):
+def params(n_axes, vmem_mib=60):
     return pltpu.CompilerParams(
         dimension_semantics=("arbitrary",) * n_axes, vmem_limit_bytes=vmem_mib << 20)
 
@@ -35,8 +37,8 @@
 
 def head_sums(rows):
     n = rows.shape[1]
-    r = lax.broadcasted_iota(jnp.int32, (n, n), 0) // 64
-    c = lax.broadcasted_iota(jnp.int32, (n, n), 1) // 64
+    r = lax.broadcasted_iota(jnp.int32, (n, n), 0) // HEAD
+    c = lax.broadcasted_iota(jnp.int32, (n, n), 1) // HEAD
     pick = jnp.where(r == (c + 1 - 2 * (c % 2)), 1.0, 0.0).astype(BF16)
     wide = rows.astype(F32)
     return dot_nn((wide * wide).astype(BF16), pick)
@@ -46,7 +48,7 @@
     step = pl.program_id(0)
     n_blk = x_ref.shape[0]
     lo = step * n_blk
-    gb = 128
+    gb = LANES
 
     @pl.when(step == 0)
     def _():
@@ -55,7 +57,7 @@
 
     rows = dot_nn(x_ref[...], w_ref[...]).astype(BF16)
     qkv_ref[...] = rows
-    kmax_ref[...] = jnp.maximum(kmax_ref[...], jnp.max(head_sums(rows[:, 256:512]), axis=0, keepdims=True))
+    kmax_ref[...] = jnp.maximum(kmax_ref[...], jnp.max(head_sums(rows[:, QB:512]), axis=0, keepdims=True))
 
     @pl.loop(0, idx_ref.shape[0] // gb)
     def _(b):
@@ -83,16 +85,16 @@
             in_specs=[pl.BlockSpec((n_glob, 1), lambda i, p: (0, 0)), pl.BlockSpec((rb, dim), lambda i, p: (i, 0)),
                       pl.BlockSpec((dim, width), lambda i, p: (0, 0))],
             out_specs=[pl.BlockSpec((rb, width), lambda i, p: (i, 0)), pl.BlockSpec((n_glob, width), lambda i, p: (0, 0)),
-                       pl.BlockSpec((1, 256), lambda i, p: (0, 0))],
+                       pl.BlockSpec((1, QB), lambda i, p: (0, 0))],
             scratch_shapes=[pltpu.VMEM((n_glob, width), F32)]),
         out_shape=[jax.ShapeDtypeStruct((n_rows, width), BF16), jax.ShapeDtypeStruct((n_glob, width), BF16),
-                   jax.ShapeDtypeStruct((1, 256), F32)],
+                   jax.ShapeDtypeStruct((1, QB), F32)],
         compiler_params=params(1), cost_estimate=cost(8e9, 24e6), name="qkv",
     )(local_idx, local_idx[:, None], tokens, w_cat)
 
 
 def low_lanes(n):
-    return lax.broadcasted_iota(jnp.int32, (n, 128), 1) < 64
+    return lax.broadcasted_iota(jnp.int32, (n, LANES), 1) < HEAD
 
 
 def shifts(q, kmax):
@@ -105,19 +107,19 @@
 
 
 def query_rows(q, neg, half):
-    lane = lax.broadcasted_iota(jnp.int32, q.shape, 1) % 64
+    lane = lax.broadcasted_iota(jnp.int32, q.shape, 1) % HEAD
     return own_half(q, jnp.where(lane == 0, neg, jnp.ones_like(neg)), half)
 
 
 def key_extra(n):
-    return jnp.where(lax.broadcasted_iota(jnp.int32, (n, 128), 1) % 64 == 0, 1.0, 0.0).astype(BF16)
+    return jnp.where(lax.broadcasted_iota(jnp.int32, (n, LANES), 1) % HEAD == 0, 1.0, 0.0).astype(BF16)
 
 
 def stream(q_rows, tiles):
     acc = total = None
     for keys, values in tiles:
         e = jnp.exp(dot_nt(q_rows, keys))
-        part = e[:, :128] + e[:, 128:]
+        part = e[:, :LANES] + e[:, LANES:]
         out = dot_nn(e.astype(BF16), values)
         acc = out if acc is None else acc + out
         total = part if total is None else total + part
@@ -133,14 +135,20 @@
     return jnp.logical_not(functools.reduce(jnp.logical_and, good))
 
 
+def exact_heads(q, n_keys, key_rows, acc_ref, m_ref, l_ref):
+    @pl.loop(0, 2)
+    def _(half):
+        exact_head(q, half, n_keys, key_rows, acc_ref, m_ref, l_ref)
+
+
 def exact_head(q, half, n_keys, key_rows, acc_ref, m_ref, l_ref):
-    low = low_lanes(q.shape[0])
-    q1 = jnp.where(low if half == 0 else jnp.logical_not(low), q, jnp.zeros_like(q))
+    mine = lax.broadcasted_iota(jnp.int32, q.shape, 1) // HEAD == half
+    q1 = jnp.where(mine, q, jnp.zeros_like(q))
     acc_ref[half] = jnp.zeros(q.shape, F32)
     l_ref[half] = jnp.zeros(q.shape, F32)
     m_ref[half] = jnp.full(q.shape, FLOOR, F32)
 
-    @pl.loop(0, n_keys // 256)
+    @pl.loop(0, n_keys // QB)
     def _(c):
         keys, values, bias = key_rows(c)
         s = dot_nt(q1, keys)
@@ -156,13 +164,14 @@
 
 
 def window_kernel(q_ref, kl_ref, kc_ref, kr_ref, vl_ref, vc_ref, vr_ref, hkl_ref, hkr_ref, hvl_ref, hvr_ref,
-                  extra_ref, bias_ref, kmax_ref, acc_ref, m_ref, l_ref, tri_ref, key_ref, val_ref, ea_ref, em_ref, el_ref):
-    i = pl.program_id(1)
+                  extra_ref, bias_ref, kmax_ref, *refs, first, n_blk):
+    acc_ref, m_ref, l_ref, tri_ref, key_ref, val_ref, ea_ref, em_ref, el_ref = refs[-9:]
+    i = first + pl.program_id(1)
     n = q_ref.shape[0]
     is_first = i == 0
-    is_last = i == pl.num_programs(1) - 1
-
-    @pl.when(i == 0)
+    is_last = i == n_blk - 1
+
+    @pl.when(pl.program_id(1) == 0)
     def _():
         r_i = lax.broadcasted_iota(jnp.int32, (QB, QB), 0)
         c_i = lax.broadcasted_iota(jnp.int32, (QB, QB), 1)
@@ -188,7 +197,7 @@
             extra = extra_ref[pl.ds(pl.multiple_of(i * n + t * QB, QB), QB), :]
             s = dot_nt(qx[b0 * QB:b1 * QB], own_half(key_ref[t * QB:(t + 1) * QB], extra, half))
             e = jnp.exp(s + window_mask(tri_ref, t, b0, b1))
-            part = e[:, :128] + e[:, 128:]
+            part = e[:, :LANES] + e[:, LANES:]
             out = dot_nn(e.astype(BF16), val_ref[t * QB:(t + 1) * QB])
             for b in range(b0, b1):
                 r = slice((b - b0) * QB, (b - b0 + 1) * QB)
@@ -199,7 +208,7 @@
     low = low_lanes(n)
     acc_ref[...] = jnp.where(low, accs[0], accs[1])
     l_ref[...] = jnp.where(low, sums[0], sums[1])
-    m_ref[...] = -pltpu.roll(neg.astype(F32), 64, 1)
+    m_ref[...] = -pltpu.roll(neg.astype(F32), HEAD, 1)
 
     @pl.when(out_of_range(*sums))
     def _():
@@ -212,8 +221,7 @@
                 bias = bias_ref[:, pl.ds(pl.multiple_of(i * n + (b + c) * QB, QB), QB)]
                 return key_ref[at], val_ref[at], bias + tri_ref[pl.ds(pl.multiple_of((2 - c) * QB, QB), QB)]
 
-            for half in range(2):
-                exact_head(q_ref[rows], half, 3 * QB, key_rows, ea_ref, em_ref, el_ref)
+            exact_heads(q_ref[rows], 3 * QB, key_rows, ea_ref, em_ref, el_ref)
             low = low_lanes(QB)
             for out, src in ((acc_ref, ea_ref), (m_ref, em_ref), (l_ref, el_ref)):
                 out[rows] = jnp.where(low, src[0], src[1])
@@ -223,28 +231,79 @@
     return tri_ref[(b0 - t + 2) * QB:(b1 - t + 2) * QB]
 
 
-def window_part(qkv, halo_l, halo_r, extra, bias, kmax):
+def window_part(qkv, halo_l, halo_r, extra, bias, kmax, first, last, win=()):
     n_rows = qkv.shape[0]
-    rb = min(1024, n_rows)
+    rb = n_rows // 4
     per = rb // QB
     n_blk, n_small = n_rows // rb, n_rows // QB
-    mid = lambda c: pl.BlockSpec((rb, 128), lambda p, i: (i, 2 * c + p))
-    left = lambda c: pl.BlockSpec((QB, 128), lambda p, i: (jnp.maximum(i * per - 1, 0), 2 * c + p))
-    right = lambda c: pl.BlockSpec((QB, 128), lambda p, i: (jnp.minimum(i * per + per, n_small - 1), 2 * c + p))
-    halo = lambda c: pl.BlockSpec((QB, 128), lambda p, i: (0, 2 * c + p))
+    mid = lambda c: pl.BlockSpec((rb, LANES), lambda p, i: (first + i, 2 * c + p))
+    left = lambda c: pl.BlockSpec((QB, LANES), lambda p, i: (jnp.maximum((first + i) * per - 1, 0), 2 * c + p))
+    right = lambda c: pl.BlockSpec((QB, LANES), lambda p, i: (jnp.minimum((first + i) * per + per, n_small - 1), 2 * c + p))
+    halo = lambda c: pl.BlockSpec((QB, LANES), lambda p, i: (0, 2 * c + p))
     whole = lambda a: pl.BlockSpec(a.shape, lambda p, i: (0,) * a.ndim)
-    out = jax.ShapeDtypeStruct((n_rows, 256), F32)
-    pair = pltpu.VMEM((2, QB, 128), F32)
+    out = jax.ShapeDtypeStruct((n_rows, QB), F32)
+    pair = pltpu.VMEM((2, QB, LANES), F32)
+    part = (last - first) / n_blk
     return pl.pallas_call(
-        window_kernel, grid=(2, n_blk),
+        functools.partial(window_kernel, first=first, n_blk=n_blk), grid=(2, last - first),
         in_specs=[mid(0), left(1), mid(1), right(1), left(2), mid(2), right(2), halo(0), halo(0), halo(1), halo(1),
-                  whole(extra), whole(bias), pl.BlockSpec((1, 128), lambda p, i: (0, p))],
-        out_specs=[pl.BlockSpec((rb, 128), lambda p, i: (i, p))] * 3,
-        out_shape=[out, out, out],
-        scratch_shapes=[pltpu.VMEM((3 * QB, QB), F32), pltpu.VMEM((rb + 2 * QB, 128), BF16),
-                        pltpu.VMEM((rb + 2 * QB, 128), BF16), pair, pair, pair],
-        compiler_params=params(2), cost_estimate=cost(30e9, 30e6, 12e6), name="window_part",
-    )(qkv, qkv, qkv, qkv, qkv, qkv, qkv, halo_l, halo_r, halo_l, halo_r, extra, bias, kmax)
+                  whole(extra), whole(bias), pl.BlockSpec((1, LANES), lambda p, i: (0, p))]
+        + [pl.BlockSpec(memory_space=pl.ANY)] * len(win),
+        out_specs=[pl.BlockSpec((rb, LANES), lambda p, i: (first + i, p))] * 3,
+        out_shape=[out, out, out], input_output_aliases={14 + n: n for n in range(len(win))},
+        scratch_shapes=[pltpu.VMEM((3 * QB, QB), F32), pltpu.VMEM((rb + 2 * QB, LANES), BF16),
+                        pltpu.VMEM((rb + 2 * QB, LANES), BF16), pair, pair, pair],
+        compiler_params=params(2), cost_estimate=cost(30e9 * part, 30e6 * part, 12e6 * part), name="window_part",
+    )(qkv, qkv, qkv, qkv, qkv, qkv, qkv, halo_l, halo_r, halo_l, halo_r, extra, bias, kmax, *win)
+
+
+def global_keys_kernel(q_ref, kg_ref, vg_ref, kmax_ref, acc_ref, m_ref, l_ref, out_ref,
+                       k_ref, ea_ref, em_ref, el_ref):
+    n = q_ref.shape[0]
+    i = pl.program_id(1)
+
+    @pl.when(i == 0)
+    def _():
+        extra = key_extra(kg_ref.shape[0])
+        for half in range(2):
+            k_ref[half] = own_half(kg_ref[...], extra, half)
+
+    def finish(acc, m, total):
+        m_all = jnp.maximum(m, m_ref[...])
+        a, b = jnp.exp(m - m_all), jnp.exp(m_ref[...] - m_all)
+        out_ref[...] = ((acc * a + acc_ref[...] * b) / (total * a + l_ref[...] * b)).astype(out_ref.dtype)
+
+    q = q_ref[...]
+    neg = shifts(q, kmax_ref[...])
+    low = low_lanes(n)
+    res = [stream(query_rows(q, neg, half), [(k_ref[half, t:t + QB], vg_ref[t:t + QB]) for t in range(0, vg_ref.shape[0], QB)])
+           for half in range(2)]
+    sums = [row_sum(r[1]) for r in res]
+    finish(jnp.where(low, res[0][0], res[1][0]), -pltpu.roll(neg.astype(F32), HEAD, 1), jnp.where(low, sums[0], sums[1]))
+
+    @pl.when(out_of_range(*sums))
+    def _():
+        def key_rows(c):
+            at = pl.ds(pl.multiple_of(c * QB, QB), QB)
+            return kg_ref[at], vg_ref[at], None
+
+        exact_heads(q_ref[...], vg_ref.shape[0], key_rows, ea_ref, em_ref, el_ref)
+        finish(*(jnp.where(low, r[0], r[1]) for r in (ea_ref, em_ref, el_ref)))
+
+
+def global_keys_part(qkv, qkv_g, kmax, win, n_rows):
+    n_glob = qkv_g.shape[0]
+    rb = min(512, n_rows)
+    row = pl.BlockSpec((rb, LANES), lambda p, i: (i, p))
+    pair = pltpu.VMEM((2, rb, LANES), F32)
+    return pl.pallas_call(
+        global_keys_kernel, grid=(2, n_rows // rb),
+        in_specs=[row, pl.BlockSpec((n_glob, LANES), lambda p, i: (0, 2 + p)), pl.BlockSpec((n_glob, LANES), lambda p, i: (0, 4 + p)),
+                  pl.BlockSpec((1, LANES), lambda p, i: (0, p)), row, row, row],
+        out_specs=row, out_shape=jax.ShapeDtypeStruct((n_rows, QB), BF16),
+        scratch_shapes=[pltpu.VMEM((2, n_glob, LANES), BF16), pair, pair, pair],
+        compiler_params=params(2), cost_estimate=cost(10e9, 8e6, 4e6), name="global_keys",
+    )(qkv, qkv_g, qkv_g, kmax, *win)
 
 
 def global_queries_kernel(q_ref, k_ref, v_ref, kmax_ref, out_ref, acc_ref, m_ref, l_ref, *, kb):
@@ -257,11 +316,11 @@
         acc_ref[...] = jnp.zeros_like(acc_ref)
         l_ref[...] = jnp.zeros_like(l_ref)
 
-    extra = key_extra(256)
+    extra = key_extra(QB)
     q = q_ref[...]
     neg = shifts(q, kmax_ref[...])
     for half in range(2):
-        rows = [pl.ds(pl.multiple_of(j * kb, kb) + t, 256) for t in range(0, kb, 256)]
+        rows = [pl.ds(pl.multiple_of(j * kb, kb) + t, QB) for t in range(0, kb, QB)]
         acc, total = stream(query_rows(q, neg, half), [(own_half(k_ref[r], extra, half), v_ref[r]) for r in rows])
         acc_ref[half] += acc
         l_ref[half] += total
@@ -270,17 +329,16 @@
     def _():
         sums = [row_sum(l_ref[half]) for half in range(2)]
         out_ref[0] = jnp.where(low, acc_ref[0], acc_ref[1])
-        out_ref[1] = -pltpu.roll(neg.astype(F32), 64, 1)
+        out_ref[1] = -pltpu.roll(neg.astype(F32), HEAD, 1)
         out_ref[2] = jnp.where(low, sums[0], sums[1])
 
         @pl.when(out_of_range(*sums))
         def _():
             def key_rows(c):
-                at = pl.ds(pl.multiple_of(c * 256, 256), 256)
+                at = pl.ds(pl.multiple_of(c * QB, QB), QB)
                 return k_ref[at], v_ref[at], None
 
-            for half in range(2):
-                exact_head(q_ref[...], half, v_ref.shape[0], key_rows, acc_ref, m_ref, l_ref)
+            exact_heads(q_ref[...], v_ref.shape[0], key_rows, acc_ref, m_ref, l_ref)
             for k, r in enumerate((acc_ref, m_ref, l_ref)):
                 out_ref[k] = jnp.where(low, r[0], r[1])
 
@@ -292,21 +350,22 @@
     kb = min(1024, n_rows)
     return pl.pallas_call(
         functools.partial(global_queries_kernel, kb=kb), grid=(2, n_glob // rb, n_rows // kb),
-        in_specs=[pl.BlockSpec((rb, 128), lambda p, i, j: (i, p)), pl.BlockSpec((n_rows, 128), lambda p, i, j: (0, 2 + p)),
-                  pl.BlockSpec((n_rows, 128), lambda p, i, j: (0, 4 + p)), pl.BlockSpec((1, 128), lambda p, i, j: (0, p))],
-        out_specs=pl.BlockSpec((3, rb, 128), lambda p, i, j: (0, i, p)),
-        out_shape=jax.ShapeDtypeStruct((3, n_glob, 256), F32),
-        scratch_shapes=[pltpu.VMEM((2, rb, 128), F32)] * 3,
+        in_specs=[pl.BlockSpec((rb, LANES), lambda p, i, j: (i, p)), pl.BlockSpec((n_rows, LANES), lambda p, i, j: (0, 2 + p)),
+                  pl.BlockSpec((n_rows, LANES), lambda p, i, j: (0, 4 + p)), pl.BlockSpec((1, LANES), lambda p, i, j: (0, p))],
+        out_specs=pl.BlockSpec((3, rb, LANES), lambda p, i, j: (0, i, p)),
+        out_shape=jax.ShapeDtypeStruct((3, n_glob, QB), F32),
+        scratch_shapes=[pltpu.VMEM((2, rb, LANES), F32)] * 3,
         compiler_params=params(3), cost_estimate=cost(34e9, 20e6, 16e6), name="global_queries",
     )(qkv_g, qkv, qkv, kmax)
 
 
-def exchange_mlp_kernel(x_hbm, w_hbm, qkv_hbm, qkvg_hbm, acc_hbm, m_hbm, l_hbm, glob_hbm, idx_ref, y_hbm,
+def exchange_mlp_kernel(x_hbm, w_hbm, qkv_hbm, qkvg_hbm, acc_hbm, m_hbm, l_hbm, glob_hbm, idx_ref, pre_ref, y_hbm,
                         x_ref, o_ref, wo_ref, w2_ref, w1_ref, q_ref, kg_ref, glob_ref, win_ref, load_sem, win_sem, y_sem,
                         up_send, up_recv, down_send, down_recv, *, n_tp, n_rep, d_o, d_f, rb):
     me = lax.axis_index('tp')
     n_blk = x_ref.shape[0] // rb
     width = n_tp * d_f
+    qb = min(QB, rb)
 
     barrier = pltpu.get_barrier_semaphore()
 
@@ -318,8 +377,8 @@
     def _():
         pl.semaphore_signal(barrier, inc=1, device_id={'tp': me + 1}, device_id_type=pl.DeviceIdType.MESH)
 
-    early = [pltpu.make_async_copy(qkv_hbm.at[:, pl.ds(0, 256)], q_ref, load_sem.at[0]),
-             pltpu.make_async_copy(qkvg_hbm.at[:, pl.ds(256, 512)], kg_ref, load_sem.at[1]),
+    early = [pltpu.make_async_copy(qkv_hbm.at[:, pl.ds(0, QB)], q_ref, load_sem.at[0]),
+             pltpu.make_async_copy(qkvg_hbm.at[:, pl.ds(QB, 512)], kg_ref, load_sem.at[1]),
              pltpu.make_async_copy(glob_hbm, glob_ref, load_sem.at[2])]
 
     def rows_of(b):
@@ -329,7 +388,7 @@
         return [pltpu.make_async_copy(h.at[rows_of(b)], win_ref.at[b % 2, n], win_sem.at[b % 2, n])
                 for n, h in enumerate((acc_hbm, m_hbm, l_hbm))]
 
-    for c in early + fetch(0):
+    for c in early + fetch(2):
         c.start()
     copies = [pltpu.make_async_copy(x_hbm, x_ref, load_sem.at[3])]
     piece = wo_ref.shape[1] // n_rep
@@ -364,14 +423,14 @@
         for c in fetch(b):
             c.wait()
 
-        @pl.loop(0, rb // QB)
+        @pl.loop(0, rb // qb)
         def _(r):
-            at = pl.ds(pl.multiple_of(r * QB, QB), QB)
-            rows = pl.ds(pl.multiple_of(b * rb + r * QB, QB), QB)
-            low = low_lanes(QB)
+            at = pl.ds(pl.multiple_of(r * qb, qb), qb)
+            rows = pl.ds(pl.multiple_of(b * rb + r * qb, qb), qb)
+            low = low_lanes(qb)
             parts = []
             for pr in range(2):
-                cols = slice(pr * 128, pr * 128 + 128)
+                cols = slice(pr * LANES, pr * LANES + LANES)
                 q = q_ref[rows, cols]
                 zero = jnp.zeros_like(q)
                 q2 = jnp.concatenate([jnp.where(low, q, zero), jnp.where(low, zero, q)], axis=0)
@@ -379,17 +438,19 @@
                 top = jnp.max(sc, axis=1, keepdims=True)
                 e = jnp.exp(sc - top)
                 total = row_sum(e)
-                acc = dot_nn(e.astype(BF16), kg_ref[:, 256 + pr * 128:256 + pr * 128 + 128])
-                acc, m, total = (jnp.where(low, v[:QB], v[QB:]) for v in (acc, top, total))
+                acc = dot_nn(e.astype(BF16), kg_ref[:, QB + pr * LANES:QB + pr * LANES + LANES])
+                acc, m, total = (jnp.where(low, v[:qb], v[qb:]) for v in (acc, top, total))
                 acc_w, m_w, l_w = (win_ref[b % 2, n, at, cols] for n in range(3))
                 m_all = jnp.maximum(m, m_w)
                 f, f_w = jnp.exp(m - m_all), jnp.exp(m_w - m_all)
                 parts.append((acc * f + acc_w * f_w) / (total * f + l_w * f_w))
-            row = b * rb + r * QB + lax.broadcasted_iota(jnp.int32, (QB, 1), 0)
-            hit = jnp.where(idx_ref[...] == row, 1.0, 0.0)
-            placed = dot_nn(hit.astype(BF16), glob_ref[...])
-            mine = row_sum(hit) > 0.5
-            o_ref[me, rows] = jnp.where(mine, placed, jnp.concatenate(parts, axis=1)).astype(BF16)
+            place(rows, b * rb + r * qb, jnp.concatenate(parts, axis=1))
+
+    def place(rows, row0, o):
+        row = row0 + lax.broadcasted_iota(jnp.int32, (o.shape[0], 1), 0)
+        hit = jnp.where(idx_ref[...] == row, 1.0, 0.0)
+        placed = dot_nn(hit.astype(BF16), glob_ref[...])
+        o_ref[me, rows] = jnp.where(row_sum(hit) > 0.5, placed, o).astype(BF16)
 
     def up(d, b):
         at = o_ref.at[me - d, rows_of(b)]
@@ -415,8 +476,8 @@
         def _():
             down(0, b).start()
 
-    attend(0)
-    attend(1)
+    for b in range(2):
+        place(pl.ds(b * rb, rb), b * rb, pre_ref[b * rb:(b + 1) * rb, :].astype(F32))
     send_own(0)
 
     def step(s, carry):
@@ -490,17 +551,17 @@
     lax.fori_loop(0, n_blk, finish, 0)
 
 
-def exchange_mlp(tokens, w_all, qkv, qkv_g, win, glob_out, local_idx, n_tp, d_o, d_f):
+def exchange_mlp(tokens, w_all, qkv, qkv_g, win, o_pre, glob_out, local_idx, n_tp, d_o, d_f):
     n_rows, dim = tokens.shape
     n_glob = local_idx.shape[0]
     n_rep = w_all.shape[0]
-    rb = min(512, n_rows // 2)
+    rb = n_rows // 8
     n_blk = n_rows // rb
     anywhere = pl.BlockSpec(memory_space=pl.ANY)
     dma = pltpu.SemaphoreType.DMA
     return pl.pallas_call(
         functools.partial(exchange_mlp_kernel, n_tp=n_tp, n_rep=n_rep, d_o=d_o, d_f=d_f, rb=rb),
-        in_specs=[anywhere] * 8 + [pl.BlockSpec(memory_space=pltpu.VMEM)], out_specs=anywhere,
+        in_specs=[anywhere] * 8 + [pl.BlockSpec(memory_space=pltpu.VMEM)] * 2, out_specs=anywhere,
         out_shape=jax.ShapeDtypeStruct(tokens.shape, BF16),
         scratch_shapes=[pltpu.VMEM((n_rows, dim), BF16), pltpu.VMEM((n_tp, n_rows, d_o), BF16),
                         pltpu.VMEM((n_tp * d_o, dim), BF16), pltpu.VMEM((n_tp * d_f, dim), BF16),
@@ -510,7 +571,7 @@
                         dma((n_tp - 1, n_blk)), dma((n_tp - 1, n_blk)), dma((n_tp - 1, n_blk)), dma((n_tp - 1, n_blk))],
         compiler_params=pltpu.CompilerParams(collective_id=1, has_side_effects=True, vmem_limit_bytes=60 << 20),
         cost_estimate=cost(2 * n_rows * dim * (dim + 2 * n_tp * d_f), 40e6), name="exchange_mlp",
-    )(tokens, w_all, qkv, qkv_g, *win, glob_out, local_idx[None, :])
+    )(tokens, w_all, qkv, qkv_g, *win, glob_out, local_idx[None, :], o_pre)
 
 
 def copy_kernel(a_ref, b_ref):
@@ -518,9 +579,9 @@
 
 
 def streamed(a):
-    rb = a.shape[0] // 4
+    rb = a.shape[0] // 16
     spec = pl.BlockSpec((rb, a.shape[1]), lambda i: (i, 0))
-    return pl.pallas_call(copy_kernel, grid=(4,), in_specs=[spec], out_specs=spec,
+    return pl.pallas_call(copy_kernel, grid=(16,), in_specs=[spec], out_specs=spec,
                           out_shape=jax.ShapeDtypeStruct(a.shape, a.dtype),
                           compiler_params=params(1), name="result")(a)
 
@@ -559,13 +620,13 @@
         w_cat = jnp.concatenate([w_query.reshape(dim, -1) * jnp.asarray(0.125, BF16),
                                  w_key.reshape(dim, -1), w_value.reshape(dim, -1)], axis=1)
         qkv, picked, kmax = qkv_part(tokens, w_cat, local_idx)
-        halo_l = lax.ppermute(qkv[n_rows - WIN:, 256:], 'sp', to_right)
-        halo_r = lax.ppermute(qkv[:WIN, 256:], 'sp', to_left)
+        halo_l = lax.ppermute(qkv[n_rows - WIN:, QB:], 'sp', to_right)
+        halo_r = lax.ppermute(qkv[:WIN, QB:], 'sp', to_left)
 
         k_pos = first_row - WIN + jnp.arange(n_rows + 2 * WIN)
         k_off = jnp.any(glob_pos[:, None] == k_pos[None, :], axis=0) | (k_pos < 0) | (k_pos >= seq_len)
         bias = jnp.where(k_off, -jnp.inf, 0.0).astype(F32)[None, :]
-        lane = jnp.arange(128) % 64
+        lane = jnp.arange(LANES) % HEAD
         extra = jnp.where(lane == 0, 1.0, jnp.where((lane == 1) & k_off[:, None], FLOOR, 0.0)).astype(BF16)
 
         half = n_glob // 2
@@ -573,19 +634,22 @@
         other = lax.ppermute(lax.dynamic_slice_in_dim(picked, (1 - core) * half, half), 'sp', core_swap)
         mine = mine + other
         got = lax.ppermute(mine, 'sp', chip_swap)
+        win = window_part(qkv, halo_l, halo_r, extra, bias, kmax, 0, 3)
+        got, win = lax.optimization_barrier((got, win))
         mine = mine + got
         other = lax.ppermute(mine, 'sp', core_swap)
         qkv_g = jnp.concatenate([jnp.where(core == 0, mine, other), jnp.where(core == 0, other, mine)], axis=0)
 
         part = global_queries_part(qkv_g, qkv, kmax)
-        part, kmax = lax.optimization_barrier((part, kmax))
 
         quarter = n_glob // 4
         got = lax.ppermute(lax.dynamic_slice_in_dim(part, (1 - core) * half, half, axis=1), 'sp', core_swap)
         joined = jnp.stack(combine(lax.dynamic_slice_in_dim(part, core * half, half, axis=1), got))
+        joined, kmax = lax.optimization_barrier((joined, kmax))
         got = lax.ppermute(lax.dynamic_slice_in_dim(joined, (1 - chip) * quarter, quarter, axis=1), 'sp', chip_swap)
-        win = window_part(qkv, halo_l, halo_r, extra, bias, kmax)
-        got, win = lax.optimization_barrier((got, win))
+        win = window_part(qkv, halo_l, halo_r, extra, bias, kmax, 3, 4, win)
+        o_pre = global_keys_part(qkv, qkv_g, kmax, win, n_rows // 4)
+        got, win, o_pre = lax.optimization_barrier((got, win, o_pre))
         g_acc, _, g_l = combine(lax.dynamic_slice_in_dim(joined, chip * quarter, quarter, axis=1), got)
         mine = (g_acc / g_l).astype(BF16)
         other = lax.ppermute(mine, 'sp', chip_swap)
@@ -593,7 +657,7 @@
         other = lax.ppermute(mine, 'sp', core_swap)
         glob_out = jnp.concatenate([jnp.where(core == 0, mine, other), jnp.where(core == 0, other, mine)], axis=0)
 
-        return streamed(exchange_mlp(tokens, w_all, qkv, qkv_g, win, glob_out, local_idx, n_tp, d_o, d_f))
+        return streamed(exchange_mlp(tokens, w_all, qkv, qkv_g, win, o_pre, glob_out, local_idx, n_tp, d_o, d_f))
 
     row_spec = P(('dp', 'sp'), None)
     head_spec = P(None, 'tp', None)

time: 532 us -> 562 us (1.056)
  Pallas kernels: 463 us -> 498 us
  waiting for transfers between devices: 27.8 us -> 10.2 us
    pallas_call x2 -> x4, Pallas kernels: 143 us -> 188 us  [the longest x2 141 us: window_part(): pl.pallas_call(functools.partial(window_kernel, first=first, n_blk=n_blk)...]
    ppermute x1, waiting for transfers between devices: 18.2 us -> 0.01 us  [device_layer(): got = lax.ppermute(mine, 'sp', chip_swap)]
    pallas_call x1, Pallas kernels: 168 us -> 156 us  [exchange_mlp(): pl.pallas_call(functools.partial(exchange_mlp_kernel, n_tp=n_tp, n_rep=n_...]
  transfers between devices with their start and end apart: 10 -> 10, of which waited for: 5 -> 4; matrix products, arithmetic and copies ran while one was open for 2% -> 4% of each run, Pallas kernels for 54% -> 59%
where the time goes in v5:
time: 562 us; the launch traced here: 561 us
  Pallas kernels  498 us (89%)
  other arithmetic  15.4 us (3%)
  starting transfers between devices  14.6 us (3%)
  between operations  13.6 us (2%)
  waiting for transfers between devices  10.2 us (2%)
  local copies, waits for them, and re-layouts  9.33 us (2%)
    pallas_call x1, Pallas kernels, exchange_mlp(): pl.pallas_call(functools.partial(exchange_mlp_kernel, n_tp=n_tp, n_rep=n_...  156 us
    pallas_call x2, Pallas kernels, window_part(): pl.pallas_call(functools.partial(window_kernel, first=first, n_blk=n_blk)...  141 us
    pallas_call x1, Pallas kernels, global_queries_part(): pl.pallas_call(functools.partial(global_queries_kernel, kb=kb), grid=(2,...  137 us
    pallas_call x1, Pallas kernels, global_keys_part(): pl.pallas_call(global_keys_kernel, grid=(2, n_rows // rb), in_specs=[row,...  36 us
    pallas_call x1, Pallas kernels, qkv_part(): pl.pallas_call(qkv_kernel, grid_spec=pltpu.PrefetchScalarGridSpec(num_sca...  17.2 us
    pallas_call x1, Pallas kernels, streamed(): pl.pallas_call(copy_kernel, grid=(16,), in_specs=[spec], out_specs=spec,...  11.9 us
  transfers between devices with their start and end apart: 10, of which 4 were waited for; matrix products, arithmetic and copies ran while one was open for 4% of the time, Pallas kernels for 59%

profile of v5, /device:TPU:0, one launch (start us, length us, event | category | flops | bytes accessed | tf_op | source)
XLA Modules:
  0.0 561.4 jit_solution(3869614294622768478)
XLA Ops:
  6.5 1.9 fusion.3
  8.4 0.0 all-gather.3.cloned.1.call-update
  8.5 1.0 copy.22.idx_ref
  9.6 0.2 copy.19
  9.8 0.2 copy.20
  10.0 0.2 copy.21
  10.2 1.3 pad_maximum_fusion.w_ref
  11.5 17.2 %qkv.1 = (bf16[4096,768]{1,0:T(8,128)(2,1)}, bf16[1024,768]{1,0:T(8,128)(2,1)}, f32[1,256]{1,0:T(1,128)}) custom-call(s32[1024]{0:T(1024)} %copy-done.7, s32[1024,1]{1,0:T(8,128)} %copy.22.idx_ref, bf16[4096,1024]{1,0:T(8,128)(2,1)} %x_hbm.1, bf16[1024,768]{1,0:T(8,128)(2,1)} %pad_maximum_fusion.w_ref), custom_call_target="tpu_custom_call" | custom-call | flops 8000000000 | bytes 24000000 | tf_op jit(solution)/shard_map/qkv/pallas_call | solution.py:81
  28.7 2.2 constant_dynamic-slice_fusion.2
  30.9 0.2 collective-permute-start
  31.1 1.8 fusion.12
  32.9 2.2 collective-permute-start.2
  35.1 1.3 collective-permute-start.3
  36.4 2.5 compare_reduce_fusion
  38.9 3.3 select_convert_fusion.extra_ref
  42.2 0.7 or_select_fusion.bias_ref
  42.9 0.0 collective-permute-done
  42.9 0.2 dynamic-slice_add_fusion
  43.1 4.9 collective-permute-start.1
  48.0 0.0 collective-permute-done.2.hkl_ref.hvl_ref
  48.1 0.7 copy-done.2
  48.7 0.1 copy-done.3
  48.8 104.2 %window_part.2 = (f32[4096,256]{1,0:T(8,128)}, f32[4096,256]{1,0:T(8,128)}, f32[4096,256]{1,0:T(8,128)}) custom-call(bf16[4096,768]{1,0:T(8,128)(2,1)} %get-tuple-element.25.q_ref.kl_ref.kc_ref.kr_ref.vl_ref.vc_ref.vr_ref.k_ref.v_ref.qkv_hbm, bf16[4096,768]{1,0:T(8,128)(2,1)} %get-tuple-element.25.q_ref.kl_ref.kc_ref.kr_ref.vl_ref.vc_ref.vr_ref.k_ref.v_ref.qkv_hbm, ...), custom_call_target="tpu_custom_call" | custom-call | flops 22499999744 | bytes 22500000 | tf_op jit(solution)/shard_map/window_part/pallas_call | solution.py:247
  153.0 0.2 add.93
  153.2 3.4 collective-permute-start.4
  156.6 1.9 collective-permute-done.4
  158.5 0.1 broadcast_select_fusion.1
  158.7 1.3 pad_maximum_fusion.1.q_ref.kg_ref.vg_ref.qkvg_hbm
  159.9 136.9 %global_queries.1 = f32[3,1024,256]{2,1,0:T(8,128)} custom-call(bf16[1024,768]{1,0:T(8,128)(2,1)} %pad_maximum_fusion.1.q_ref.kg_ref.vg_ref.qkvg_hbm, bf16[4096,768]{1,0:T(8,128)(2,1)} %get-tuple-element.25.q_ref.kl_ref.kc_ref.kr_ref.vl_ref.vc_ref.vr_ref.k_ref.v_ref.qkv_hbm, ...), custom_call_target="tpu_custom_call" | custom-call | flops 33999998976 | bytes 20000000 | tf_op jit(solution)/shard_map/global_queries/pallas_call | solution.py:351
  296.9 2.8 constant_dynamic-slice_fusion.1
  299.7 0.4 collective-permute-start.5
  300.1 3.0 collective-permute-done.5
  303.1 1.4 fusion.1
  304.5 1.4 fusion
  305.9 0.1 pad_maximum_fusion.2
  306.0 0.1 constant_dynamic-slice_fusion
  306.1 0.1 collective-permute-start.6
  306.2 36.5 %window_part.3 = (f32[4096,256]{1,0:T(8,128)}, f32[4096,256]{1,0:T(8,128)}, f32[4096,256]{1,0:T(8,128)}) custom-call(bf16[4096,768]{1,0:T(8,128)(2,1)} %get-tuple-element.25.q_ref.kl_ref.kc_ref.kr_ref.vl_ref.vc_ref.vr_ref.k_ref.v_ref.qkv_hbm, ...), custom_call_target="tpu_custom_call", output_to_operand_aliasing={{0}: (14, {}), {1}: (15, {}), {2}: (16, {})} | custom-call | flops 7500000256 | bytes 7500000 | tf_op jit(solution)/shard_map/window_part/pallas_call | solution.py:247
  342.6 36.0 %global_keys.1.pre_ref = bf16[1024,256]{1,0:T(8,128)(2,1)} custom-call(bf16[4096,768]{1,0:T(8,128)(2,1)} %get-tuple-element.25.q_ref.kl_ref.kc_ref.kr_ref.vl_ref.vc_ref.vr_ref.k_ref.v_ref.qkv_hbm, bf16[1024,768]{1,0:T(8,128)(2,1)} %pad_maximum_fusion.1.q_ref.kg_ref.vg_ref.qkvg_hbm, bf16[1024,768]{1,0:T(8,128)(2,1)} %pad_maximum_fusion.1.q_ref.kg_ref.vg_ref.qkvg_hbm, ...), custom_call_target="tpu_custom_call" | custom-call | flops 10000000000 | bytes 8000000 | tf_op jit(solution)/shard_map/global_keys/pallas_call | solution.py:299
  378.6 0.1 fusion.11
  378.8 2.1 collective-permute-start.7
  380.8 3.7 collective-permute-done.7
  384.6 0.1 collective-permute-start.8
  384.7 1.5 collective-permute-done.8
  386.2 0.1 broadcast_select_fusion.3
  386.3 0.8 pad_maximum_fusion.3.glob_hbm
  387.1 155.6 %exchange_mlp.1.a_ref = bf16[4096,1024]{1,0:T(8,128)(2,1)} custom-call(bf16[4096,1024]{1,0:T(8,128)(2,1)} %x_hbm.1, bf16[8,4,1568,128]{3,2,1,0:T(8,128)(2,1)} %bitcast.57, bf16[4096,768]{1,0:T(8,128)(2,1)} %get-tuple-element.25.q_ref.kl_ref.kc_ref.kr_ref.vl_ref.vc_ref.vr_ref.k_ref.v_ref.qkv_hbm, ...), custom_call_target="tpu_custom_call" | custom-call | flops 52613349376 | bytes 40000000 | tf_op jit(solution)/shard_map/exchange_mlp/pallas_call | solution.py:562
  542.7 11.9 %result.1 = bf16[4096,1024]{1,0:T(8,128)(2,1)} custom-call(bf16[4096,1024]{1,0:T(8,128)(2,1)} %exchange_mlp.1.a_ref), custom_call_target="tpu_custom_call" | custom-call | tf_op jit(solution)/shard_map/result/pallas_call | solution.py:584
  (28 shorter events, 0.2 us)
Async XLA Ops:
  6.5 1.9 copy-start.8
  6.5 3.0 copy-start.4
  6.5 380.6 %all-gather.3.cloned.1.call-start = ((), (), s32[]{:S(2)}) async-start(), calls=%async_computation | async-start | bytes 13246464 | tf_op jit(solution)/shard_map/all_gather | solution.py:617
  8.4 1.4 copy-start.5
  8.4 1.6 copy-start.6
  8.5 1.7 copy-start.7
  28.7 14.2 %copy-start.1 = (bf16[1024,768]{1,0:T(8,128)(2,1)S(1)}, bf16[1024,768]{1,0:T(8,128)(2,1)}, u32[]{:S(2)}) copy-start(bf16[1024,768]{1,0:T(8,128)(2,1)} %get-tuple-element.26) | copy-start | bytes 4718596
  30.9 12.0 %collective-permute-start = (bf16[512,768]{1,0:T(8,128)(2,1)}, bf16[512,768]{1,0:T(8,128)(2,1)S(1)}, u32[]{:S(2)}, u32[]{:S(2)}) collective-permute-start(bf16[512,768]{1,0:T(8,128)(2,1)} %constant_dynamic-slice_fusion.2), channel_id=1, source_target_pairs={{0,1},{1,0},{2,3},{3,2},{4,5},{5,4},{6,7},{7,6},{8,9},{9,8},{10,11... | collective-permute-start | bytes 2359304 | tf_op jit(solution)/shard_map/ppermute | solution.py:634
  32.9 15.2 %collective-permute-start.2 = (bf16[256,512]{1,0:T(8,128)(2,1)}, bf16[256,512]{1,0:T(8,128)(2,1)S(1)}, u32[]{:S(2)}, u32[]{:S(2)}) collective-permute-start(bf16[256,512]{1,0:T(8,128)(2,1)} %get-tuple-element.48), channel_id=1, source_target_pairs={{0,1},{1,2},{2,3},{4,5},{5,6},{6,7},{8,9},{9,10},{10,11},{12,13},{... | collective-permute-start | bytes 786440 | tf_op jit(solution)/shard_map/ppermute | solution.py:623
  35.1 13.0 %collective-permute-start.3 = (bf16[256,512]{1,0:T(8,128)(2,1)S(1)}, bf16[256,512]{1,0:T(8,128)(2,1)S(1)}, u32[]{:S(2)}, u32[]{:S(2)}) collective-permute-start(bf16[256,512]{1,0:T(8,128)(2,1)S(1)} %get-tuple-element.47), channel_id=1, source_target_pairs={{1,0},{2,1},{3,2},{5,4},{6,5},{7,6},{9,8},{10,9},{11,10},{13,12},{... | collective-permute-start | bytes 786440 | tf_op jit(solution)/shard_map/ppermute | solution.py:624
  43.1 109.9 %collective-permute-start.1 = (bf16[512,768]{1,0:T(8,128)(2,1)S(1)}, bf16[512,768]{1,0:T(8,128)(2,1)S(1)}, u32[]{:S(2)}, u32[]{:S(2)}) collective-permute-start(bf16[512,768]{1,0:T(8,128)(2,1)S(1)} %dynamic-slice_add_fusion), channel_id=1, source_target_pairs={{0,2},{1,3},{2,0},{3,1},{4,6},{5,7},{6,4},{7,5},{8,10},{9,11},{10,... | collective-permute-start | bytes 2359304 | tf_op jit(solution)/shard_map/ppermute | solution.py:636
  48.0 0.7 copy-start.2
  48.0 0.8 copy-start.3
  153.2 5.3 collective-permute-start.4
  296.9 6.3 %copy-start = (f32[3,1024,256]{2,1,0:T(8,128)S(1)}, f32[3,1024,256]{2,1,0:T(8,128)}, u32[]{:S(2)}) copy-start(f32[3,1024,256]{2,1,0:T(8,128)} %global_queries.1) | copy-start | bytes 9437188
  299.7 3.4 collective-permute-start.5
  306.1 72.5 %collective-permute-start.6 = (f32[3,256,256]{2,1,0:T(8,128)S(1)}, f32[3,256,256]{2,1,0:T(8,128)S(1)}, u32[]{:S(2)}, u32[]{:S(2)}) collective-permute-start(f32[3,256,256]{2,1,0:T(8,128)S(1)} %constant_dynamic-slice_fusion), channel_id=1, source_target_pairs={{0,2},{1,3},{2,0},{3,1},{4,6},{5,7},{6,4},{7,5},{8,10},{9,11},{10,... | collective-permute-start | bytes 2359304 | tf_op jit(solution)/shard_map/ppermute | solution.py:649
  378.8 5.8 %collective-permute-start.7 = (bf16[256,256]{1,0:T(8,128)(2,1)S(1)}, bf16[256,256]{1,0:T(8,128)(2,1)S(1)}, u32[]{:S(2)}, u32[]{:S(2)}) collective-permute-start(bf16[256,256]{1,0:T(8,128)(2,1)S(1)} %fusion.11), channel_id=1, source_target_pairs={{0,2},{1,3},{2,0},{3,1},{4,6},{5,7},{6,4},{7,5},{8,10},{9,11},{10,... | collective-permute-start | bytes 393224 | tf_op jit(solution)/shard_map/ppermute | solution.py:655
  384.6 1.6 collective-permute-start.8
Sparse Core Ops, SparseCore 0:
  10.2 99.6 all-gather.2

commit v6 on v5

--- a/solution.py
+++ b/solution.py
@@ -26,7 +26,7 @@
     return jnp.dot(a, b, preferred_element_type=F32)
 
 
-def params(n_axes, vmem_mib=60):
+def params(n_axes, vmem_mib=48):
     return pltpu.CompilerParams(
         dimension_semantics=("arbitrary",) * n_axes, vmem_limit_bytes=vmem_mib << 20)
 
@@ -253,7 +253,7 @@
         out_shape=[out, out, out], input_output_aliases={14 + n: n for n in range(len(win))},
         scratch_shapes=[pltpu.VMEM((3 * QB, QB), F32), pltpu.VMEM((rb + 2 * QB, LANES), BF16),
                         pltpu.VMEM((rb + 2 * QB, LANES), BF16), pair, pair, pair],
-        compiler_params=params(2), cost_estimate=cost(30e9 * part, 30e6 * part, 12e6 * part), name="window_part",
+        compiler_params=params(2, 60), cost_estimate=cost(30e9 * part, 30e6 * part, 12e6 * part), name="window_part",
     )(qkv, qkv, qkv, qkv, qkv, qkv, qkv, halo_l, halo_r, halo_l, halo_r, extra, bias, kmax, *win)
 
 
@@ -574,16 +574,28 @@
     )(tokens, w_all, qkv, qkv_g, *win, glob_out, local_idx[None, :], o_pre)
 
 
-def copy_kernel(a_ref, b_ref):
-    b_ref[...] = a_ref[...]
+def copy_kernel(a_hbm, b_hbm, buf_ref, in_sem, out_sem):
+    n, rows = buf_ref.shape[:2]
+    at = [pl.ds(i * rows, rows) for i in range(n)]
+    loads = [pltpu.make_async_copy(a_hbm.at[r], buf_ref.at[i], in_sem.at[i]) for i, r in enumerate(at)]
+    stores = [pltpu.make_async_copy(buf_ref.at[i], b_hbm.at[r], out_sem.at[i]) for i, r in enumerate(at)]
+    for c in loads:
+        c.start()
+    for load, store in zip(loads, stores):
+        load.wait()
+        store.start()
+    for c in stores:
+        c.wait()
 
 
 def streamed(a):
-    rb = a.shape[0] // 16
-    spec = pl.BlockSpec((rb, a.shape[1]), lambda i: (i, 0))
-    return pl.pallas_call(copy_kernel, grid=(16,), in_specs=[spec], out_specs=spec,
+    n = 8
+    anywhere = pl.BlockSpec(memory_space=pl.ANY)
+    dma = pltpu.SemaphoreType.DMA
+    return pl.pallas_call(copy_kernel, in_specs=[anywhere], out_specs=anywhere,
                           out_shape=jax.ShapeDtypeStruct(a.shape, a.dtype),
-                          compiler_params=params(1), name="result")(a)
+                          scratch_shapes=[pltpu.VMEM((n, a.shape[0] // n, a.shape[1]), a.dtype), dma((n,)), dma((n,))],
+                          compiler_params=pltpu.CompilerParams(vmem_limit_bytes=params(0).vmem_limit_bytes), name="result")(a)
 
 
 def combine(a, b):
@@ -623,16 +635,16 @@
         halo_l = lax.ppermute(qkv[n_rows - WIN:, QB:], 'sp', to_right)
         halo_r = lax.ppermute(qkv[:WIN, QB:], 'sp', to_left)
 
-        k_pos = first_row - WIN + jnp.arange(n_rows + 2 * WIN)
-        k_off = jnp.any(glob_pos[:, None] == k_pos[None, :], axis=0) | (k_pos < 0) | (k_pos >= seq_len)
-        bias = jnp.where(k_off, -jnp.inf, 0.0).astype(F32)[None, :]
-        lane = jnp.arange(LANES) % HEAD
-        extra = jnp.where(lane == 0, 1.0, jnp.where((lane == 1) & k_off[:, None], FLOOR, 0.0)).astype(BF16)
-
         half = n_glob // 2
         mine = lax.dynamic_slice_in_dim(picked, core * half, half)
         other = lax.ppermute(lax.dynamic_slice_in_dim(picked, (1 - core) * half, half), 'sp', core_swap)
         mine = mine + other
+        mine, flag_pos = lax.optimization_barrier((mine, glob_pos))
+        k_pos = first_row - WIN + jnp.arange(n_rows + 2 * WIN)
+        k_off = jnp.any(flag_pos[:, None] == k_pos[None, :], axis=0) | (k_pos < 0) | (k_pos >= seq_len)
+        bias = jnp.where(k_off, -jnp.inf, 0.0).astype(F32)[None, :]
+        lane = jnp.arange(LANES) % HEAD
+        extra = jnp.where(lane == 0, 1.0, jnp.where((lane == 1) & k_off[:, None], FLOOR, 0.0)).astype(BF16)
         got = lax.ppermute(mine, 'sp', chip_swap)
         win = window_part(qkv, halo_l, halo_r, extra, bias, kmax, 0, 3)
         got, win = lax.optimization_barrier((got, win))

time: 562 us -> 549 us (0.977)
  Pallas kernels: 498 us -> 490 us
  transfers between devices with their start and end apart: 10 -> 10, of which waited for: 4 -> 4; matrix products, arithmetic and copies ran while one was open for 4% -> 3% of each run, Pallas kernels for 59% -> 60%
where the time goes in v6:
time: 549 us; the launch traced here: 548 us
  Pallas kernels  490 us (89%)
  other arithmetic  15.3 us (3%)
  between operations  13.8 us (3%)
  starting transfers between devices  11 us (2%)
  waiting for transfers between devices  10.7 us (2%)
  local copies, waits for them, and re-layouts  7.3 us (1%)
    pallas_call x1, Pallas kernels, exchange_mlp(): pl.pallas_call(functools.partial(exchange_mlp_kernel, n_tp=n_tp, n_rep=n_...  155 us
    pallas_call x2, Pallas kernels, window_part(): pl.pallas_call(functools.partial(window_kernel, first=first, n_blk=n_blk)...  141 us
    pallas_call x1, Pallas kernels, global_queries_part(): pl.pallas_call(functools.partial(global_queries_kernel, kb=kb), grid=(2,...  137 us
    pallas_call x1, Pallas kernels, global_keys_part(): pl.pallas_call(global_keys_kernel, grid=(2, n_rows // rb), in_specs=[row,...  35.3 us
    pallas_call x1, Pallas kernels, qkv_part(): pl.pallas_call(qkv_kernel, grid_spec=pltpu.PrefetchScalarGridSpec(num_sca...  15.9 us
  transfers between devices with their start and end apart: 10, of which 4 were waited for; matrix products, arithmetic and copies ran while one was open for 3% of the time, Pallas kernels for 60%

profile of v6, /device:TPU:0, one launch (start us, length us, event | category | flops | bytes accessed | tf_op | source)
XLA Modules:
  0.0 548.2 jit_solution(6639224212149127156)
XLA Ops:
  6.5 1.9 fusion.3
  8.5 0.2 copy.22.idx_ref
  8.8 0.2 copy.19
  9.0 0.5 copy-done.10
  9.4 0.2 copy.20
  9.7 0.2 copy.21
  9.9 0.1 pad_maximum_fusion.w_ref
  10.0 15.9 %qkv.1 = (bf16[4096,768]{1,0:T(8,128)(2,1)}, bf16[1024,768]{1,0:T(8,128)(2,1)S(1)}, f32[1,256]{1,0:T(1,128)S(1)}) custom-call(s32[1024]{0:T(1024)S(1)} %broadcast_subtract_fusion.pos_ref, s32[1024,1]{1,0:T(8,128)S(1)} %copy.22.idx_ref, bf16[4096,1024]{1,0:T(8,128)(2,1)} %x_hbm.1, bf16[1024,768]{1,0:T(8,128)(2,1)S(1)} %pad_maximum_fusion.w_ref), custom_call_target="tpu_custom_call" | custom-call | flops 8000000000 | bytes 24000000 | tf_op jit(solution)/shard_map/qkv/pallas_call | solution.py:81
  25.8 0.5 copy-done.3
  26.4 0.1 constant_dynamic-slice_fusion.2
  26.4 0.6 collective-permute-start
  27.0 1.1 fusion.12
  28.1 1.9 collective-permute-start.2
  30.0 1.3 collective-permute-start.3
  31.4 1.3 dynamic-slice_add_fusion
  32.7 4.9 collective-permute-start.1
  37.6 2.5 compare_reduce_fusion
  40.2 3.3 select_convert_fusion.extra_ref
  43.5 0.7 or_select_fusion.bias_ref
  44.2 0.7 copy-done.7
  44.9 0.1 copy-done.8
  45.0 104.2 %window_part.2 = (f32[4096,256]{1,0:T(8,128)}, f32[4096,256]{1,0:T(8,128)}, f32[4096,256]{1,0:T(8,128)}) custom-call(bf16[4096,768]{1,0:T(8,128)(2,1)} %get-tuple-element.27.q_ref.kl_ref.kc_ref.kr_ref.vl_ref.vc_ref.vr_ref.k_ref.v_ref.qkv_hbm, bf16[4096,768]{1,0:T(8,128)(2,1)} %get-tuple-element.27.q_ref.kl_ref.kc_ref.kr_ref.vl_ref.vc_ref.vr_ref.k_ref.v_ref.qkv_hbm, ...), custom_call_target="tpu_custom_call" | custom-call | flops 22499999744 | bytes 22500000 | tf_op jit(solution)/shard_map/window_part/pallas_call | solution.py:247
  149.1 0.2 add.93
  149.3 0.1 collective-permute-start.4
  149.4 2.3 collective-permute-done.4
  151.7 0.1 broadcast_select_fusion.1
  151.8 0.1 pad_maximum_fusion.1.q_ref.kg_ref.vg_ref.qkvg_hbm
  151.9 0.5 copy-done.4
  152.4 136.5 %global_queries.1 = f32[3,1024,256]{2,1,0:T(8,128)S(1)} custom-call(bf16[1024,768]{1,0:T(8,128)(2,1)S(1)} %pad_maximum_fusion.1.q_ref.kg_ref.vg_ref.qkvg_hbm, bf16[4096,768]{1,0:T(8,128)(2,1)} %get-tuple-element.27.q_ref.kl_ref.kc_ref.kr_ref.vl_ref.vc_ref.vr_ref.k_ref.v_ref.qkv_hbm, ...), custom_call_target="tpu_custom_call" | custom-call | flops 33999998976 | bytes 20000000 | tf_op jit(solution)/shard_map/global_queries/pallas_call | solution.py:351
  288.9 1.3 constant_dynamic-slice_fusion.1
  290.2 0.1 collective-permute-start.5
  290.4 3.2 collective-permute-done.5
  293.6 1.4 fusion.1
  295.0 1.4 fusion
  296.3 0.1 pad_maximum_fusion.2
  296.4 0.9 constant_dynamic-slice_fusion
  297.4 36.6 %window_part.3 = (f32[4096,256]{1,0:T(8,128)}, f32[4096,256]{1,0:T(8,128)}, f32[4096,256]{1,0:T(8,128)}) custom-call(bf16[4096,768]{1,0:T(8,128)(2,1)} %get-tuple-element.27.q_ref.kl_ref.kc_ref.kr_ref.vl_ref.vc_ref.vr_ref.k_ref.v_ref.qkv_hbm, ...), custom_call_target="tpu_custom_call", output_to_operand_aliasing={{0}: (14, {}), {1}: (15, {}), {2}: (16, {})} | custom-call | flops 7500000256 | bytes 7500000 | tf_op jit(solution)/shard_map/window_part/pallas_call | solution.py:247
  334.0 35.3 %global_keys.1.pre_ref = bf16[1024,256]{1,0:T(8,128)(2,1)S(1)} custom-call(bf16[4096,768]{1,0:T(8,128)(2,1)} %get-tuple-element.27.q_ref.kl_ref.kc_ref.kr_ref.vl_ref.vc_ref.vr_ref.k_ref.v_ref.qkv_hbm, bf16[1024,768]{1,0:T(8,128)(2,1)S(1)} %copy-done.1, bf16[1024,768]{1,0:T(8,128)(2,1)S(1)} %copy-done.1, f32[1,256]{1,0:T(1,128)S(1)} %copy-done.5, ...), custom_call_target="tpu_custom_call" | custom-call | flops 10000000000 | bytes 8000000 | tf_op jit(solution)/shard_map/global_keys/pallas_call | solution.py:299
  369.3 0.8 copy-done.6
  370.1 1.3 fusion.11
  371.4 2.0 collective-permute-start.7
  373.4 3.7 collective-permute-done.7
  377.1 0.1 collective-permute-start.8
  377.2 1.5 collective-permute-done.8
  378.7 0.1 broadcast_select_fusion.3
  378.8 0.8 pad_maximum_fusion.3.glob_hbm
  379.6 155.3 %exchange_mlp.1.a_hbm = bf16[4096,1024]{1,0:T(8,128)(2,1)} custom-call(bf16[4096,1024]{1,0:T(8,128)(2,1)} %x_hbm.1, bf16[8,4,1568,128]{3,2,1,0:T(8,128)(2,1)} %bitcast.57, bf16[4096,768]{1,0:T(8,128)(2,1)} %get-tuple-element.27.q_ref.kl_ref.kc_ref.kr_ref.vl_ref.vc_ref.vr_ref.k_ref.v_ref.qkv_hbm, bf16[1024,768]{1,0:T(8,128)(2,1)} %copy-done, ...), custom_call_target="tpu_custom_call" | custom-call | flops 52613349376 | bytes 40000000 | tf_op jit(solution)/shard_map/exchange_mlp/pallas_call | solution.py:562
  534.9 6.4 %result.1 = bf16[4096,1024]{1,0:T(8,128)(2,1)} custom-call(bf16[4096,1024]{1,0:T(8,128)(2,1)} %exchange_mlp.1.a_hbm), custom_call_target="tpu_custom_call" | custom-call | tf_op jit(solution)/shard_map/result/pallas_call | solution.py:595
  (36 shorter events, 0.2 us)
Async XLA Ops:
  6.5 1.9 copy-start.12
  6.5 2.2 copy-start.9
  6.5 373.1 %all-gather.3.cloned.1.call-start = ((), (), s32[]{:S(2)}) async-start(), calls=%async_computation | async-start | bytes 13246464 | tf_op jit(solution)/shard_map/all_gather | solution.py:629
  8.4 1.0 copy-start.10
  8.4 1.3 copy-start.11
  8.5 1.5 copy-start.2
  25.8 0.5 copy-start.3
  26.4 4.9 collective-permute-start
  28.1 16.1 %collective-permute-start.2 = (bf16[256,512]{1,0:T(8,128)(2,1)S(1)}, bf16[256,512]{1,0:T(8,128)(2,1)S(1)}, u32[]{:S(2)}, u32[]{:S(2)}) collective-permute-start(bf16[256,512]{1,0:T(8,128)(2,1)S(1)} %get-tuple-element.52), channel_id=1, source_target_pairs={{0,1},{1,2},{2,3},{4,5},{5,6},{6,7},{8,9},{9,10},{10,11},{12,13},{... | collective-permute-start | bytes 786440 | tf_op jit(solution)/shard_map/ppermute | solution.py:635
  30.0 14.1 %collective-permute-start.3 = (bf16[256,512]{1,0:T(8,128)(2,1)S(1)}, bf16[256,512]{1,0:T(8,128)(2,1)S(1)}, u32[]{:S(2)}, u32[]{:S(2)}) collective-permute-start(bf16[256,512]{1,0:T(8,128)(2,1)S(1)} %get-tuple-element.51), channel_id=1, source_target_pairs={{1,0},{2,1},{3,2},{5,4},{6,5},{7,6},{9,8},{10,9},{11,10},{13,12},{... | collective-permute-start | bytes 786440 | tf_op jit(solution)/shard_map/ppermute | solution.py:636
  32.7 116.4 %collective-permute-start.1 = (bf16[512,768]{1,0:T(8,128)(2,1)S(1)}, bf16[512,768]{1,0:T(8,128)(2,1)S(1)}, u32[]{:S(2)}, u32[]{:S(2)}) collective-permute-start(bf16[512,768]{1,0:T(8,128)(2,1)S(1)} %dynamic-slice_add_fusion), channel_id=1, source_target_pairs={{0,2},{1,3},{2,0},{3,1},{4,6},{5,7},{6,4},{7,5},{8,10},{9,11},{10,... | collective-permute-start | bytes 2359304 | tf_op jit(solution)/shard_map/ppermute | solution.py:648
  44.1 0.7 copy-start.7
  44.1 0.8 copy-start.8
  149.3 2.4 collective-permute-start.4
  151.8 0.6 copy-start.4
  152.4 136.5 %copy-start = (bf16[1024,768]{1,0:T(8,128)(2,1)}, bf16[1024,768]{1,0:T(8,128)(2,1)S(1)}, u32[]{:S(2)}) copy-start(bf16[1024,768]{1,0:T(8,128)(2,1)S(1)} %pad_maximum_fusion.1.q_ref.kg_ref.vg_ref.qkvg_hbm) | copy-start | bytes 4718596
  290.2 3.4 collective-permute-start.5
  297.4 36.6 %copy-start.1 = (bf16[1024,768]{1,0:T(8,128)(2,1)S(1)}, bf16[1024,768]{1,0:T(8,128)(2,1)}, u32[]{:S(2)}) copy-start(bf16[1024,768]{1,0:T(8,128)(2,1)} %copy-done) | copy-start | bytes 4718596
  297.4 36.6 %copy-start.5 = (f32[1,256]{1,0:T(1,128)S(1)}, f32[1,256]{1,0:T(1,128)}, u32[]{:S(2)}) copy-start(f32[1,256]{1,0:T(1,128)} %copy-done.3) | copy-start | bytes 3076
  297.4 72.7 %collective-permute-start.6 = (f32[3,256,256]{2,1,0:T(8,128)}, f32[3,256,256]{2,1,0:T(8,128)}, u32[]{:S(2)}, u32[]{:S(2)}) collective-permute-start(f32[3,256,256]{2,1,0:T(8,128)} %constant_dynamic-slice_fusion), channel_id=1, source_target_pairs={{0,2},{1,3},{2,0},{3,1},{4,6},{5,7},{6,4},{7,5},{8,10},{9,11},{10,... | collective-permute-start | bytes 2359304 | tf_op jit(solution)/shard_map/ppermute | solution.py:661
  369.3 0.8 copy-start.6
  371.4 5.6 %collective-permute-start.7 = (bf16[256,256]{1,0:T(8,128)(2,1)S(1)}, bf16[256,256]{1,0:T(8,128)(2,1)S(1)}, u32[]{:S(2)}, u32[]{:S(2)}) collective-permute-start(bf16[256,256]{1,0:T(8,128)(2,1)S(1)} %fusion.11), channel_id=1, source_target_pairs={{0,2},{1,3},{2,0},{3,1},{4,6},{5,7},{6,4},{7,5},{8,10},{9,11},{10,... | collective-permute-start | bytes 393224 | tf_op jit(solution)/shard_map/ppermute | solution.py:667
  377.1 1.6 collective-permute-start.8
Sparse Core Ops, SparseCore 0:
  10.2 101.7 all-gather.2

commit v7 on v6

--- a/solution.py
+++ b/solution.py
@@ -485,24 +485,19 @@
         def _():
             send_own(s + 1)
 
-        for d in range(1, n_tp):
+        for d in range(n_tp - 2, 0, -1):
             b = s - (d - 1)
-
-            @pl.when((b >= 0) & (b < n_blk) & (me >= d))
+            here = (b >= 0) & (b < n_blk)
+
+            @pl.when(here & (me >= d) & (me < n_tp - 1))
             def _():
                 landed(up_recv, d, me - d, b)
-                if d < n_tp - 1:
-                    @pl.when(me < n_tp - 1)
-                    def _():
-                        up(d, b).start()
-
-            @pl.when((b >= 0) & (b < n_blk) & (me + d <= n_tp - 1))
+                up(d, b).start()
+
+            @pl.when(here & (me + d <= n_tp - 1) & (me > 0))
             def _():
                 landed(down_recv, d, me + d, b)
-                if d < n_tp - 1:
-                    @pl.when(me > 0)
-                    def _():
-                        down(d, b).start()
+                down(d, b).start()
 
         @pl.when(s + 2 < n_blk)
         def _():
@@ -517,6 +512,15 @@
         def _():
             b = s - (n_tp - 2)
             rows = rows_of(b)
+            for d in range(1, n_tp):
+                @pl.when(me == n_tp - 1)
+                def _():
+                    landed(up_recv, d, me - d, b)
+
+                @pl.when(me == 0)
+                def _():
+                    landed(down_recv, d, me + d, b)
+
             mixed = dot_nn(o_ref[0, rows], wo_ref[:d_o, :])
             for t in range(1, n_tp):
                 mixed += dot_nn(o_ref[t, rows], wo_ref[t * d_o:(t + 1) * d_o, :])

time: 549 us -> 546 us (level)
  no operation moved by 1% of the time
where the time goes in v7:
time: 546 us; the launch traced here: 545 us
  Pallas kernels  487 us (89%)
  other arithmetic  15.3 us (3%)
  between operations  13.8 us (3%)
  starting transfers between devices  10.7 us (2%)
  waiting for transfers between devices  10.7 us (2%)
  local copies, waits for them, and re-layouts  7.3 us (1%)
    pallas_call x1, Pallas kernels, exchange_mlp(): pl.pallas_call(functools.partial(exchange_mlp_kernel, n_tp=n_tp, n_rep=n_...  152 us
    pallas_call x2, Pallas kernels, window_part(): pl.pallas_call(functools.partial(window_kernel, first=first, n_blk=n_blk)...  141 us
    pallas_call x1, Pallas kernels, global_queries_part(): pl.pallas_call(functools.partial(global_queries_kernel, kb=kb), grid=(2,...  137 us
    pallas_call x1, Pallas kernels, global_keys_part(): pl.pallas_call(global_keys_kernel, grid=(2, n_rows // rb), in_specs=[row,...  35.3 us
    pallas_call x1, Pallas kernels, qkv_part(): pl.pallas_call(qkv_kernel, grid_spec=pltpu.PrefetchScalarGridSpec(num_sca...  15.9 us
  transfers between devices with their start and end apart: 10, of which 4 were waited for; matrix products, arithmetic and copies ran while one was open for 3% of the time, Pallas kernels for 60%

profile of v7, /device:TPU:0, one launch (start us, length us, event | category | flops | bytes accessed | tf_op | source)
XLA Modules:
  0.0 544.8 jit_solution(1811887174953452514)
XLA Ops:
  6.5 1.9 fusion.3
  8.5 0.2 copy.22.idx_ref
  8.8 0.2 copy.19
  9.0 0.5 copy-done.10
  9.4 0.2 copy.20
  9.7 0.2 copy.21
  9.9 0.1 pad_maximum_fusion.w_ref
  10.0 15.9 %qkv.1 = (bf16[4096,768]{1,0:T(8,128)(2,1)}, bf16[1024,768]{1,0:T(8,128)(2,1)S(1)}, f32[1,256]{1,0:T(1,128)S(1)}) custom-call(s32[1024]{0:T(1024)S(1)} %broadcast_subtract_fusion.pos_ref, s32[1024,1]{1,0:T(8,128)S(1)} %copy.22.idx_ref, bf16[4096,1024]{1,0:T(8,128)(2,1)} %x_hbm.1, bf16[1024,768]{1,0:T(8,128)(2,1)S(1)} %pad_maximum_fusion.w_ref), custom_call_target="tpu_custom_call" | custom-call | flops 8000000000 | bytes 24000000 | tf_op jit(solution)/shard_map/qkv/pallas_call | solution.py:81
  25.8 0.5 copy-done.3
  26.4 0.1 constant_dynamic-slice_fusion.2
  26.4 0.6 collective-permute-start
  27.0 1.1 fusion.12
  28.1 1.9 collective-permute-start.2
  30.0 1.3 collective-permute-start.3
  31.4 1.3 dynamic-slice_add_fusion
  32.7 4.6 collective-permute-start.1
  37.3 2.5 compare_reduce_fusion
  39.9 3.3 select_convert_fusion.extra_ref
  43.2 0.7 or_select_fusion.bias_ref
  43.9 0.7 copy-done.7
  44.6 0.1 copy-done.8
  44.7 104.2 %window_part.2 = (f32[4096,256]{1,0:T(8,128)}, f32[4096,256]{1,0:T(8,128)}, f32[4096,256]{1,0:T(8,128)}) custom-call(bf16[4096,768]{1,0:T(8,128)(2,1)} %get-tuple-element.27.q_ref.kl_ref.kc_ref.kr_ref.vl_ref.vc_ref.vr_ref.k_ref.v_ref.qkv_hbm, bf16[4096,768]{1,0:T(8,128)(2,1)} %get-tuple-element.27.q_ref.kl_ref.kc_ref.kr_ref.vl_ref.vc_ref.vr_ref.k_ref.v_ref.qkv_hbm, ...), custom_call_target="tpu_custom_call" | custom-call | flops 22499999744 | bytes 22500000 | tf_op jit(solution)/shard_map/window_part/pallas_call | solution.py:247
  148.8 0.2 add.93
  149.0 0.1 collective-permute-start.4
  149.1 2.3 collective-permute-done.4
  151.4 0.1 broadcast_select_fusion.1
  151.5 0.1 pad_maximum_fusion.1.q_ref.kg_ref.vg_ref.qkvg_hbm
  151.6 0.5 copy-done.4
  152.1 136.5 %global_queries.1 = f32[3,1024,256]{2,1,0:T(8,128)S(1)} custom-call(bf16[1024,768]{1,0:T(8,128)(2,1)S(1)} %pad_maximum_fusion.1.q_ref.kg_ref.vg_ref.qkvg_hbm, bf16[4096,768]{1,0:T(8,128)(2,1)} %get-tuple-element.27.q_ref.kl_ref.kc_ref.kr_ref.vl_ref.vc_ref.vr_ref.k_ref.v_ref.qkv_hbm, ...), custom_call_target="tpu_custom_call" | custom-call | flops 33999998976 | bytes 20000000 | tf_op jit(solution)/shard_map/global_queries/pallas_call | solution.py:351
  288.6 1.3 constant_dynamic-slice_fusion.1
  289.9 0.1 collective-permute-start.5
  290.0 3.2 collective-permute-done.5
  293.3 1.4 fusion.1
  294.7 1.4 fusion
  296.0 0.1 pad_maximum_fusion.2
  296.1 0.9 constant_dynamic-slice_fusion
  297.1 36.6 %window_part.3 = (f32[4096,256]{1,0:T(8,128)}, f32[4096,256]{1,0:T(8,128)}, f32[4096,256]{1,0:T(8,128)}) custom-call(bf16[4096,768]{1,0:T(8,128)(2,1)} %get-tuple-element.27.q_ref.kl_ref.kc_ref.kr_ref.vl_ref.vc_ref.vr_ref.k_ref.v_ref.qkv_hbm, ...), custom_call_target="tpu_custom_call", output_to_operand_aliasing={{0}: (14, {}), {1}: (15, {}), {2}: (16, {})} | custom-call | flops 7500000256 | bytes 7500000 | tf_op jit(solution)/shard_map/window_part/pallas_call | solution.py:247
  333.7 35.3 %global_keys.1.pre_ref = bf16[1024,256]{1,0:T(8,128)(2,1)S(1)} custom-call(bf16[4096,768]{1,0:T(8,128)(2,1)} %get-tuple-element.27.q_ref.kl_ref.kc_ref.kr_ref.vl_ref.vc_ref.vr_ref.k_ref.v_ref.qkv_hbm, bf16[1024,768]{1,0:T(8,128)(2,1)S(1)} %copy-done.1, bf16[1024,768]{1,0:T(8,128)(2,1)S(1)} %copy-done.1, f32[1,256]{1,0:T(1,128)S(1)} %copy-done.5, ...), custom_call_target="tpu_custom_call" | custom-call | flops 10000000000 | bytes 8000000 | tf_op jit(solution)/shard_map/global_keys/pallas_call | solution.py:299
  369.0 0.8 copy-done.6
  369.8 1.3 fusion.11
  371.1 2.0 collective-permute-start.7
  373.1 3.7 collective-permute-done.7
  376.8 0.1 collective-permute-start.8
  376.9 1.5 collective-permute-done.8
  378.4 0.1 broadcast_select_fusion.3
  378.5 0.8 pad_maximum_fusion.3.glob_hbm
  379.3 152.2 %exchange_mlp.1.a_hbm = bf16[4096,1024]{1,0:T(8,128)(2,1)} custom-call(bf16[4096,1024]{1,0:T(8,128)(2,1)} %x_hbm.1, bf16[8,4,1568,128]{3,2,1,0:T(8,128)(2,1)} %bitcast.57, bf16[4096,768]{1,0:T(8,128)(2,1)} %get-tuple-element.27.q_ref.kl_ref.kc_ref.kr_ref.vl_ref.vc_ref.vr_ref.k_ref.v_ref.qkv_hbm, bf16[1024,768]{1,0:T(8,128)(2,1)} %copy-done, ...), custom_call_target="tpu_custom_call" | custom-call | flops 52613349376 | bytes 40000000 | tf_op jit(solution)/shard_map/exchange_mlp/pallas_call | solution.py:566
  531.5 6.4 %result.1 = bf16[4096,1024]{1,0:T(8,128)(2,1)} custom-call(bf16[4096,1024]{1,0:T(8,128)(2,1)} %exchange_mlp.1.a_hbm), custom_call_target="tpu_custom_call" | custom-call | tf_op jit(solution)/shard_map/result/pallas_call | solution.py:599
  (36 shorter events, 0.2 us)
Async XLA Ops:
  6.5 1.9 copy-start.12
  6.5 2.2 copy-start.9
  6.5 372.8 %all-gather.3.cloned.1.call-start = ((), (), s32[]{:S(2)}) async-start(), calls=%async_computation | async-start | bytes 13246464 | tf_op jit(solution)/shard_map/all_gather | solution.py:633
  8.4 1.0 copy-start.10
  8.4 1.3 copy-start.11
  8.5 1.5 copy-start.2
  25.8 0.5 copy-start.3
  26.4 4.9 collective-permute-start
  28.1 15.8 %collective-permute-start.2 = (bf16[256,512]{1,0:T(8,128)(2,1)S(1)}, bf16[256,512]{1,0:T(8,128)(2,1)S(1)}, u32[]{:S(2)}, u32[]{:S(2)}) collective-permute-start(bf16[256,512]{1,0:T(8,128)(2,1)S(1)} %get-tuple-element.52), channel_id=1, source_target_pairs={{0,1},{1,2},{2,3},{4,5},{5,6},{6,7},{8,9},{9,10},{10,11},{12,13},{... | collective-permute-start | bytes 786440 | tf_op jit(solution)/shard_map/ppermute | solution.py:639
  30.0 13.8 %collective-permute-start.3 = (bf16[256,512]{1,0:T(8,128)(2,1)S(1)}, bf16[256,512]{1,0:T(8,128)(2,1)S(1)}, u32[]{:S(2)}, u32[]{:S(2)}) collective-permute-start(bf16[256,512]{1,0:T(8,128)(2,1)S(1)} %get-tuple-element.51), channel_id=1, source_target_pairs={{1,0},{2,1},{3,2},{5,4},{6,5},{7,6},{9,8},{10,9},{11,10},{13,12},{... | collective-permute-start | bytes 786440 | tf_op jit(solution)/shard_map/ppermute | solution.py:640
  32.7 116.1 %collective-permute-start.1 = (bf16[512,768]{1,0:T(8,128)(2,1)S(1)}, bf16[512,768]{1,0:T(8,128)(2,1)S(1)}, u32[]{:S(2)}, u32[]{:S(2)}) collective-permute-start(bf16[512,768]{1,0:T(8,128)(2,1)S(1)} %dynamic-slice_add_fusion), channel_id=1, source_target_pairs={{0,2},{1,3},{2,0},{3,1},{4,6},{5,7},{6,4},{7,5},{8,10},{9,11},{10,... | collective-permute-start | bytes 2359304 | tf_op jit(solution)/shard_map/ppermute | solution.py:652
  43.8 0.7 copy-start.7
  43.8 0.8 copy-start.8
  149.0 2.4 collective-permute-start.4
  151.5 0.6 copy-start.4
  152.1 136.5 %copy-start = (bf16[1024,768]{1,0:T(8,128)(2,1)}, bf16[1024,768]{1,0:T(8,128)(2,1)S(1)}, u32[]{:S(2)}) copy-start(bf16[1024,768]{1,0:T(8,128)(2,1)S(1)} %pad_maximum_fusion.1.q_ref.kg_ref.vg_ref.qkvg_hbm) | copy-start | bytes 4718596
  289.9 3.4 collective-permute-start.5
  297.1 36.6 %copy-start.1 = (bf16[1024,768]{1,0:T(8,128)(2,1)S(1)}, bf16[1024,768]{1,0:T(8,128)(2,1)}, u32[]{:S(2)}) copy-start(bf16[1024,768]{1,0:T(8,128)(2,1)} %copy-done) | copy-start | bytes 4718596
  297.1 36.6 %copy-start.5 = (f32[1,256]{1,0:T(1,128)S(1)}, f32[1,256]{1,0:T(1,128)}, u32[]{:S(2)}) copy-start(f32[1,256]{1,0:T(1,128)} %copy-done.3) | copy-start | bytes 3076
  297.1 72.7 %collective-permute-start.6 = (f32[3,256,256]{2,1,0:T(8,128)}, f32[3,256,256]{2,1,0:T(8,128)}, u32[]{:S(2)}, u32[]{:S(2)}) collective-permute-start(f32[3,256,256]{2,1,0:T(8,128)} %constant_dynamic-slice_fusion), channel_id=1, source_target_pairs={{0,2},{1,3},{2,0},{3,1},{4,6},{5,7},{6,4},{7,5},{8,10},{9,11},{10,... | collective-permute-start | bytes 2359304 | tf_op jit(solution)/shard_map/ppermute | solution.py:665
  369.0 0.8 copy-start.6
  371.1 5.6 %collective-permute-start.7 = (bf16[256,256]{1,0:T(8,128)(2,1)S(1)}, bf16[256,256]{1,0:T(8,128)(2,1)S(1)}, u32[]{:S(2)}, u32[]{:S(2)}) collective-permute-start(bf16[256,256]{1,0:T(8,128)(2,1)S(1)} %fusion.11), channel_id=1, source_target_pairs={{0,2},{1,3},{2,0},{3,1},{4,6},{5,7},{6,4},{7,5},{8,10},{9,11},{10,... | collective-permute-start | bytes 393224 | tf_op jit(solution)/shard_map/ppermute | solution.py:671
  376.8 1.6 collective-permute-start.8
Sparse Core Ops, SparseCore 0:
  10.2 101.7 all-gather.2
